TPU v7x, 32 devices: a whole 2x2x4 slice. The times are simulated.
32 devices in a mesh: dp: 2 (over x), sp2: 4 (over z), sp: 4 (over y, core).
Axes of the slice: x: 2, y: 2, z: 4, core: 2. Of those that a mesh axis runs over, the one named last changes fastest.
Arguments:
- x: bfloat16 [16, 16, 128, 1280], P('dp', 'sp', 'sp2'), parts along dimension 0
- time_emb: bfloat16 [16, 1280], P('dp'), parts along dimension 0
- gn_scale: bfloat16 [5, 1280], replicated
- gn_shift: bfloat16 [5, 1280], replicated
- conv_w: bfloat16 [4, 3, 3, 1280, 1280], replicated
- time_w: bfloat16 [2, 1280, 1280], replicated
- w_qkv: bfloat16 [3, 1280, 20, 64], replicated
- w_out: bfloat16 [20, 64, 1280], replicated
Outputs:
- output: bfloat16 [16, 16, 128, 1280], P('dp', 'sp', 'sp2'), parts along dimension 0
There are 2 independent parts. A program takes and returns all parts, laid end to end along the dimension named above; an argument that names none is the same for every part.
All inputs are finite; a program needn't handle non-finite values.
Results may differ from a plain program's by a relative error of at most 0.00966543.
Values are sent between devices in bfloat16 or wider.
A program may use at most 1 GiB of HBM per device.

v0:
```python
import jax
import jax.numpy as jnp
from jax import lax
from jax.sharding import PartitionSpec as P

GROUPS = 32
NORM_EPS = 1e-5
SPACE = ("sp", "sp2")


def group_norm(tile, scale, shift, positions):
    batch, tile_rows, tile_cols, channels = tile.shape
    grouped = tile.astype(jnp.float32).reshape(batch, tile_rows, tile_cols, GROUPS, channels // GROUPS)
    local_moments = jnp.stack([jnp.sum(grouped, axis=(1, 2, 4)), jnp.sum(grouped * grouped, axis=(1, 2, 4))])
    moments = lax.psum(local_moments, SPACE)
    count = positions * (channels // GROUPS)
    mean = moments[0] / count
    inv_std = lax.rsqrt(moments[1] / count - mean * mean + NORM_EPS)
    normed = (grouped - mean[:, None, None, :, None]) * inv_std[:, None, None, :, None]
    return normed.reshape(tile.shape) * scale.astype(jnp.float32) + shift.astype(jnp.float32)


def with_halo(tile, row_devs, col_devs):
    down_pairs = [(i, i + 1) for i in range(row_devs - 1)]
    up_pairs = [(i + 1, i) for i in range(row_devs - 1)]
    from_above = lax.ppermute(tile[:, -1:], "sp", down_pairs)
    from_below = lax.ppermute(tile[:, :1], "sp", up_pairs)
    tall = jnp.concatenate([from_above, tile, from_below], axis=1)
    right_pairs = [(j, j + 1) for j in range(col_devs - 1)]
    left_pairs = [(j + 1, j) for j in range(col_devs - 1)]
    from_left = lax.ppermute(tall[:, :, -1:], "sp2", right_pairs)
    from_right = lax.ppermute(tall[:, :, :1], "sp2", left_pairs)
    return jnp.concatenate([from_left, tall, from_right], axis=2)


def conv3x3(padded, kernel):
    return lax.conv_general_dilated(padded, kernel, (1, 1), "VALID", dimension_numbers=("NHWC", "HWIO", "NHWC"), preferred_element_type=jnp.float32)


def res_block(tile, time_vec, gn_scale, gn_shift, conv_w, norm_idx, conv_idx, row_devs, col_devs, positions):
    first = jax.nn.silu(group_norm(tile, gn_scale[norm_idx], gn_shift[norm_idx], positions)).astype(jnp.bfloat16)
    hidden = (conv3x3(with_halo(first, row_devs, col_devs), conv_w[conv_idx]) + time_vec[:, None, None, :]).astype(jnp.bfloat16)
    second = jax.nn.silu(group_norm(hidden, gn_scale[norm_idx + 1], gn_shift[norm_idx + 1], positions)).astype(jnp.bfloat16)
    return (tile.astype(jnp.float32) + conv3x3(with_halo(second, row_devs, col_devs), conv_w[conv_idx + 1])).astype(jnp.bfloat16)


def attention_block(tile, scale, shift, w_qkv, w_out, positions):
    batch, tile_rows, tile_cols, channels = tile.shape
    num_heads, head_dim = w_out.shape[0], w_out.shape[1]
    tokens = tile_rows * tile_cols
    normed = group_norm(tile, scale, shift, positions).astype(jnp.bfloat16)
    query = jnp.einsum("bijc,chd->bijhd", normed, w_qkv[0], preferred_element_type=jnp.float32).astype(jnp.bfloat16).reshape(batch, tokens, num_heads, head_dim)
    key_val = jnp.einsum("bijc,schd->sbijhd", normed, w_qkv[1:], preferred_element_type=jnp.float32).astype(jnp.bfloat16).reshape(2, batch, tokens, num_heads, head_dim)
    gathered = lax.all_gather(key_val, SPACE)
    logit_scale = head_dim ** -0.5

    def absorb(carry, block):
        peak, weight_sum, running_out = carry
        logits = jnp.einsum("bqhd,bkhd->bhqk", query, block[0], preferred_element_type=jnp.float32) * logit_scale
        new_peak = jnp.maximum(peak, jnp.max(logits, axis=-1))
        rescale = jnp.exp(peak - new_peak)
        weights = jnp.exp(logits - new_peak[..., None])
        weight_sum = weight_sum * rescale + jnp.sum(weights, axis=-1)
        running_out = running_out * rescale[..., None] + jnp.einsum("bhqk,bkhd->bhqd", weights.astype(jnp.bfloat16), block[1], preferred_element_type=jnp.float32)
        return (new_peak, weight_sum, running_out), None

    start_carry = (
        jnp.full((batch, num_heads, tokens), -jnp.inf, jnp.float32),
        jnp.zeros((batch, num_heads, tokens), jnp.float32),
        jnp.zeros((batch, num_heads, tokens, head_dim), jnp.float32),
    )
    final_carry, _ = lax.scan(absorb, start_carry, gathered)
    attended = (final_carry[2] / final_carry[1][..., None]).astype(jnp.bfloat16)
    out = jnp.einsum("bhqd,hdc->bqc", attended, w_out, preferred_element_type=jnp.float32)
    return (tile.astype(jnp.float32) + out.reshape(tile.shape)).astype(jnp.bfloat16)


def solution(mesh):
    row_devs = mesh.shape["sp"]
    col_devs = mesh.shape["sp2"]
    lat_spec = P("dp", "sp", "sp2", None)

    def local(x, time_emb, gn_scale, gn_shift, conv_w, time_w, w_qkv, w_out):
        positions = x.shape[1] * row_devs * x.shape[2] * col_devs
        time_act = jax.nn.silu(time_emb.astype(jnp.float32)).astype(jnp.bfloat16)
        time_vecs = jnp.einsum("bt,stc->sbc", time_act, time_w, preferred_element_type=jnp.float32)
        first = res_block(x, time_vecs[0], gn_scale, gn_shift, conv_w, 0, 0, row_devs, col_devs, positions)
        middle = attention_block(first, gn_scale[2], gn_shift[2], w_qkv, w_out, positions)
        return res_block(middle, time_vecs[1], gn_scale, gn_shift, conv_w, 3, 2, row_devs, col_devs, positions)

    return jax.shard_map(local, mesh=mesh, in_specs=(lat_spec, P("dp", None), P(), P(), P(), P(), P(), P()), out_specs=lat_spec, check_vma=False)
```

profile of v0, /device:TPU:31, one launch (start us, length us, event | category | flops | bytes accessed | tf_op | source)
XLA Modules:
  0.0 1383.3 jit_solution(17413093375135485181)
XLA Ops:
  11.8 29.8 %psum.35 = f32[2,8,32]{2,1,0:T(8,128)S(1)} all-reduce(f32[2,8,32]{2,1,0:T(8,128)S(1)} %pad_maximum_fusion.12), channel_id=1, replica_groups=mesh['dp'=2,'sp2'=4,'sp'=4] {'sp','sp2'}, use_global_device_ids=true, to_apply=%region_4.5 | all-reduce | flops 512 | bytes 4096 | tf_op jit(solution)/shard_map/psum | solution.py:15
  63.2 35.1 %convert_reduce_fusion.4 = (f32[8,1280]{1,0:T(8,128)S(1)}, f32[8,1280]{1,0:T(8,128)S(1)}, bf16[8,4,32,1280]{3,0,2,1:T(8,128)(2,1)}) fusion(f32[8,1280]{1,0:T(8,128)S(1)} %get-tuple-element.135, bf16[4,3,3,1280,1280]{4,3,2,1,0:T(8,128)(2,1)} %param.14, bf16[8,6,1,1280]{3,0,2,1:T(8,128)(2,1)S(1)} %collective-permute-done.3, ...), kind=kOutput, calls=%fused_computation.50 | convolution fusion | flops 30215188480 | bytes 36413440 | tf_op jit(solution)/shard_map/conv_general_dilated | solution.py:37
  98.8 35.1 %psum.36 = f32[2,8,32]{2,1,0:T(8,128)S(1)} all-reduce(f32[2,8,32]{2,1,0:T(8,128)S(1)} %pad_maximum_fusion.13), channel_id=1, replica_groups=mesh['dp'=2,'sp2'=4,'sp'=4] {'sp','sp2'}, use_global_device_ids=true, to_apply=%region_9.10 | all-reduce | flops 512 | bytes 4096 | tf_op jit(solution)/shard_map/psum | solution.py:15
  154.9 35.6 %convert_reduce_fusion.1 = (f32[8,1280]{1,0:T(8,128)S(1)}, f32[8,1280]{1,0:T(8,128)S(1)}, bf16[8,4,32,1280]{3,0,2,1:T(8,128)(2,1)}) fusion(bf16[4,3,3,1280,1280]{4,3,2,1,0:T(8,128)(2,1)} %param.14, bf16[8,6,1,1280]{3,0,2,1:T(8,128)(2,1)S(1)} %collective-permute-done.7, bf16[8,1,32,1280]{3,0,2,1:T(8,128)(2,1)S(1)} %collective-permute-done.5, ...), kind=kOutput, calls=%fused_computation.40 | convolution fusion | flops 30216499200 | bytes 38993920 | tf_op jit(solution)/shard_map/conv_general_dilated | solution.py:37
  191.0 38.7 %psum.37 = f32[2,8,32]{2,1,0:T(8,128)S(1)} all-reduce(f32[2,8,32]{2,1,0:T(8,128)S(1)} %pad_maximum_fusion.14), channel_id=1, replica_groups=mesh['dp'=2,'sp2'=4,'sp'=4] {'sp','sp2'}, use_global_device_ids=true, to_apply=%region_14.15 | all-reduce | flops 512 | bytes 4096 | tf_op jit(solution)/shard_map/psum | solution.py:15
  234.4 17.6 %convert_bitcast_fusion = bf16[2,8,4,32,20,64]{5,3,4,0,2,1:T(8,128)(2,1)} fusion(bf16[3,1280,20,64]{1,3,2,0:T(8,128)(2,1)} %param.16, bf16[8,4,32,1280,1,1]{3,0,2,1,5,4:T(8,128)(2,1)S(1)} %get-tuple-element.125), kind=kOutput, calls=%fused_computation.32 | convolution fusion | flops 6713507840 | bytes 14417920 | tf_op jit(solution)/shard_map/bijc,schd->sbijhd/dot_general | solution.py:53
  252.0 11.3 copy.38
  263.3 10.3 copy.39
  273.7 9.6 fusion.129
  293.5 415.9 %all-gather.2.cloned.1.call-done = bf16[16,2,8,128,20,64]{3,5,4,2,1,0:T(8,128)(2,1)} async-done(((bf16[1,2,8,128,20,64]{3,5,4,2,1,0:T(8,128)(2,1)}), bf16[16,2,8,128,20,64]{3,5,4,2,1,0:T(8,128)(2,1)}) %all-gather.2.cloned.1.call-update) | async-done | bytes 83886096 | tf_op jit(solution)/shard_map/all_gather | solution.py:54
  709.3 465.9 %while.15 = (s32[]{:T(128)}, f32[8,20,128]{2,1,0:T(8,128)}, f32[8,20,128]{2,1,0:T(8,128)}, f32[8,20,128,64]{2,3,1,0:T(8,128)}, bf16[16,2,8,128,20,64]{3,5,4,2,1,...) while((s32[]{:T(128)}, f32[8,20,128]{2,1,0:T(8,128)}, ...), condition=%wide.region_18.19_spmd.clone, body=%wide.region_15.18_spmd.clone.sunk | while | flops 696094720 | bytes 52102348 | solution.py:72
  709.5 8.4 bitcast_reduce_fusion.2
  717.9 7.0 fusion.188
  725.6 10.1 fusion.190
  736.4 8.4 bitcast_reduce_fusion.2
  745.7 7.0 fusion.188
  753.4 11.6 fusion.190
  765.6 8.4 bitcast_reduce_fusion.2
  774.9 7.0 fusion.188
  782.6 11.6 fusion.190
  794.9 8.4 bitcast_reduce_fusion.2
  804.2 7.0 fusion.188
  811.9 11.6 fusion.190
  824.1 8.4 bitcast_reduce_fusion.2
  833.4 7.0 fusion.188
  841.1 11.6 fusion.190
  853.4 8.4 bitcast_reduce_fusion.2
  862.7 7.0 fusion.188
  870.4 11.6 fusion.190
  882.6 8.4 bitcast_reduce_fusion.2
  891.9 7.0 fusion.188
  899.6 11.6 fusion.190
  911.9 8.4 bitcast_reduce_fusion.2
  921.2 7.0 fusion.188
  928.9 11.6 fusion.190
  941.1 8.4 bitcast_reduce_fusion.2
  950.5 7.0 fusion.188
  958.2 11.6 fusion.190
  970.4 8.4 bitcast_reduce_fusion.2
  979.7 7.0 fusion.188
  987.4 11.6 fusion.190
  999.7 8.4 bitcast_reduce_fusion.2
  1009.0 7.0 fusion.188
  1016.7 11.6 fusion.190
  1028.9 8.4 bitcast_reduce_fusion.2
  1038.2 7.0 fusion.188
  1045.9 11.6 fusion.190
  1058.2 8.4 bitcast_reduce_fusion.2
  1067.5 7.0 fusion.188
  1075.2 11.6 fusion.190
  1087.4 8.4 bitcast_reduce_fusion.2
  1096.7 7.0 fusion.188
  1104.4 11.6 fusion.190
  1116.7 8.4 bitcast_reduce_fusion.2
  1126.0 7.0 fusion.188
  1133.7 11.6 fusion.190
  1145.9 8.4 bitcast_reduce_fusion.2
  1155.2 7.0 fusion.188
  1162.9 11.6 fusion.190
  1180.0 8.9 copy.50
  1198.3 29.9 %psum.38 = f32[2,8,32]{2,1,0:T(8,128)S(1)} all-reduce(f32[2,8,32]{2,1,0:T(8,128)S(1)} %pad_maximum_fusion.15), channel_id=1, replica_groups=mesh['dp'=2,'sp2'=4,'sp'=4] {'sp','sp2'}, use_global_device_ids=true, to_apply=%region_23.24 | all-reduce | flops 512 | bytes 4096 | tf_op jit(solution)/shard_map/psum | solution.py:15
  1245.6 35.2 %convert_reduce_fusion.3 = (f32[8,1280]{1,0:T(8,128)S(1)}, f32[8,1280]{1,0:T(8,128)S(1)}, bf16[8,4,32,1280]{3,0,2,1:T(8,128)(2,1)}) fusion(f32[8,1280]{1,0:T(8,128)S(1)} %copy-done.7, bf16[4,3,3,1280,1280]{4,3,2,1,0:T(8,128)(2,1)} %param.14, bf16[8,6,1,1280]{3,0,2,1:T(8,128)(2,1)S(1)} %collective-permute-done.11, ...), kind=kOutput, calls=%fused_computation.47 | convolution fusion | flops 30215188480 | bytes 36413440 | tf_op jit(solution)/shard_map/conv_general_dilated | solution.py:37
  1281.3 37.2 %psum.39 = f32[2,8,32]{2,1,0:T(8,128)S(1)} all-reduce(f32[2,8,32]{2,1,0:T(8,128)S(1)} %pad_maximum_fusion.16), channel_id=1, replica_groups=mesh['dp'=2,'sp2'=4,'sp'=4] {'sp','sp2'}, use_global_device_ids=true, to_apply=%region_28.29 | all-reduce | flops 512 | bytes 4096 | tf_op jit(solution)/shard_map/psum | solution.py:15
  1339.6 34.4 %fusion.79 = bf16[8,4,32,1280]{3,0,2,1:T(8,128)(2,1)S(1)} fusion(bf16[8,4,32,1280]{3,0,2,1:T(8,128)(2,1)S(1)} %copy-done.1, bf16[4,3,3,1280,1280]{4,3,2,1,0:T(8,128)(2,1)} %param.14, bf16[8,6,1,1280]{3,0,2,1:T(8,128)(2,1)S(1)} %collective-permute-done.15, bf16[8,1,32,1280]{3,0,2,1:T(8,128)(2,1)S(1)} %collective-permute-done.13, ...), kind=kOutput, calls=%fused_computation.101 | convolution fusion | flops 30211276800 | bytes 38912000 | tf_op jit(solution)/shard_map/conv_general_dilated | solution.py:37
  (283 shorter events, 152.9 us)
Async XLA Ops:
  6.5 1182.4 %copy-start = (bf16[20,64,1280]{2,1,0:T(8,128)(2,1)S(1)}, bf16[20,64,1280]{2,1,0:T(8,128)(2,1)}, u32[]{:S(2)}) copy-start(bf16[20,64,1280]{2,1,0:T(8,128)(2,1)} %param.17) | copy-start | bytes 9830404
  6.5 702.8 %all-gather.2.cloned.1.call-start = ((), (), s32[]{:S(2)}) async-start(), calls=%async_computation | async-start | bytes 89128960 | tf_op jit(solution)/shard_map/all_gather | solution.py:54
  11.8 40.4 %copy-start.14 = (bf16[8,1280]{1,0:T(8,128)(2,1)S(1)}, bf16[8,1280]{1,0:T(8,128)(2,1)}, u32[]{:S(2)}) copy-start(bf16[8,1280]{1,0:T(8,128)(2,1)} %param.11) | copy-start | bytes 61444
  47.8 8.2 collective-permute-start
  49.1 6.9 collective-permute-start.1
  56.0 5.9 collective-permute-start.2
  57.3 5.8 collective-permute-start.3
  134.3 20.6 %copy-start.3 = (bf16[8,4,32,1280]{3,2,1,0:T(8,128)(2,1)S(1)}, bf16[8,4,32,1280]{3,2,1,0:T(8,128)(2,1)}, u32[]{:S(2)}) copy-start(bf16[8,4,32,1280]{3,2,1,0:T(8,128)(2,1)} %param.10) | copy-start | bytes 7864324
  138.1 7.8 collective-permute-start.4
  139.4 8.1 collective-permute-start.5
  147.6 5.9 collective-permute-start.6
  148.9 81.2 %copy-start.12 = (f32[1280]{0:T(1024)S(1)}, f32[1280]{0:T(1024)}, u32[]{:S(2)}) copy-start(f32[1280]{0:T(1024)} %get-tuple-element.95) | copy-start | bytes 15364
  148.9 81.2 %copy-start.13 = (f32[1280]{0:T(1024)S(1)}, f32[1280]{0:T(1024)}, u32[]{:S(2)}) copy-start(f32[1280]{0:T(1024)} %get-tuple-element.142) | copy-start | bytes 15364
  148.9 6.0 collective-permute-start.7
  717.9 7.0 copy-start.4
  717.9 7.0 copy-start.5
  745.7 7.0 copy-start.4
  745.7 7.0 copy-start.5
  774.9 7.0 copy-start.4
  774.9 7.0 copy-start.5
  804.2 7.0 copy-start.4
  804.2 7.0 copy-start.5
  833.4 7.0 copy-start.4
  833.4 7.0 copy-start.5
  840.5 0.6 copy-start.6
  862.7 7.0 copy-start.4
  862.7 7.0 copy-start.5
  869.8 0.6 copy-start.6
  891.9 7.0 copy-start.4
  891.9 7.0 copy-start.5
  899.0 0.6 copy-start.6
  921.2 7.0 copy-start.4
  921.2 7.0 copy-start.5
  950.4 7.0 copy-start.4
  950.4 7.0 copy-start.5
  979.7 7.0 copy-start.4
  979.7 7.0 copy-start.5
  1008.9 7.0 copy-start.4
  1009.0 7.0 copy-start.5
  1038.2 7.0 copy-start.4
  1038.2 7.0 copy-start.5
  1067.5 7.0 copy-start.4
  1067.5 7.0 copy-start.5
  1096.7 7.0 copy-start.4
  1096.7 7.0 copy-start.5
  1126.0 7.0 copy-start.4
  1126.0 7.0 copy-start.5
  1155.2 7.0 copy-start.4
  1155.2 7.0 copy-start.5
  1188.9 6.4 copy-start.2
  1195.3 33.5 %copy-start.10 = (f32[1280]{0:T(1024)S(1)}, f32[1280]{0:T(1024)}, u32[]{:S(2)}) copy-start(f32[1280]{0:T(1024)} %get-tuple-element.98) | copy-start | bytes 15364
  1195.3 33.5 %copy-start.11 = (f32[1280]{0:T(1024)S(1)}, f32[1280]{0:T(1024)}, u32[]{:S(2)}) copy-start(f32[1280]{0:T(1024)} %get-tuple-element.139) | copy-start | bytes 15364
  1228.7 16.9 %copy-start.7 = (f32[8,1280]{1,0:T(8,128)S(1)}, f32[8,1280]{1,0:T(8,128)}, u32[]{:S(2)}) copy-start(f32[8,1280]{1,0:T(8,128)} %get-tuple-element.134) | copy-start | bytes 122884
  1232.4 4.4 collective-permute-start.8
  1233.7 4.7 collective-permute-start.9
  1238.5 5.6 collective-permute-start.10
  1239.8 5.8 collective-permute-start.11
  1245.6 73.3 %copy-start.8 = (f32[1280]{0:T(1024)S(1)}, f32[1280]{0:T(1024)}, u32[]{:S(2)}) copy-start(f32[1280]{0:T(1024)} %get-tuple-element.94) | copy-start | bytes 15364
  1245.6 73.3 %copy-start.9 = (f32[1280]{0:T(1024)S(1)}, f32[1280]{0:T(1024)}, u32[]{:S(2)}) copy-start(f32[1280]{0:T(1024)} %get-tuple-element.143) | copy-start | bytes 15364
  1318.9 20.6 %copy-start.1 = (bf16[8,4,32,1280]{3,0,2,1:T(8,128)(2,1)S(1)}, bf16[8,4,32,1280]{3,0,2,1:T(8,128)(2,1)}, u32[]{:S(2)}) copy-start(bf16[8,4,32,1280]{3,0,2,1:T(8,128)(2,1)} %get-tuple-element.113) | copy-start | bytes 7864324
  1322.7 8.0 collective-permute-start.12
  1324.0 8.3 collective-permute-start.13
  1332.4 5.9 collective-permute-start.14
  1333.7 5.8 collective-permute-start.15
  (13 other events, 8.2 us)
Sparse Core Ops, SparseCore 0:
  273.8 435.4 all-gather.1
where the time goes:
time: 1410 us; the launch traced here: 1380 us
  matrix products  496 us (35%)
  waiting for transfers between devices  428 us (30%)
  blocking collectives  171 us (12%)
  other arithmetic  160 us (11%)
  local copies, waits for them, and re-layouts  67.8 us (5%)
  starting transfers between devices  45.7 us (3%)
  between operations  14.7 us (1%)
    all_gather x1, waiting for transfers between devices, attention_block(): gathered = lax.all_gather(key_val, SPACE)  416 us
    dot_general x16, matrix products, absorb(): jnp.einsum('bhqk,bkhd->bhqd', weights.astype(jnp.bfloat16), block[1], pre...  184 us
    psum x5, blocking collectives, group_norm(): moments = lax.psum(local_moments, SPACE)  171 us
    conv_general_dilated x4, matrix products, conv3x3(): lax.conv_general_dilated(padded, kernel, (1, 1), 'VALID', dimension_numbe...  140 us
    dot_general x16, matrix products, absorb(): jnp.einsum('bqhd,bkhd->bhqk', query, block[0], preferred_element_type=jnp...  134 us
    reduce_sum x16, other arithmetic, absorb(): weight_sum = weight_sum * rescale + jnp.sum(weights, axis=-1)  112 us
  transfers between devices with their start and end apart: 17, of which 11 were waited for; matrix products, arithmetic and copies ran while one was open for 2% of the time, Pallas kernels for 0%

commit v1 on v0

v1 whole, which is shorter than its diff:
```python
import functools

import jax
import jax.numpy as jnp
from jax import lax
from jax.experimental import pallas as pl
from jax.experimental.pallas import tpu as pltpu
from jax.sharding import PartitionSpec as P

GROUPS = 32
NORM_EPS = 1e-5
MESH = pl.DeviceIdType.MESH
SP, SP2 = "sp", "sp2"


def place(sp, cores=2):
    return sp // cores, lax.rem(sp, cores)


def to_images_kernel(x_ref, out_ref, stage, send_sem, recv_sem, self_sem):
    images, rows, cols, _ = x_ref.shape
    sp, z = lax.axis_index(SP), lax.axis_index(SP2)
    y, core = place(sp)
    mine = y * 4 + z
    to_core = z // 2
    own = to_core == core
    barrier = pltpu.get_barrier_semaphore()
    for s in range(8):
        src_sp, src_z = s // 2, 2 * core + s % 2

        @pl.when(jnp.logical_not((src_sp == sp) & (src_z == z)))
        def _():
            pl.semaphore_signal(barrier, inc=1, device_id={SP: src_sp, SP2: src_z}, device_id_type=MESH)

    pl.semaphore_wait(barrier, 8 - own.astype(jnp.int32))

    def piece(src_sp, src_z):
        return out_ref.at[pl.ds(src_sp * rows, rows), pl.ds(lax.rem(src_z, 2) * cols, cols), :]

    def send(i):
        return pltpu.make_async_remote_copy(
            src_ref=x_ref.at[i], dst_ref=piece(sp, z), send_sem=send_sem.at[i], recv_sem=recv_sem.at[sp * 2 + lax.rem(z, 2)],
            device_id={SP: (i // 4) * 2 + to_core, SP2: i % 4}, device_id_type=MESH)

    def is_self(i):
        return own & (mine == i)

    for i in range(images):
        @pl.when(jnp.logical_not(is_self(i)))
        def _():
            send(i).start()

    @pl.when(own)
    def _():
        load = pltpu.make_async_copy(x_ref.at[mine], stage, self_sem)
        load.start()
        load.wait()
        store = pltpu.make_async_copy(stage, piece(sp, z), self_sem)
        store.start()
        store.wait()

    for s in range(8):
        src_sp, src_z = s // 2, 2 * core + s % 2

        @pl.when(jnp.logical_not((src_sp == sp) & (src_z == z)))
        def _():
            pltpu.make_async_remote_copy(
                src_ref=x_ref.at[0], dst_ref=piece(src_sp, src_z), send_sem=send_sem.at[0], recv_sem=recv_sem.at[s],
                device_id={SP: src_sp, SP2: src_z}, device_id_type=MESH).wait_recv()

    for i in range(images):
        @pl.when(jnp.logical_not(is_self(i)))
        def _():
            send(i).wait_send()


def to_images(x):
    images, rows, cols, channels = x.shape
    return pl.pallas_call(
        to_images_kernel,
        out_shape=jax.ShapeDtypeStruct((4 * rows, 2 * cols, channels), x.dtype),
        in_specs=[pl.BlockSpec(memory_space=pl.ANY)],
        out_specs=pl.BlockSpec(memory_space=pl.ANY),
        scratch_shapes=[pltpu.VMEM((rows, cols, channels), x.dtype), pltpu.SemaphoreType.DMA((8,)), pltpu.SemaphoreType.DMA((8,)), pltpu.SemaphoreType.DMA],
        compiler_params=pltpu.CompilerParams(collective_id=0, has_side_effects=True),
        name="to_images",
    )(x)


def to_tiles_kernel(h_ref, out_ref, stage, send_sem, recv_sem, self_sem):
    images, rows, cols, _ = out_ref.shape
    sp, z = lax.axis_index(SP), lax.axis_index(SP2)
    y, core = place(sp)
    mine = y * 4 + z
    from_core = z // 2
    own = from_core == core
    barrier = pltpu.get_barrier_semaphore()
    for i in range(images):
        @pl.when(jnp.logical_not(own & (mine == i)))
        def _():
            pl.semaphore_signal(barrier, inc=1, device_id={SP: (i // 4) * 2 + from_core, SP2: i % 4}, device_id_type=MESH)

    pl.semaphore_wait(barrier, 8 - own.astype(jnp.int32))

    def piece(dst_sp, dst_z):
        return h_ref.at[pl.ds(dst_sp * rows, rows), pl.ds(lax.rem(dst_z, 2) * cols, cols), :]

    def send(s):
        dst_sp, dst_z = s // 2, 2 * core + s % 2
        return pltpu.make_async_remote_copy(
            src_ref=piece(dst_sp, dst_z), dst_ref=out_ref.at[mine], send_sem=send_sem.at[s], recv_sem=recv_sem.at[mine],
            device_id={SP: dst_sp, SP2: dst_z}, device_id_type=MESH)

    def is_self(s):
        return (s // 2 == sp) & (2 * core + s % 2 == z)

    for s in range(8):
        @pl.when(jnp.logical_not(is_self(s)))
        def _():
            send(s).start()

    @pl.when(own)
    def _():
        load = pltpu.make_async_copy(piece(sp, z), stage, self_sem)
        load.start()
        load.wait()
        store = pltpu.make_async_copy(stage, out_ref.at[mine], self_sem)
        store.start()
        store.wait()

    for i in range(images):
        @pl.when(jnp.logical_not(own & (mine == i)))
        def _():
            pltpu.make_async_remote_copy(
                src_ref=piece(0, 0), dst_ref=out_ref.at[i], send_sem=send_sem.at[0], recv_sem=recv_sem.at[i],
                device_id={SP: (i // 4) * 2 + from_core, SP2: i % 4}, device_id_type=MESH).wait_recv()

    for s in range(8):
        @pl.when(jnp.logical_not(is_self(s)))
        def _():
            send(s).wait_send()


def to_tiles(h):
    rows, cols, channels = h.shape[0] // 4, h.shape[1] // 2, h.shape[2]
    return pl.pallas_call(
        to_tiles_kernel,
        out_shape=jax.ShapeDtypeStruct((8, rows, cols, channels), h.dtype),
        in_specs=[pl.BlockSpec(memory_space=pl.ANY)],
        out_specs=pl.BlockSpec(memory_space=pl.ANY),
        scratch_shapes=[pltpu.VMEM((rows, cols, channels), h.dtype), pltpu.SemaphoreType.DMA((8,)), pltpu.SemaphoreType.DMA((8,)), pltpu.SemaphoreType.DMA],
        compiler_params=pltpu.CompilerParams(collective_id=1, has_side_effects=True),
        name="to_tiles",
    )(h)


def swap_cores(value):
    return lax.ppermute(value, SP, [(0, 1), (1, 0), (2, 3), (3, 2)])


def silu(v):
    return v / (1.0 + jnp.exp(-v))

def conv_kernel(steps, mb, residual, core_ref, h_ref, other_ref, norm_ref, w_ref, add_ref, out_ref, sums_ref, act, acc):
    rows, cols, channels = h_ref.shape
    n, t = pl.program_id(0), pl.program_id(1)
    taps = 9 // steps

    @pl.when((n == 0) & (t == 0))
    def _():
        core = core_ref[0]
        mean, mult, shift = norm_ref[0:1, :], norm_ref[1:2, :], norm_ref[2:3, :]

        def activate(v):
            return silu((v.astype(jnp.float32) - mean) * mult + shift)

        zeros = jnp.zeros((cols, channels), jnp.bfloat16)
        for dx in range(3):
            act[dx, 0] = zeros
            act[dx, rows + 1] = zeros
        line = lax.broadcasted_iota(jnp.int32, (cols, channels), 0)

        def one_row(r, carry):
            u = activate(h_ref[r])
            edge = activate(other_ref[r])
            left = jnp.where(core == 1, edge, 0.0)
            right = jnp.where(core == 0, edge, 0.0)
            act[1, r + 1] = u.astype(jnp.bfloat16)
            act[0, r + 1] = jnp.where(line == 0, left, pltpu.roll(u, 1, 0)).astype(jnp.bfloat16)
            act[2, r + 1] = jnp.where(line == cols - 1, right, pltpu.roll(u, cols - 1, 0)).astype(jnp.bfloat16)
            return carry

        lax.fori_loop(0, rows, one_row, 0)

    mrows = mb // cols
    width = w_ref.shape[-1]

    def block(m, carry):
        total = None
        for k in range(taps):
            if steps == 9:
                dy, dx = t // 3, lax.rem(t, 3)
            elif steps == 3:
                dy, dx = t, k
            else:
                dy, dx = k // 3, k % 3
            lhs = act[dx, pl.ds(m * mrows + dy, mrows)].reshape(mb, channels)
            part = jnp.dot(lhs, w_ref[0, k] if steps != 1 else w_ref[dy, dx], preferred_element_type=jnp.float32)
            total = part if total is None else total + part
        rowsl = pl.ds(m * mb, mb)
        if steps > 1:
            @pl.when(t == 0)
            def _():
                acc[rowsl, :] = total
            @pl.when((t > 0) & (t < steps - 1))
            def _():
                acc[rowsl, :] += total
        def finish():
            full = acc[rowsl, :] + total if steps > 1 else total
            if residual:
                full = full + add_ref[pl.ds(m * mrows, mrows)].reshape(mb, width).astype(jnp.float32)
            else:
                full = full + add_ref[...]
            half = full.astype(jnp.bfloat16)
            out_ref[pl.ds(m * mrows, mrows)] = half.reshape(mrows, cols, width)
            kept = half.astype(jnp.float32)
            s = jnp.concatenate([jnp.sum(kept, axis=0, keepdims=True), jnp.sum(kept * kept, axis=0, keepdims=True)], axis=0)
            @pl.when(m == 0)
            def _():
                sums_ref[...] = s
            @pl.when(m > 0)
            def _():
                sums_ref[...] += s
        if steps > 1:
            pl.when(t == steps - 1)(finish)
        else:
            finish()
        return carry

    lax.fori_loop(0, rows * cols // mb, block, 0)

def conv(core, h, other, norm, w, j, add, nb=256, steps=1, mb=1024):
    rows, cols, channels = h.shape
    residual = add.ndim == 3
    outw = w.shape[-1]
    whole = lambda *s: pl.BlockSpec(s, lambda n, t: (0,) * len(s))
    if steps == 9:
        wspec = pl.BlockSpec((None, 1, 1, channels, nb), lambda n, t: (j, t // 3, t % 3, 0, n))
    elif steps == 3:
        wspec = pl.BlockSpec((None, 1, 3, channels, nb), lambda n, t: (j, t, 0, 0, n))
    else:
        wspec = pl.BlockSpec((None, 3, 3, channels, nb), lambda n, t: (j, 0, 0, 0, n))
    addspec = pl.BlockSpec((rows, cols, nb), lambda n, t: (0, 0, n)) if residual else pl.BlockSpec((1, nb), lambda n, t: (0, n))
    return pl.pallas_call(
        functools.partial(conv_kernel, steps, mb, residual),
        grid=(outw // nb, steps),
        in_specs=[pl.BlockSpec(memory_space=pltpu.SMEM), whole(rows, cols, channels), whole(rows, 1, channels), whole(3, channels), wspec, addspec],
        out_specs=[pl.BlockSpec((rows, cols, nb), lambda n, t: (0, 0, n)), pl.BlockSpec((2, nb), lambda n, t: (0, n))],
        out_shape=[jax.ShapeDtypeStruct((rows, cols, outw), jnp.bfloat16), jax.ShapeDtypeStruct((2, outw), jnp.float32)],
        scratch_shapes=[pltpu.VMEM((3, rows + 2, cols, channels), jnp.bfloat16), pltpu.VMEM((rows * cols if steps > 1 else 8, nb), jnp.float32)],
        compiler_params=pltpu.CompilerParams(vmem_limit_bytes=62 * 1024 * 1024),
        name="conv",
    )(core, h, other, norm, w, add)


NT = (((1,), (1,)), ((), ()))

def attend_kernel(q_ref, k0_ref, k1_ref, v0_ref, v1_ref, o_ref, vt):
    tokens = k0_ref.shape[0]
    @pl.when(pl.program_id(1) == 0)
    def _():
        vt[:, :tokens] = v0_ref[...].T
        vt[:, tokens:] = v1_ref[...].T
    q = q_ref[...] * jnp.bfloat16(0.125)
    lane = lax.broadcasted_iota(jnp.int32, q.shape, 1)
    outs = []
    for head in range(2):
        keep = (lane >= 64) if head else (lane < 64)
        qh = jnp.where(keep, q, jnp.zeros_like(q))
        s0 = lax.dot_general(k0_ref[...], qh, NT, preferred_element_type=jnp.float32)
        s1 = lax.dot_general(k1_ref[...], qh, NT, preferred_element_type=jnp.float32)
        peak = jnp.maximum(jnp.max(s0, axis=0, keepdims=True), jnp.max(s1, axis=0, keepdims=True))
        p0 = jnp.exp(s0 - peak)
        p1 = jnp.exp(s1 - peak)
        total = jnp.sum(p0, axis=0, keepdims=True) + jnp.sum(p1, axis=0, keepdims=True)
        vh = vt[64 * head:64 * head + 64, :]
        acc = jnp.dot(vh[:, :tokens], p0.astype(jnp.bfloat16), preferred_element_type=jnp.float32)
        acc = acc + jnp.dot(vh[:, tokens:], p1.astype(jnp.bfloat16), preferred_element_type=jnp.float32)
        outs.append(acc / total)
    o_ref[...] = jnp.concatenate(outs, axis=0).T.astype(o_ref.dtype)

def attend(query, keys, vals, other_keys, other_vals, block=512):
    tokens, width = query.shape
    kv = lambda p, b: (0, p)
    return pl.pallas_call(
        attend_kernel, grid=(width // 128, tokens // block),
        in_specs=[pl.BlockSpec((block, 128), lambda p, b: (b, p))] + [pl.BlockSpec((tokens, 128), kv)] * 4,
        out_specs=pl.BlockSpec((block, 128), lambda p, b: (b, p)),
        out_shape=jax.ShapeDtypeStruct((tokens, width), jnp.bfloat16),
        scratch_shapes=[pltpu.VMEM((128, 2 * tokens), jnp.bfloat16)],
        compiler_params=pltpu.CompilerParams(vmem_limit_bytes=60 * 1024 * 1024), name="attend",
    )(query, keys, other_keys, vals, other_vals)


def norm_rows(sums, scale, shift, count):
    channels = sums.shape[1]
    width = channels // GROUPS
    grouped = jnp.sum(sums.reshape(2, GROUPS, width), axis=-1)
    moments = (grouped + swap_cores(grouped)) / count
    mean = moments[0]
    inv_std = lax.rsqrt(moments[1] - mean * mean + NORM_EPS)
    return jnp.stack([jnp.repeat(mean, width), jnp.repeat(inv_std, width) * scale.astype(jnp.float32), shift.astype(jnp.float32)])


def channel_sums(half):
    wide = half.astype(jnp.float32)
    return jnp.stack([jnp.sum(wide, axis=(0, 1)), jnp.sum(wide * wide, axis=(0, 1))])


def edge_of(half, core):
    return swap_cores(jnp.where(core == 0, half[:, -1:], half[:, :1]))


def res_block(half, sums, time_vec, gn_scale, gn_shift, conv_w, norm_idx, conv_idx, core):
    count = 2 * half.shape[0] * half.shape[1] * (half.shape[2] // GROUPS)
    core_arg = core.reshape(1).astype(jnp.int32)
    norm = norm_rows(sums, gn_scale[norm_idx], gn_shift[norm_idx], count)
    hidden, sums = conv(core_arg, half, edge_of(half, core), norm, conv_w, conv_idx, time_vec[None])
    norm = norm_rows(sums, gn_scale[norm_idx + 1], gn_shift[norm_idx + 1], count)
    return conv(core_arg, hidden, edge_of(hidden, core), norm, conv_w, conv_idx + 1, half)


def attention_block(half, sums, scale, shift, w_qkv, w_out):
    rows, cols, channels = half.shape
    norm = norm_rows(sums, scale, shift, 2 * rows * cols * (channels // GROUPS))
    normed = ((half.astype(jnp.float32) - norm[0]) * norm[1] + norm[2]).astype(jnp.bfloat16).reshape(rows * cols, channels)
    flat = w_qkv.reshape(3, channels, channels)

    def project(weight):
        return jnp.dot(normed, weight, preferred_element_type=jnp.float32).astype(jnp.bfloat16)

    keys, vals = project(flat[1]), project(flat[2])
    other_keys, other_vals = swap_cores(keys), swap_cores(vals)
    query = project(flat[0])
    attended = attend(query, keys, vals, other_keys, other_vals)
    out = jnp.dot(attended, w_out.reshape(channels, channels), preferred_element_type=jnp.float32)
    return (half.astype(jnp.float32) + out.reshape(half.shape)).astype(jnp.bfloat16)


def solution(mesh):
    lat_spec = P("dp", "sp", "sp2", None)

    def local(x, time_emb, gn_scale, gn_shift, conv_w, time_w, w_qkv, w_out):
        y, core = place(lax.axis_index(SP))
        image = y * 4 + lax.axis_index(SP2)
        time_act = jax.nn.silu(time_emb.astype(jnp.float32)).astype(jnp.bfloat16)
        time_vecs = jnp.einsum("bt,stc->sbc", time_act, time_w, preferred_element_type=jnp.float32)
        time_vecs = lax.dynamic_index_in_dim(time_vecs, image, 1, keepdims=False)
        half = to_images(x)
        first, sums = res_block(half, channel_sums(half), time_vecs[0], gn_scale, gn_shift, conv_w, 0, 0, core)
        middle = attention_block(first, sums, gn_scale[2], gn_shift[2], w_qkv, w_out)
        last, _ = res_block(middle, channel_sums(middle), time_vecs[1], gn_scale, gn_shift, conv_w, 3, 2, core)
        return to_tiles(last)

    return jax.shard_map(local, mesh=mesh, in_specs=(lat_spec, P("dp", None), P(), P(), P(), P(), P(), P()), out_specs=lat_spec, check_vma=False)
```

time: 1410 us -> 413 us (0.29); the launches traced: 1380 us -> 413 us
  matrix products: 496 us -> 23.7 us
  waiting for transfers between devices: 428 us -> 2.96 us
  Pallas kernels: 0 us -> 334 us
  blocking collectives: 171 us -> 0 us
  other arithmetic: 160 us -> 11.8 us
  local copies, waits for them, and re-layouts: 67.8 us -> 20.6 us
  starting transfers between devices: 45.7 us -> 19.8 us
  between operations: 14.7 us -> 0.38 us
    all_gather x1 -> x0, waiting for transfers between devices: 416 us -> none  [attention_block(): gathered = lax.all_gather(key_val, SPACE)]
    pallas_call x0 -> x7, Pallas kernels: none -> 334 us  [the longest x4 156 us: conv(): pl.pallas_call(functools.partial(conv_kernel, steps, mb, residual), grid=...]
    dot_general x35 -> x4, matrix products: 352 us -> 19.8 us  [the longest x3 12.7 us: project(): jnp.dot(normed, weight, preferred_element_type=jnp.float32)]
    psum x5 -> x0, blocking collectives: 171 us -> none  [group_norm(): moments = lax.psum(local_moments, SPACE)]
    conv_general_dilated x4 -> x0, matrix products: 140 us -> none  [conv3x3(): lax.conv_general_dilated(padded, kernel, (1, 1), 'VALID', dimension_numbe...]
    reduce_sum x28 -> x6, other arithmetic: 119 us -> 2.93 us  [the longest x1 2.49 us: channel_sums(): jnp.sum(wide, axis=(0, 1))]
    convert_element_type x4 -> x0, local copies, waits for them, and re-layouts: 26.2 us -> none  [the longest x1 11.3 us: attention_block(): jnp.einsum('bijc,schd->sbijhd', normed, w_qkv[1:], preferred_element_type...]
    ppermute x16 -> x11, starting transfers between devices: 45.7 us -> 19.8 us  [swap_cores(): return lax.ppermute(value, SP, [(0, 1), (1, 0), (2, 3), (3, 2)])]
  transfers between devices with their start and end apart: 17 -> 11, of which waited for: 11 -> 3; matrix products, arithmetic and copies ran while one was open for 2% -> 6% of each run, Pallas kernels for 0% -> 0%
where the time goes in v1:
time: 413 us
  Pallas kernels  334 us (81%)
  matrix products  23.7 us (6%)
  local copies, waits for them, and re-layouts  20.6 us (5%)
  starting transfers between devices  19.8 us (5%)
  other arithmetic  11.8 us (3%)
    pallas_call x4, Pallas kernels, conv(): pl.pallas_call(functools.partial(conv_kernel, steps, mb, residual), grid=...  156 us
    pallas_call x1, Pallas kernels, attend(): pl.pallas_call(attend_kernel, grid=(width // 128, tokens // block), in_sp...  68.9 us
    pallas_call x1, Pallas kernels, to_tiles(): pl.pallas_call(to_tiles_kernel, out_shape=jax.ShapeDtypeStruct((8, rows,...  62.7 us
    pallas_call x1, Pallas kernels, to_images(): pl.pallas_call(to_images_kernel, out_shape=jax.ShapeDtypeStruct((4 * rows...  45.8 us
    ppermute x11, starting transfers between devices, swap_cores(): return lax.ppermute(value, SP, [(0, 1), (1, 0), (2, 3), (3, 2)])  19.8 us
    dot_general x3, matrix products, project(): jnp.dot(normed, weight, preferred_element_type=jnp.float32)  12.7 us
    unnamed x29, local copies, waits for them, and re-layouts  8.42 us
  transfers between devices with their start and end apart: 11, of which 3 were waited for; matrix products, arithmetic and copies ran while one was open for 6% of the time, Pallas kernels for 0%

profile of v1, /device:TPU:31, one launch (start us, length us, event | category | flops | bytes accessed | tf_op | source)
XLA Modules:
  0.0 412.9 jit_solution(17375533791078007156)
XLA Ops:
  0.0 45.8 %to_images.1.h_ref.add_ref = bf16[16,64,1280]{2,1,0:T(8,128)(2,1)} custom-call(bf16[8,4,32,1280]{3,2,1,0:T(8,128)(2,1)} %x_ref.1), custom_call_target="tpu_custom_call" | custom-call | tf_op jit(solution)/shard_map/to_images/pallas_call | solution.py:79
  45.8 2.5 convert_reduce_fusion.1
  48.3 0.1 stack.38
  48.4 0.1 maximum_reduce_fusion
  48.5 17.2 %collective-permute-start.1 = (f32[2,32]{1,0:T(2,128)S(1)}, f32[2,32]{1,0:T(2,128)S(1)}, u32[]{:S(2)}, u32[]{:S(2)}) collective-permute-start(f32[2,32]{1,0:T(2,128)S(1)} %maximum_reduce_fusion), channel_id=1, source_target_pairs={{0,1},{1,0},{2,3},{3,2},{4,5},{5,4},{6,7},{7,6},{8,9},{9,8},{10,11... | collective-permute-start | bytes 776 | tf_op jit(solution)/shard_map/ppermute | solution.py:158
  65.7 1.2 broadcast_select_fusion.3
  66.9 0.1 collective-permute-start
  67.1 7.1 %fusion.25 = (bf16[1,1280,20,64]{1,3,2,0:T(8,128)(2,1)}, bf16[1,1280,20,64]{1,3,2,0:T(8,128)(2,1)}, bf16[1,1280,20,64]{1,3,2,0:T(8,128)(2,1)}) fusion(bf16[3,1280,20,64]{1,3,2,0:T(8,128)(2,1)} %param.14), kind=kLoop, calls=%fused_computation.72 | loop fusion | bytes 19660800 | tf_op jit(solution)/shard_map/slice | solution.py:342
  74.2 3.8 fusion.11
  78.0 0.6 dynamic-slice_bitcast_fusion
  78.8 0.1 stack_reshape.12
  78.9 0.1 reshape.85
  79.0 0.6 pad_maximum_fusion.norm_ref
  79.7 0.7 copy-done.7
  80.3 38.9 %conv.4 = (bf16[16,64,1280]{2,1,0:T(8,128)(2,1)}, f32[2,1280]{1,0:T(2,128)}) custom-call(s32[1]{0:T(128)} %bitcast.core_ref, bf16[16,64,1280]{2,1,0:T(8,128)(2,1)} %to_images.1.h_ref.add_ref, bf16[16,1,1280]{2,1,0:T(2,128)(2,1)} %copy-done.7, f32[3,1280]{1,0:T(4,128)} %pad_maximum_fusion.norm_ref, bf16[4,3,3,1280,1280]{4,3,2,1,0:T(8,128)(2,1)} %w_ref.7, ...), custom_call_target="tpu_custom_call" | custom-call | tf_op jit(solution)/shard_map/conv/pallas_call | solution.py:254
  119.3 0.8 reshape.86
  120.1 0.1 reduce_sum.84
  120.2 0.5 collective-permute-start.3
  120.6 1.2 broadcast_select_fusion.2
  121.8 0.1 collective-permute-start.2
  122.0 0.1 stack_reshape.13
  122.2 0.1 reshape.87
  122.3 0.6 pad_maximum_fusion.1.norm_ref
  123.0 0.2 collective-permute-done.2.other_ref
  123.2 0.6 copy-done.8
  123.8 39.1 %conv.5 = (bf16[16,64,1280]{2,1,0:T(8,128)(2,1)}, f32[2,1280]{1,0:T(2,128)}) custom-call(s32[1]{0:T(128)} %bitcast.core_ref, bf16[16,64,1280]{2,1,0:T(8,128)(2,1)} %get-tuple-element.12.h_ref, bf16[16,1,1280]{2,1,0:T(2,128)(2,1)} %copy-done.8, f32[3,1280]{1,0:T(4,128)} %pad_maximum_fusion.1.norm_ref, bf16[4,3,3,1280,1280]{4,3,2,1,0:T(8,128)(2,1)} %w_ref.7, ...), custom_call_target="tpu_custom_call" | custom-call | tf_op jit(solution)/shard_map/conv/pallas_call | solution.py:254
  162.9 0.9 reshape.88
  163.9 0.1 reduce_sum.85
  164.0 0.3 collective-permute-start.4
  164.2 0.9 collective-permute-done.4
  165.2 0.1 sub.32
  165.4 0.1 reshape.89
  165.5 2.5 fusion.3
  168.0 3.8 convolution_convert_fusion.v0_ref
  171.9 4.0 convolution_convert_fusion.1.k0_ref
  175.9 0.3 collective-permute-start.5
  176.2 0.3 collective-permute-start.6
  176.5 4.8 %convolution_convert_fusion.2.q_ref = bf16[1024,1280]{1,0:T(8,128)(2,1)} fusion(bf16[1024,1280]{1,0:T(8,128)(2,1)S(1)} %bitcast.80, bf16[1280,1280]{0,1:T(8,128)(2,1)S(1)} %bitcast.75), kind=kOutput, calls=%fused_computation.14 | convolution fusion | flops 3356753920 | bytes 8519680 | tf_op jit(solution)/shard_map/dot_general | solution.py:340
  181.4 1.5 copy-done.6
  182.8 1.8 collective-permute-done.6.v1_ref
  184.6 68.9 %attend.1 = bf16[1024,1280]{1,0:T(8,128)(2,1)} custom-call(bf16[1024,1280]{1,0:T(8,128)(2,1)} %convolution_convert_fusion.2.q_ref, bf16[1024,1280]{1,0:T(8,128)(2,1)} %copy-done.5, bf16[1024,1280]{1,0:T(8,128)(2,1)} %copy-done.6, bf16[1024,1280]{1,0:T(8,128)(2,1)} %copy-done.4, bf16[1024,1280]{1,0:T(8,128)(2,1)} %collective-permute-done.6.v1_ref), custom_call_target="tpu_custom_call" | custom-call | tf_op jit(solution)/shard_map/attend/pallas_call | solution.py:295
  253.5 7.2 %convert_reduce_fusion = (f32[1280]{0:T(1024)S(1)}, f32[1280]{0:T(1024)S(1)}, bf16[16,64,1280]{2,1,0:T(8,128)(2,1)S(1)}) fusion(bf16[16,64,1280]{2,1,0:T(8,128)(2,1)} %bitcast.81, bf16[1280,1280,1]{1,0,2:T(8,128)(2,1)} %bitcast.82, bf16[16,64,1280]{2,1,0:T(8,128)(2,1)} %get-tuple-element.14), kind=kOutput, calls=%fused_computation.1 | convolution fusion | flops 3364615680 | bytes 11151360 | tf_op jit(solution)/shard_map/dot_general | solution.py:346
  260.9 0.1 maximum_reduce_fusion.1
  261.0 0.3 collective-permute-start.8
  261.2 1.0 copy-done
  262.2 0.1 broadcast_select_fusion.1
  262.3 0.3 collective-permute-start.7
  262.7 0.1 stack_reshape.14
  262.9 0.1 reshape.92
  263.0 0.6 pad_maximum_fusion.2.norm_ref
  263.7 0.6 copy-done.10
  264.3 39.0 %conv.6 = (bf16[16,64,1280]{2,1,0:T(8,128)(2,1)}, f32[2,1280]{1,0:T(2,128)}) custom-call(s32[1]{0:T(128)} %bitcast.core_ref, bf16[16,64,1280]{2,1,0:T(8,128)(2,1)} %copy-done, bf16[16,1,1280]{2,1,0:T(2,128)(2,1)} %copy-done.10, f32[3,1280]{1,0:T(4,128)} %pad_maximum_fusion.2.norm_ref, bf16[4,3,3,1280,1280]{4,3,2,1,0:T(8,128)(2,1)} %w_ref.7, ...), custom_call_target="tpu_custom_call" | custom-call | tf_op jit(solution)/shard_map/conv/pallas_call | solution.py:254
  303.3 0.8 reshape.93
  304.1 0.1 reduce_sum.89
  304.2 0.3 collective-permute-start.10
  304.5 1.2 broadcast_select_fusion
  305.7 0.3 collective-permute-start.9
  306.1 0.1 stack_reshape.15
  306.3 0.1 reshape.94
  306.4 0.6 pad_maximum_fusion.3.norm_ref
  307.0 0.6 copy-done.9
  307.6 39.1 %conv.7 = (bf16[16,64,1280]{2,1,0:T(8,128)(2,1)}, f32[2,1280]{1,0:T(2,128)}) custom-call(s32[1]{0:T(128)} %bitcast.core_ref, bf16[16,64,1280]{2,1,0:T(8,128)(2,1)} %get-tuple-element.16.h_ref, bf16[16,1,1280]{2,1,0:T(2,128)(2,1)} %copy-done.9, f32[3,1280]{1,0:T(4,128)} %pad_maximum_fusion.3.norm_ref, bf16[4,3,3,1280,1280]{4,3,2,1,0:T(8,128)(2,1)} %w_ref.7, ...), custom_call_target="tpu_custom_call" | custom-call | tf_op jit(solution)/shard_map/conv/pallas_call | solution.py:254
  346.8 62.7 %to_tiles.1 = bf16[8,4,32,1280]{3,2,1,0:T(8,128)(2,1)} custom-call(bf16[16,64,1280]{2,1,0:T(8,128)(2,1)} %get-tuple-element.18.h_ref), custom_call_target="tpu_custom_call" | custom-call | tf_op jit(solution)/shard_map/to_tiles/pallas_call | solution.py:146
  409.5 3.4 copy.10
  (65 shorter events, 1.2 us)
Async XLA Ops:
  0.0 67.0 %copy-start.11 = (bf16[5,1280]{1,0:T(8,128)(2,1)S(1)}, bf16[5,1280]{1,0:T(8,128)(2,1)}, u32[]{:S(2)}) copy-start(bf16[5,1280]{1,0:T(8,128)(2,1)} %param.11) | copy-start | bytes 38404
  48.5 30.1 %collective-permute-start.1 = (f32[2,32]{1,0:T(2,128)S(1)}, f32[2,32]{1,0:T(2,128)S(1)}, u32[]{:S(2)}, u32[]{:S(2)}) collective-permute-start(f32[2,32]{1,0:T(2,128)S(1)} %maximum_reduce_fusion), channel_id=1, source_target_pairs={{0,1},{1,0},{2,3},{3,2},{4,5},{5,4},{6,7},{7,6},{8,9},{9,8},{10,11... | collective-permute-start | bytes 776 | tf_op jit(solution)/shard_map/ppermute | solution.py:158
  66.9 12.7 %collective-permute-start = (bf16[16,1,1280]{2,1,0:T(2,128)(2,1)S(1)}, bf16[16,1,1280]{2,1,0:T(2,128)(2,1)S(1)}, u32[]{:S(2)}, u32[]{:S(2)}) collective-permute-start(bf16[16,1,1280]{2,1,0:T(2,128)(2,1)S(1)} %broadcast_select_fusion.3), channel_id=1, source_target_pairs={{0,1},{1,0},{2,3},{3,2},{4,5},{5,4},{6,7},{7,6},{8,9},{9,8},{10,11... | collective-permute-start | bytes 122888 | tf_op jit(solution)/shard_map/ppermute | solution.py:158
  67.1 7.1 %copy-start.13 = (bf16[8,1280]{1,0:T(8,128)(2,1)S(1)}, bf16[8,1280]{1,0:T(8,128)(2,1)}, u32[]{:S(2)}) copy-start(bf16[8,1280]{1,0:T(8,128)(2,1)} %param.9) | copy-start | bytes 61444
  74.2 4.8 %copy-start.12 = (bf16[5,1280]{1,0:T(8,128)(2,1)S(1)}, bf16[5,1280]{1,0:T(8,128)(2,1)}, u32[]{:S(2)}) copy-start(bf16[5,1280]{1,0:T(8,128)(2,1)} %param.10) | copy-start | bytes 38404
  79.7 0.7 copy-start.7
  120.2 1.8 collective-permute-start.3
  121.8 1.3 collective-permute-start.2
  123.2 0.6 copy-start.8
  162.9 5.1 %copy-start.3 = (bf16[1,1280,20,64]{1,3,2,0:T(8,128)(2,1)S(1)}, bf16[1,1280,20,64]{1,3,2,0:T(8,128)(2,1)}, u32[]{:S(2)}) copy-start(bf16[1,1280,20,64]{1,3,2,0:T(8,128)(2,1)} %get-tuple-element.23) | copy-start | bytes 9830404
  164.0 1.2 collective-permute-start.4
  168.0 3.9 copy-start.2
  171.9 4.4 %copy-start.4 = (bf16[1024,1280]{1,0:T(8,128)(2,1)}, bf16[1024,1280]{1,0:T(8,128)(2,1)S(1)}, u32[]{:S(2)}) copy-start(bf16[1024,1280]{1,0:T(8,128)(2,1)S(1)} %convolution_convert_fusion.v0_ref) | copy-start | bytes 7864324
  171.9 4.6 %copy-start.1 = (bf16[1,1280,20,64]{1,3,2,0:T(8,128)(2,1)S(1)}, bf16[1,1280,20,64]{1,3,2,0:T(8,128)(2,1)}, u32[]{:S(2)}) copy-start(bf16[1,1280,20,64]{1,3,2,0:T(8,128)(2,1)} %get-tuple-element.24) | copy-start | bytes 9830404
  175.9 5.4 %copy-start.5 = (bf16[1024,1280]{1,0:T(8,128)(2,1)}, bf16[1024,1280]{1,0:T(8,128)(2,1)S(1)}, u32[]{:S(2)}) copy-start(bf16[1024,1280]{1,0:T(8,128)(2,1)S(1)} %convolution_convert_fusion.1.k0_ref) | copy-start | bytes 7864324
  175.9 5.4 %collective-permute-start.5 = (bf16[1024,1280]{1,0:T(8,128)(2,1)S(1)}, bf16[1024,1280]{1,0:T(8,128)(2,1)S(1)}, u32[]{:S(2)}, u32[]{:S(2)}) collective-permute-start(bf16[1024,1280]{1,0:T(8,128)(2,1)S(1)} %convolution_convert_fusion.1.k0_ref), channel_id=1, source_target_pairs={{0,1},{1,0},{2,3},{3,2},{4,5},{5,4},{6,7},{7,6},{8,9},{9,8},{10,11... | collective-permute-start | bytes 7864328 | tf_op jit(solution)/shard_map/ppermute | solution.py:158
  176.2 8.4 %collective-permute-start.6 = (bf16[1024,1280]{1,0:T(8,128)(2,1)S(1)}, bf16[1024,1280]{1,0:T(8,128)(2,1)}, u32[]{:S(2)}, u32[]{:S(2)}) collective-permute-start(bf16[1024,1280]{1,0:T(8,128)(2,1)S(1)} %convolution_convert_fusion.v0_ref), channel_id=1, source_target_pairs={{0,1},{1,0},{2,3},{3,2},{4,5},{5,4},{6,7},{7,6},{8,9},{9,8},{10,11... | collective-permute-start | bytes 7864328 | tf_op jit(solution)/shard_map/ppermute | solution.py:158
  181.3 1.5 copy-start.6
  260.7 1.5 copy-start
  261.0 1.7 collective-permute-start.8
  262.3 1.3 collective-permute-start.7
  263.7 0.6 copy-start.10
  304.2 1.8 collective-permute-start.10
  305.7 1.3 collective-permute-start.9
  307.0 0.6 copy-start.9

commit v2 on v1

v2 whole, which is shorter than its diff:
```python
import functools

import jax
import jax.numpy as jnp
from jax import lax
from jax.experimental import pallas as pl
from jax.experimental.pallas import tpu as pltpu
from jax.sharding import PartitionSpec as P

GROUPS = 32
NORM_EPS = 1e-5
MESH = pl.DeviceIdType.MESH
SP, SP2 = "sp", "sp2"


def place(sp, cores=2):
    return sp // cores, lax.rem(sp, cores)


def to_images_kernel(x_ref, out_ref, stage, send_sem, recv_sem, self_sem):
    images, rows, cols, _ = x_ref.shape
    sp, z = lax.axis_index(SP), lax.axis_index(SP2)
    y, core = place(sp)
    mine = y * 4 + z
    to_core = z // 2
    own = to_core == core
    barrier = pltpu.get_barrier_semaphore()
    for s in range(8):
        src_sp, src_z = s // 2, 2 * core + s % 2

        @pl.when(jnp.logical_not((src_sp == sp) & (src_z == z)))
        def _():
            pl.semaphore_signal(barrier, inc=1, device_id={SP: src_sp, SP2: src_z}, device_id_type=MESH)

    pl.semaphore_wait(barrier, 8 - own.astype(jnp.int32))

    def piece(src_sp, src_z):
        return out_ref.at[pl.ds(src_sp * rows, rows), pl.ds(lax.rem(src_z, 2) * cols, cols), :]

    def send(i):
        return pltpu.make_async_remote_copy(
            src_ref=x_ref.at[i], dst_ref=piece(sp, z), send_sem=send_sem.at[i], recv_sem=recv_sem.at[sp * 2 + lax.rem(z, 2)],
            device_id={SP: (i // 4) * 2 + to_core, SP2: i % 4}, device_id_type=MESH)

    def is_self(i):
        return own & (mine == i)

    for i in range(images):
        @pl.when(jnp.logical_not(is_self(i)))
        def _():
            send(i).start()

    @pl.when(own)
    def _():
        load = pltpu.make_async_copy(x_ref.at[mine], stage, self_sem)
        load.start()
        load.wait()
        store = pltpu.make_async_copy(stage, piece(sp, z), self_sem)
        store.start()
        store.wait()

    for s in range(8):
        src_sp, src_z = s // 2, 2 * core + s % 2

        @pl.when(jnp.logical_not((src_sp == sp) & (src_z == z)))
        def _():
            pltpu.make_async_remote_copy(
                src_ref=x_ref.at[0], dst_ref=piece(src_sp, src_z), send_sem=send_sem.at[0], recv_sem=recv_sem.at[s],
                device_id={SP: src_sp, SP2: src_z}, device_id_type=MESH).wait_recv()

    for i in range(images):
        @pl.when(jnp.logical_not(is_self(i)))
        def _():
            send(i).wait_send()


def to_images(x):
    images, rows, cols, channels = x.shape
    return pl.pallas_call(
        to_images_kernel,
        out_shape=jax.ShapeDtypeStruct((4 * rows, 2 * cols, channels), x.dtype),
        in_specs=[pl.BlockSpec(memory_space=pl.ANY)],
        out_specs=pl.BlockSpec(memory_space=pl.ANY),
        scratch_shapes=[pltpu.VMEM((rows, cols, channels), x.dtype), pltpu.SemaphoreType.DMA((8,)), pltpu.SemaphoreType.DMA((8,)), pltpu.SemaphoreType.DMA],
        compiler_params=pltpu.CompilerParams(collective_id=0, has_side_effects=True),
        name="to_images",
    )(x)


def swap_cores(value):
    return lax.ppermute(value, SP, [(0, 1), (1, 0), (2, 3), (3, 2)])


def silu(v):
    return v / (1.0 + jnp.exp(-v))


def fill_act(core, h_ref, other_ref, norm_ref, act):
    rows, cols, channels = h_ref.shape
    mean, mult, shift = norm_ref[0:1, :], norm_ref[1:2, :], norm_ref[2:3, :]

    def activate(v):
        return silu((v.astype(jnp.float32) - mean) * mult + shift)

    zeros = jnp.zeros((cols, channels), jnp.bfloat16)
    for dx in range(3):
        act[dx, 0] = zeros
        act[dx, rows + 1] = zeros
    line = lax.broadcasted_iota(jnp.int32, (cols, channels), 0)

    def one_row(r, carry):
        u = activate(h_ref[r])
        edge = activate(other_ref[r])
        left = jnp.where(core == 1, edge, 0.0)
        right = jnp.where(core == 0, edge, 0.0)
        act[1, r + 1] = u.astype(jnp.bfloat16)
        act[0, r + 1] = jnp.where(line == 0, left, pltpu.roll(u, 1, 0)).astype(jnp.bfloat16)
        act[2, r + 1] = jnp.where(line == cols - 1, right, pltpu.roll(u, cols - 1, 0)).astype(jnp.bfloat16)
        return carry

    lax.fori_loop(0, rows, one_row, 0)


def taps(act, w_ref, rows, cols, channels):
    total = None
    for k in range(9):
        lhs = act[k % 3, pl.ds(k // 3, rows)].reshape(rows * cols, channels)
        part = jnp.dot(lhs, w_ref[k // 3, k % 3], preferred_element_type=jnp.float32)
        total = part if total is None else total + part
    return total


def conv_kernel(residual, h_ref, other_ref, norm_ref, w_ref, add_ref, out_ref, sums_ref, edge_ref, act):
    rows, cols, channels = h_ref.shape
    width = w_ref.shape[-1]
    _, core = place(lax.axis_index(SP))

    @pl.when(pl.program_id(0) == 0)
    def _():
        fill_act(core, h_ref, other_ref, norm_ref, act)

    full = taps(act, w_ref, rows, cols, channels)
    full = full + (add_ref[...].reshape(rows * cols, width).astype(jnp.float32) if residual else add_ref[...])
    half = full.astype(jnp.bfloat16)
    out_ref[...] = half.reshape(rows, cols, width)
    kept = half.astype(jnp.float32)
    sums_ref[...] = jnp.concatenate([jnp.sum(kept, axis=0, keepdims=True), jnp.sum(kept * kept, axis=0, keepdims=True)], axis=0)

    @pl.when(core == 0)
    def _():
        edge_ref[...] = out_ref[:, cols - 1:, :]

    @pl.when(core == 1)
    def _():
        edge_ref[...] = out_ref[:, :1, :]


def conv_specs(rows, cols, channels, j, nb, residual):
    whole = lambda *s: pl.BlockSpec(s, lambda n: (0,) * len(s))
    add = pl.BlockSpec((rows, cols, nb), lambda n: (0, 0, n)) if residual else pl.BlockSpec((1, nb), lambda n: (0, n))
    return [whole(rows, cols, channels), whole(rows, 1, channels), whole(3, channels), pl.BlockSpec((None, 3, 3, channels, nb), lambda n: (j, 0, 0, 0, n)), add]


def conv_cost(rows, cols, channels):
    return pl.CostEstimate(flops=18 * rows * cols * channels * channels, bytes_accessed=18 * channels * channels, transcendentals=rows * cols * channels)


def conv(h, other, norm, w, j, add, nb=256):
    rows, cols, channels = h.shape
    return pl.pallas_call(
        functools.partial(conv_kernel, add.ndim == 3),
        grid=(channels // nb,),
        in_specs=conv_specs(rows, cols, channels, j, nb, add.ndim == 3),
        out_specs=[pl.BlockSpec((rows, cols, nb), lambda n: (0, 0, n)), pl.BlockSpec((2, nb), lambda n: (0, n)), pl.BlockSpec((rows, 1, nb), lambda n: (0, 0, n))],
        out_shape=[jax.ShapeDtypeStruct((rows, cols, channels), jnp.bfloat16), jax.ShapeDtypeStruct((2, channels), jnp.float32), jax.ShapeDtypeStruct((rows, 1, channels), jnp.bfloat16)],
        scratch_shapes=[pltpu.VMEM((3, rows + 2, cols, channels), jnp.bfloat16)],
        compiler_params=pltpu.CompilerParams(vmem_limit_bytes=62 * 1024 * 1024),
        cost_estimate=conv_cost(rows, cols, channels),
        name="conv",
    )(h, other, norm, w, add)


def conv_out_kernel(h_ref, other_ref, norm_ref, w_ref, add_ref, out_ref, act, done, send_sem, recv_sem, self_sem):
    rows, cols, channels = h_ref.shape
    images, trows, tcols, _ = out_ref.shape
    width = w_ref.shape[-1]
    n, chunks = pl.program_id(0), pl.num_programs(0)
    sp, z = lax.axis_index(SP), lax.axis_index(SP2)
    y, core = place(sp)
    mine = y * 4 + z
    from_core = z // 2
    own = from_core == core

    @pl.when(n == 0)
    def _():
        barrier = pltpu.get_barrier_semaphore()
        for i in range(images):
            @pl.when(jnp.logical_not(own & (mine == i)))
            def _():
                pl.semaphore_signal(barrier, inc=1, device_id={SP: (i // 4) * 2 + from_core, SP2: i % 4}, device_id_type=MESH)

        fill_act(core, h_ref, other_ref, norm_ref, act)
        pl.semaphore_wait(barrier, 8 - own.astype(jnp.int32))

    full = taps(act, w_ref, rows, cols, channels) + add_ref[...].reshape(rows * cols, width).astype(jnp.float32)
    done[n] = full.astype(jnp.bfloat16).reshape(rows, cols, width)

    def lanes(c):
        return pl.ds(pl.multiple_of(c * width, width), width)

    def piece(c, dst_sp, dst_z):
        return done.at[c, pl.ds(dst_sp * trows, trows), pl.ds(pl.multiple_of(lax.rem(dst_z, 2) * tcols, tcols), tcols), :]

    def send(c, s):
        dst_sp, dst_z = s // 2, 2 * core + s % 2
        return pltpu.make_async_remote_copy(
            src_ref=piece(c, dst_sp, dst_z), dst_ref=out_ref.at[mine, :, :, lanes(c)], send_sem=send_sem.at[c, s], recv_sem=recv_sem.at[c, mine],
            device_id={SP: dst_sp, SP2: dst_z}, device_id_type=MESH)

    def keep(c):
        return pltpu.make_async_copy(piece(c, sp, z), out_ref.at[mine, :, :, lanes(c)], self_sem.at[c])

    def is_self(s):
        return (s // 2 == sp) & (2 * core + s % 2 == z)

    for s in range(8):
        @pl.when(jnp.logical_not(is_self(s)))
        def _():
            send(n, s).start()

    @pl.when(own)
    def _():
        keep(n).start()

    @pl.when(n == chunks - 1)
    def _():
        def drain(c, carry):
            for i in range(images):
                @pl.when(jnp.logical_not(own & (mine == i)))
                def _():
                    pltpu.make_async_remote_copy(
                        src_ref=piece(c, 0, 0), dst_ref=out_ref.at[i, :, :, lanes(c)], send_sem=send_sem.at[c, 0], recv_sem=recv_sem.at[c, i],
                        device_id={SP: (i // 4) * 2 + from_core, SP2: i % 4}, device_id_type=MESH).wait_recv()

            for s in range(8):
                @pl.when(jnp.logical_not(is_self(s)))
                def _():
                    send(c, s).wait_send()

            @pl.when(own)
            def _():
                keep(c).wait()
            return carry

        lax.fori_loop(0, channels // width, drain, 0)


def conv_out(h, other, norm, w, j, add, nb=256):
    rows, cols, channels = h.shape
    chunks = channels // nb
    return pl.pallas_call(
        conv_out_kernel,
        grid=(chunks,),
        in_specs=conv_specs(rows, cols, channels, j, nb, True),
        out_specs=pl.BlockSpec(memory_space=pl.ANY),
        out_shape=jax.ShapeDtypeStruct((8, rows // 4, cols // 2, channels), jnp.bfloat16),
        scratch_shapes=[pltpu.VMEM((3, rows + 2, cols, channels), jnp.bfloat16), pltpu.VMEM((chunks, rows, cols, nb), jnp.bfloat16),
                        pltpu.SemaphoreType.DMA((chunks, 8)), pltpu.SemaphoreType.DMA((chunks, 8)), pltpu.SemaphoreType.DMA((chunks,))],
        compiler_params=pltpu.CompilerParams(collective_id=1, has_side_effects=True, vmem_limit_bytes=62 * 1024 * 1024),
        cost_estimate=conv_cost(rows, cols, channels),
        name="conv_out",
    )(h, other, norm, w, add)


NT = (((1,), (1,)), ((), ()))

def attend_kernel(q_ref, k0_ref, k1_ref, v0_ref, v1_ref, o_ref, vt):
    tokens = k0_ref.shape[0]
    @pl.when(pl.program_id(1) == 0)
    def _():
        vt[:, :tokens] = v0_ref[...].T
        vt[:, tokens:] = v1_ref[...].T
    q = q_ref[...] * jnp.bfloat16(0.125)
    lane = lax.broadcasted_iota(jnp.int32, q.shape, 1)
    outs = []
    for head in range(2):
        keep = (lane >= 64) if head else (lane < 64)
        qh = jnp.where(keep, q, jnp.zeros_like(q))
        s0 = lax.dot_general(k0_ref[...], qh, NT, preferred_element_type=jnp.float32)
        s1 = lax.dot_general(k1_ref[...], qh, NT, preferred_element_type=jnp.float32)
        peak = jnp.maximum(jnp.max(s0, axis=0, keepdims=True), jnp.max(s1, axis=0, keepdims=True))
        p0 = jnp.exp(s0 - peak)
        p1 = jnp.exp(s1 - peak)
        total = jnp.sum(p0, axis=0, keepdims=True) + jnp.sum(p1, axis=0, keepdims=True)
        vh = vt[64 * head:64 * head + 64, :]
        acc = jnp.dot(vh[:, :tokens], p0.astype(jnp.bfloat16), preferred_element_type=jnp.float32)
        acc = acc + jnp.dot(vh[:, tokens:], p1.astype(jnp.bfloat16), preferred_element_type=jnp.float32)
        outs.append(acc / total)
    o_ref[...] = jnp.concatenate(outs, axis=0).T.astype(o_ref.dtype)

def attend(query, keys, vals, other_keys, other_vals, block=512):
    tokens, width = query.shape
    kv = lambda p, b: (0, p)
    return pl.pallas_call(
        attend_kernel, grid=(width // 128, tokens // block),
        in_specs=[pl.BlockSpec((block, 128), lambda p, b: (b, p))] + [pl.BlockSpec((tokens, 128), kv)] * 4,
        out_specs=pl.BlockSpec((block, 128), lambda p, b: (b, p)),
        out_shape=jax.ShapeDtypeStruct((tokens, width), jnp.bfloat16),
        scratch_shapes=[pltpu.VMEM((128, 2 * tokens), jnp.bfloat16)],
        compiler_params=pltpu.CompilerParams(vmem_limit_bytes=60 * 1024 * 1024), name="attend",
    )(query, keys, other_keys, vals, other_vals)


def norm_rows(sums, scale, shift, count):
    channels = sums.shape[1]
    width = channels // GROUPS
    grouped = jnp.sum(sums.reshape(2, GROUPS, width), axis=-1)
    moments = (grouped + swap_cores(grouped)) / count
    mean = moments[0]
    inv_std = lax.rsqrt(moments[1] - mean * mean + NORM_EPS)
    return jnp.stack([jnp.repeat(mean, width), jnp.repeat(inv_std, width) * scale.astype(jnp.float32), shift.astype(jnp.float32)])


def channel_sums(half):
    wide = half.astype(jnp.float32)
    return jnp.stack([jnp.sum(wide, axis=(0, 1)), jnp.sum(wide * wide, axis=(0, 1))])


def edge_of(half, core):
    return swap_cores(jnp.where(core == 0, half[:, -1:], half[:, :1]))


def res_block(half, sums, time_vec, gn_scale, gn_shift, conv_w, norm_idx, conv_idx, core, last):
    count = 2 * half.shape[0] * half.shape[1] * (half.shape[2] // GROUPS)
    norm = norm_rows(sums, gn_scale[norm_idx], gn_shift[norm_idx], count)
    hidden, sums, edge = conv(half, edge_of(half, core), norm, conv_w, conv_idx, time_vec[None])
    norm = norm_rows(sums, gn_scale[norm_idx + 1], gn_shift[norm_idx + 1], count)
    return last(hidden, swap_cores(edge), norm, conv_w, conv_idx + 1, half)


def attention_block(half, sums, scale, shift, w_qkv, w_out):
    rows, cols, channels = half.shape
    norm = norm_rows(sums, scale, shift, 2 * rows * cols * (channels // GROUPS))
    normed = ((half.astype(jnp.float32) - norm[0]) * norm[1] + norm[2]).astype(jnp.bfloat16).reshape(rows * cols, channels)
    flat = w_qkv.reshape(3, channels, channels)

    def project(weight):
        return jnp.dot(normed, weight, preferred_element_type=jnp.float32).astype(jnp.bfloat16)

    keys, vals = project(flat[1]), project(flat[2])
    other_keys, other_vals = swap_cores(keys), swap_cores(vals)
    query = project(flat[0])
    attended = attend(query, keys, vals, other_keys, other_vals)
    out = jnp.dot(attended, w_out.reshape(channels, channels), preferred_element_type=jnp.float32)
    return (half.astype(jnp.float32) + out.reshape(half.shape)).astype(jnp.bfloat16)


def solution(mesh):
    lat_spec = P("dp", "sp", "sp2", None)

    def local(x, time_emb, gn_scale, gn_shift, conv_w, time_w, w_qkv, w_out):
        y, core = place(lax.axis_index(SP))
        image = y * 4 + lax.axis_index(SP2)
        time_act = jax.nn.silu(time_emb.astype(jnp.float32)).astype(jnp.bfloat16)
        time_vecs = jnp.einsum("bt,stc->sbc", time_act, time_w, preferred_element_type=jnp.float32)
        time_vecs = lax.dynamic_index_in_dim(time_vecs, image, 1, keepdims=False)
        half = to_images(x)
        first, sums, _ = res_block(half, channel_sums(half), time_vecs[0], gn_scale, gn_shift, conv_w, 0, 0, core, conv)
        middle = attention_block(first, sums, gn_scale[2], gn_shift[2], w_qkv, w_out)
        return res_block(middle, channel_sums(middle), time_vecs[1], gn_scale, gn_shift, conv_w, 3, 2, core, conv_out)

    return jax.shard_map(local, mesh=mesh, in_specs=(lat_spec, P("dp", None), P(), P(), P(), P(), P(), P()), out_specs=lat_spec, check_vma=False)
```

time: 413 us -> 381 us (0.923)
  Pallas kernels: 334 us -> 304 us
    pallas_call x5 -> x4, Pallas kernels: 219 us -> 189 us  [the longest x3 118 us: conv(): pl.pallas_call(functools.partial(conv_kernel, add.ndim == 3), grid=(chann...]
    unnamed x29 -> x31, local copies, waits for them, and re-layouts: 8.42 us -> 8.47 us
  transfers between devices with their start and end apart: 11 -> 11, of which waited for: 3 -> 4; matrix products, arithmetic and copies ran while one was open for 6% -> 6% of each run, Pallas kernels for 0% -> 0%
where the time goes in v2:
time: 381 us
  Pallas kernels  304 us (80%)
  matrix products  23.5 us (6%)
  local copies, waits for them, and re-layouts  20.5 us (5%)
  starting transfers between devices  19.6 us (5%)
  other arithmetic  9.43 us (2%)
    pallas_call x3, Pallas kernels, conv(): pl.pallas_call(functools.partial(conv_kernel, add.ndim == 3), grid=(chann...  118 us
    pallas_call x1, Pallas kernels, conv_out(): pl.pallas_call(conv_out_kernel, grid=(chunks,), in_specs=conv_specs(rows,...  71.6 us
    pallas_call x1, Pallas kernels, attend(): pl.pallas_call(attend_kernel, grid=(width // 128, tokens // block), in_sp...  69 us
    pallas_call x1, Pallas kernels, to_images(): pl.pallas_call(to_images_kernel, out_shape=jax.ShapeDtypeStruct((4 * rows...  45.8 us
    ppermute x11, starting transfers between devices, swap_cores(): return lax.ppermute(value, SP, [(0, 1), (1, 0), (2, 3), (3, 2)])  19.6 us
    dot_general x3, matrix products, project(): jnp.dot(normed, weight, preferred_element_type=jnp.float32)  12.5 us
    unnamed x31, local copies, waits for them, and re-layouts  8.47 us
  transfers between devices with their start and end apart: 11, of which 4 were waited for; matrix products, arithmetic and copies ran while one was open for 6% of the time, Pallas kernels for 0%

profile of v2, /device:TPU:31, one launch (start us, length us, event | category | flops | bytes accessed | tf_op | source)
XLA Modules:
  0.0 381.0 jit_solution(1655980856482583128)
XLA Ops:
  0.0 45.8 %to_images.1.h_ref.add_ref = bf16[16,64,1280]{2,1,0:T(8,128)(2,1)} custom-call(bf16[8,4,32,1280]{3,2,1,0:T(8,128)(2,1)} %x_ref.1), custom_call_target="tpu_custom_call" | custom-call | tf_op jit(solution)/shard_map/to_images/pallas_call | solution.py:79
  45.8 2.5 convert_reduce_fusion.1
  48.3 0.1 stack.38
  48.4 0.1 stack.39
  48.5 0.1 maximum_reduce_fusion
  48.6 17.2 %collective-permute-start.1 = (f32[2,32]{1,0:T(2,128)S(1)}, f32[2,32]{1,0:T(2,128)S(1)}, u32[]{:S(2)}, u32[]{:S(2)}) collective-permute-start(f32[2,32]{1,0:T(2,128)S(1)} %maximum_reduce_fusion), channel_id=1, source_target_pairs={{0,1},{1,0},{2,3},{3,2},{4,5},{5,4},{6,7},{7,6},{8,9},{9,8},{10,11... | collective-permute-start | bytes 776 | tf_op jit(solution)/shard_map/ppermute | solution.py:91
  65.8 1.2 broadcast_select_fusion.1
  67.0 0.1 collective-permute-start
  67.1 3.8 %fusion.11 = f32[8,2,1280]{2,0,1:T(8,128)S(1)} fusion(bf16[2,1280,1280]{2,1,0:T(8,128)(2,1)} %param.13, bf16[8,1280]{1,0:T(8,128)(2,1)S(1)} %copy-done.13), kind=kOutput, calls=%fused_computation.26 | convolution fusion | flops 52490240 | bytes 6656000 | tf_op jit(solution)/shard_map/bt,stc->sbc/dot_general | solution.py:365
  70.9 0.6 dynamic-slice_bitcast_fusion
  71.7 0.1 stack_reshape.12
  71.8 0.1 reshape.80
  72.0 0.6 pad_maximum_fusion.norm_ref
  72.6 0.6 copy-done.7
  73.2 39.1 %conv.3 = (bf16[16,64,1280]{2,1,0:T(8,128)(2,1)}, f32[2,1280]{1,0:T(2,128)}, bf16[16,1,1280]{2,1,0:T(2,128)(2,1)}) custom-call(bf16[16,64,1280]{2,1,0:T(8,128)(2,1)} %to_images.1.h_ref.add_ref, bf16[16,1,1280]{2,1,0:T(2,128)(2,1)} %copy-done.7, f32[3,1280]{1,0:T(4,128)} %pad_maximum_fusion.norm_ref, bf16[4,3,3,1280,1280]{4,3,2,1,0:T(8,128)(2,1)} %w_ref.7, ...), custom_call_target="tpu_custom_call" | custom-call | flops 30198988800 | bytes 29491200 | tf_op jit(solution)/shard_map/conv/pallas_call | solution.py:170
  112.3 0.8 reshape.81
  113.1 0.1 reduce_sum.84
  113.2 0.5 collective-permute-start.3
  113.7 6.9 %fusion.25 = (bf16[1,1280,20,64]{1,3,2,0:T(8,128)(2,1)}, bf16[1,1280,20,64]{1,3,2,0:T(8,128)(2,1)}, bf16[1,1280,20,64]{1,3,2,0:T(8,128)(2,1)}) fusion(bf16[3,1280,20,64]{1,3,2,0:T(8,128)(2,1)} %param.14), kind=kLoop, calls=%fused_computation.70 | loop fusion | bytes 19660800 | tf_op jit(solution)/shard_map/slice | solution.py:350
  120.8 0.1 stack_reshape.13
  120.9 0.1 reshape.82
  121.1 0.6 pad_maximum_fusion.1.norm_ref
  121.7 0.2 collective-permute-done.2.other_ref
  121.9 0.6 copy-done.8
  122.5 39.4 %conv.4 = (bf16[16,64,1280]{2,1,0:T(8,128)(2,1)}, f32[2,1280]{1,0:T(2,128)}, bf16[16,1,1280]{2,1,0:T(2,128)(2,1)}) custom-call(bf16[16,64,1280]{2,1,0:T(8,128)(2,1)} %get-tuple-element.13.h_ref, bf16[16,1,1280]{2,1,0:T(2,128)(2,1)} %copy-done.8, f32[3,1280]{1,0:T(4,128)} %pad_maximum_fusion.1.norm_ref, bf16[4,3,3,1280,1280]{4,3,2,1,0:T(8,128)(2,1)} %w_ref.7, ...), custom_call_target="tpu_custom_call" | custom-call | flops 30198988800 | bytes 29491200 | tf_op jit(solution)/shard_map/conv/pallas_call | solution.py:170
  161.9 0.9 reshape.83
  162.9 0.1 reduce_sum.85
  163.0 0.2 collective-permute-start.4
  163.2 0.9 collective-permute-done.4
  164.2 0.1 sub.32
  164.4 0.1 reshape.84
  164.5 2.5 fusion.3
  167.0 3.8 %convolution_convert_fusion.v0_ref = bf16[1024,1280]{1,0:T(8,128)(2,1)S(1)} fusion(bf16[1024,1280]{1,0:T(8,128)(2,1)S(1)} %bitcast.77, bf16[1280,1280]{0,1:T(8,128)(2,1)S(1)} %bitcast.76), kind=kOutput, calls=%fused_computation.12 | convolution fusion | flops 3356753920 | bytes 8519680 | tf_op jit(solution)/shard_map/dot_general | solution.py:348
  170.9 3.8 %convolution_convert_fusion.1.k0_ref = bf16[1024,1280]{1,0:T(8,128)(2,1)S(1)} fusion(bf16[1024,1280]{1,0:T(8,128)(2,1)S(1)} %bitcast.78, bf16[1280,1280]{0,1:T(8,128)(2,1)S(1)} %bitcast.75), kind=kOutput, calls=%fused_computation.13 | convolution fusion | flops 3356753920 | bytes 8519680 | tf_op jit(solution)/shard_map/dot_general | solution.py:348
  174.7 0.3 collective-permute-start.5
  175.0 0.3 collective-permute-start.6
  175.3 4.8 %convolution_convert_fusion.2.q_ref = bf16[1024,1280]{1,0:T(8,128)(2,1)} fusion(bf16[1024,1280]{1,0:T(8,128)(2,1)S(1)} %bitcast.79, bf16[1280,1280]{0,1:T(8,128)(2,1)S(1)} %bitcast.74), kind=kOutput, calls=%fused_computation.14 | convolution fusion | flops 3356753920 | bytes 8519680 | tf_op jit(solution)/shard_map/dot_general | solution.py:348
  180.2 1.5 copy-done.6
  181.7 1.8 collective-permute-done.6.v1_ref
  183.4 69.0 %attend.1 = bf16[1024,1280]{1,0:T(8,128)(2,1)} custom-call(bf16[1024,1280]{1,0:T(8,128)(2,1)} %convolution_convert_fusion.2.q_ref, bf16[1024,1280]{1,0:T(8,128)(2,1)} %copy-done.5, bf16[1024,1280]{1,0:T(8,128)(2,1)} %copy-done.6, bf16[1024,1280]{1,0:T(8,128)(2,1)} %copy-done.4, bf16[1024,1280]{1,0:T(8,128)(2,1)} %collective-permute-done.6.v1_ref), custom_call_target="tpu_custom_call" | custom-call | tf_op jit(solution)/shard_map/attend/pallas_call | solution.py:304
  252.4 7.2 %convert_reduce_fusion = (f32[1280]{0:T(1024)S(1)}, f32[1280]{0:T(1024)S(1)}, bf16[16,64,1280]{2,1,0:T(8,128)(2,1)S(1)}) fusion(bf16[16,64,1280]{2,1,0:T(8,128)(2,1)} %bitcast.80, bf16[1280,1280,1]{1,0,2:T(8,128)(2,1)} %bitcast.81, bf16[16,64,1280]{2,1,0:T(8,128)(2,1)} %get-tuple-element.16), kind=kOutput, calls=%fused_computation.1 | convolution fusion | flops 3364615680 | bytes 11151360 | tf_op jit(solution)/shard_map/dot_general | solution.py:354
  259.6 0.1 stack.43
  259.7 0.1 stack.44
  259.7 0.1 maximum_reduce_fusion.1
  259.8 0.2 collective-permute-start.8
  260.1 1.0 copy-done
  261.1 0.1 broadcast_select_fusion
  261.2 0.3 collective-permute-start.7
  261.6 0.1 stack_reshape.14
  261.8 0.1 reshape.87
  261.9 0.6 pad_maximum_fusion.2.norm_ref
  262.5 0.6 copy-done.9
  263.2 39.1 %conv.5 = (bf16[16,64,1280]{2,1,0:T(8,128)(2,1)}, f32[2,1280]{1,0:T(2,128)}, bf16[16,1,1280]{2,1,0:T(2,128)(2,1)}) custom-call(bf16[16,64,1280]{2,1,0:T(8,128)(2,1)} %copy-done, bf16[16,1,1280]{2,1,0:T(2,128)(2,1)} %copy-done.9, f32[3,1280]{1,0:T(4,128)} %pad_maximum_fusion.2.norm_ref, bf16[4,3,3,1280,1280]{4,3,2,1,0:T(8,128)(2,1)} %w_ref.7, ...), custom_call_target="tpu_custom_call" | custom-call | flops 30198988800 | bytes 29491200 | tf_op jit(solution)/shard_map/conv/pallas_call | solution.py:170
  302.3 0.8 reshape.88
  303.1 0.1 reduce_sum.89
  303.2 0.2 collective-permute-start.10
  303.4 0.3 collective-permute-start.9
  303.7 0.7 collective-permute-done.10
  304.4 0.1 stack_reshape.15
  304.6 0.1 reshape.89
  304.7 0.6 pad_maximum_fusion.3.norm_ref
  305.4 0.6 copy-done.10
  306.0 71.6 %conv_out.1 = bf16[8,4,32,1280]{3,2,1,0:T(8,128)(2,1)} custom-call(bf16[16,64,1280]{2,1,0:T(8,128)(2,1)} %get-tuple-element.18.h_ref, bf16[16,1,1280]{2,1,0:T(2,128)(2,1)} %copy-done.10, f32[3,1280]{1,0:T(4,128)} %pad_maximum_fusion.3.norm_ref, bf16[4,3,3,1280,1280]{4,3,2,1,0:T(8,128)(2,1)} %w_ref.7, bf16[16,64,1280]{2,1,0:T(8,128)(2,1)} %copy-done), custom_call_target="tpu_custom_call" | custom-call | flops 30198988800 | bytes 29491200 | tf_op jit(solution)/shard_map/conv_out/pallas_call | solution.py:261
  377.6 3.4 copy.10
  (64 shorter events, 1.1 us)
Async XLA Ops:
  0.0 67.1 %copy-start.11 = (bf16[5,1280]{1,0:T(8,128)(2,1)S(1)}, bf16[5,1280]{1,0:T(8,128)(2,1)}, u32[]{:S(2)}) copy-start(bf16[5,1280]{1,0:T(8,128)(2,1)} %param.11) | copy-start | bytes 38404
  0.0 67.1 %copy-start.13 = (bf16[8,1280]{1,0:T(8,128)(2,1)S(1)}, bf16[8,1280]{1,0:T(8,128)(2,1)}, u32[]{:S(2)}) copy-start(bf16[8,1280]{1,0:T(8,128)(2,1)} %param.9) | copy-start | bytes 61444
  48.6 23.0 %collective-permute-start.1 = (f32[2,32]{1,0:T(2,128)S(1)}, f32[2,32]{1,0:T(2,128)S(1)}, u32[]{:S(2)}, u32[]{:S(2)}) collective-permute-start(f32[2,32]{1,0:T(2,128)S(1)} %maximum_reduce_fusion), channel_id=1, source_target_pairs={{0,1},{1,0},{2,3},{3,2},{4,5},{5,4},{6,7},{7,6},{8,9},{9,8},{10,11... | collective-permute-start | bytes 776 | tf_op jit(solution)/shard_map/ppermute | solution.py:91
  67.0 5.6 %collective-permute-start = (bf16[16,1,1280]{2,1,0:T(2,128)(2,1)S(1)}, bf16[16,1,1280]{2,1,0:T(2,128)(2,1)S(1)}, u32[]{:S(2)}, u32[]{:S(2)}) collective-permute-start(bf16[16,1,1280]{2,1,0:T(2,128)(2,1)S(1)} %broadcast_select_fusion.1), channel_id=1, source_target_pairs={{0,1},{1,0},{2,3},{3,2},{4,5},{5,4},{6,7},{7,6},{8,9},{9,8},{10,11... | collective-permute-start | bytes 122888 | tf_op jit(solution)/shard_map/ppermute | solution.py:91
  67.1 4.8 %copy-start.12 = (bf16[5,1280]{1,0:T(8,128)(2,1)S(1)}, bf16[5,1280]{1,0:T(8,128)(2,1)}, u32[]{:S(2)}) copy-start(bf16[5,1280]{1,0:T(8,128)(2,1)} %param.10) | copy-start | bytes 38404
  72.6 0.6 copy-start.7
  113.2 7.4 %copy-start.14 = (bf16[16,1,1280]{2,1,0:T(2,128)(2,1)S(1)}, bf16[16,1,1280]{2,1,0:T(2,128)(2,1)}, u32[]{:S(2)}) copy-start(bf16[16,1,1280]{2,1,0:T(2,128)(2,1)} %get-tuple-element.14) | copy-start | bytes 122884
  113.2 7.5 %collective-permute-start.3 = (f32[2,32]{1,0:T(2,128)S(1)}, f32[2,32]{1,0:T(2,128)S(1)}, u32[]{:S(2)}, u32[]{:S(2)}) collective-permute-start(f32[2,32]{1,0:T(2,128)S(1)} %reduce_sum.84), channel_id=1, source_target_pairs={{0,1},{1,0},{2,3},{3,2},{4,5},{5,4},{6,7},{7,6},{8,9},{9,8},{10,11... | collective-permute-start | bytes 776 | tf_op jit(solution)/shard_map/ppermute | solution.py:91
  120.6 1.3 collective-permute-start.2
  121.9 0.6 copy-start.8
  161.9 5.1 %copy-start.3 = (bf16[1,1280,20,64]{1,3,2,0:T(8,128)(2,1)S(1)}, bf16[1,1280,20,64]{1,3,2,0:T(8,128)(2,1)}, u32[]{:S(2)}) copy-start(bf16[1,1280,20,64]{1,3,2,0:T(8,128)(2,1)} %get-tuple-element.25) | copy-start | bytes 9830404
  163.0 1.2 collective-permute-start.4
  167.0 3.9 %copy-start.2 = (bf16[1,1280,20,64]{1,3,2,0:T(8,128)(2,1)S(1)}, bf16[1,1280,20,64]{1,3,2,0:T(8,128)(2,1)}, u32[]{:S(2)}) copy-start(bf16[1,1280,20,64]{1,3,2,0:T(8,128)(2,1)} %get-tuple-element.27) | copy-start | bytes 9830404
  170.9 4.2 %copy-start.4 = (bf16[1024,1280]{1,0:T(8,128)(2,1)}, bf16[1024,1280]{1,0:T(8,128)(2,1)S(1)}, u32[]{:S(2)}) copy-start(bf16[1024,1280]{1,0:T(8,128)(2,1)S(1)} %convolution_convert_fusion.v0_ref) | copy-start | bytes 7864324
  170.9 4.4 %copy-start.1 = (bf16[1,1280,20,64]{1,3,2,0:T(8,128)(2,1)S(1)}, bf16[1,1280,20,64]{1,3,2,0:T(8,128)(2,1)}, u32[]{:S(2)}) copy-start(bf16[1,1280,20,64]{1,3,2,0:T(8,128)(2,1)} %get-tuple-element.26) | copy-start | bytes 9830404
  174.7 5.4 %copy-start.5 = (bf16[1024,1280]{1,0:T(8,128)(2,1)}, bf16[1024,1280]{1,0:T(8,128)(2,1)S(1)}, u32[]{:S(2)}) copy-start(bf16[1024,1280]{1,0:T(8,128)(2,1)S(1)} %convolution_convert_fusion.1.k0_ref) | copy-start | bytes 7864324
  174.7 5.4 %collective-permute-start.5 = (bf16[1024,1280]{1,0:T(8,128)(2,1)S(1)}, bf16[1024,1280]{1,0:T(8,128)(2,1)S(1)}, u32[]{:S(2)}, u32[]{:S(2)}) collective-permute-start(bf16[1024,1280]{1,0:T(8,128)(2,1)S(1)} %convolution_convert_fusion.1.k0_ref), channel_id=1, source_target_pairs={{0,1},{1,0},{2,3},{3,2},{4,5},{5,4},{6,7},{7,6},{8,9},{9,8},{10,11... | collective-permute-start | bytes 7864328 | tf_op jit(solution)/shard_map/ppermute | solution.py:91
  175.0 8.4 %collective-permute-start.6 = (bf16[1024,1280]{1,0:T(8,128)(2,1)S(1)}, bf16[1024,1280]{1,0:T(8,128)(2,1)}, u32[]{:S(2)}, u32[]{:S(2)}) collective-permute-start(bf16[1024,1280]{1,0:T(8,128)(2,1)S(1)} %convolution_convert_fusion.v0_ref), channel_id=1, source_target_pairs={{0,1},{1,0},{2,3},{3,2},{4,5},{5,4},{6,7},{7,6},{8,9},{9,8},{10,11... | collective-permute-start | bytes 7864328 | tf_op jit(solution)/shard_map/ppermute | solution.py:91
  180.2 1.5 copy-start.6
  259.6 1.5 copy-start
  259.8 1.7 collective-permute-start.8
  261.2 1.3 collective-permute-start.7
  262.5 0.6 copy-start.9
  303.2 1.2 collective-permute-start.10
  303.4 2.0 collective-permute-start.9
  305.4 0.6 copy-start.10

commit v3 on v2

--- a/solution.py
+++ b/solution.py
@@ -17,78 +17,25 @@
     return sp // cores, lax.rem(sp, cores)
 
 
-def to_images_kernel(x_ref, out_ref, stage, send_sem, recv_sem, self_sem):
-    images, rows, cols, _ = x_ref.shape
-    sp, z = lax.axis_index(SP), lax.axis_index(SP2)
-    y, core = place(sp)
-    mine = y * 4 + z
-    to_core = z // 2
-    own = to_core == core
-    barrier = pltpu.get_barrier_semaphore()
-    for s in range(8):
-        src_sp, src_z = s // 2, 2 * core + s % 2
-
-        @pl.when(jnp.logical_not((src_sp == sp) & (src_z == z)))
-        def _():
-            pl.semaphore_signal(barrier, inc=1, device_id={SP: src_sp, SP2: src_z}, device_id_type=MESH)
-
-    pl.semaphore_wait(barrier, 8 - own.astype(jnp.int32))
-
-    def piece(src_sp, src_z):
-        return out_ref.at[pl.ds(src_sp * rows, rows), pl.ds(lax.rem(src_z, 2) * cols, cols), :]
-
-    def send(i):
-        return pltpu.make_async_remote_copy(
-            src_ref=x_ref.at[i], dst_ref=piece(sp, z), send_sem=send_sem.at[i], recv_sem=recv_sem.at[sp * 2 + lax.rem(z, 2)],
-            device_id={SP: (i // 4) * 2 + to_core, SP2: i % 4}, device_id_type=MESH)
-
-    def is_self(i):
-        return own & (mine == i)
-
-    for i in range(images):
-        @pl.when(jnp.logical_not(is_self(i)))
-        def _():
-            send(i).start()
-
-    @pl.when(own)
-    def _():
-        load = pltpu.make_async_copy(x_ref.at[mine], stage, self_sem)
-        load.start()
-        load.wait()
-        store = pltpu.make_async_copy(stage, piece(sp, z), self_sem)
-        store.start()
-        store.wait()
-
-    for s in range(8):
-        src_sp, src_z = s // 2, 2 * core + s % 2
-
-        @pl.when(jnp.logical_not((src_sp == sp) & (src_z == z)))
-        def _():
-            pltpu.make_async_remote_copy(
-                src_ref=x_ref.at[0], dst_ref=piece(src_sp, src_z), send_sem=send_sem.at[0], recv_sem=recv_sem.at[s],
-                device_id={SP: src_sp, SP2: src_z}, device_id_type=MESH).wait_recv()
-
-    for i in range(images):
-        @pl.when(jnp.logical_not(is_self(i)))
-        def _():
-            send(i).wait_send()
-
-
-def to_images(x):
-    images, rows, cols, channels = x.shape
-    return pl.pallas_call(
-        to_images_kernel,
-        out_shape=jax.ShapeDtypeStruct((4 * rows, 2 * cols, channels), x.dtype),
-        in_specs=[pl.BlockSpec(memory_space=pl.ANY)],
-        out_specs=pl.BlockSpec(memory_space=pl.ANY),
-        scratch_shapes=[pltpu.VMEM((rows, cols, channels), x.dtype), pltpu.SemaphoreType.DMA((8,)), pltpu.SemaphoreType.DMA((8,)), pltpu.SemaphoreType.DMA],
-        compiler_params=pltpu.CompilerParams(collective_id=0, has_side_effects=True),
-        name="to_images",
-    )(x)
-
-
 def swap_cores(value):
     return lax.ppermute(value, SP, [(0, 1), (1, 0), (2, 3), (3, 2)])
+
+
+def group_rows(sums, scale, shift, count):
+    channels = sums.shape[1]
+    width = channels // GROUPS
+
+    def member(shape, channel_dim):
+        channel = lax.broadcasted_iota(jnp.int32, shape, channel_dim).astype(jnp.float32)
+        group = lax.broadcasted_iota(jnp.int32, shape, 1 - channel_dim).astype(jnp.float32)
+        return (jnp.floor((channel + 0.5) / width) == group).astype(jnp.float32)
+
+    exact = lax.Precision.HIGHEST
+    moments = jnp.dot(sums, member((channels, 128), 0), precision=exact, preferred_element_type=jnp.float32) / count
+    mean = moments[0:1]
+    inv_std = lax.rsqrt(moments[1:2] - mean * mean + NORM_EPS)
+    spread = jnp.dot(jnp.concatenate([mean, inv_std], axis=0), member((128, channels), 1), precision=exact, preferred_element_type=jnp.float32)
+    return jnp.concatenate([spread[0:1], spread[1:2] * scale.astype(jnp.float32), shift.astype(jnp.float32)], axis=0)
 
 
 def silu(v):
@@ -130,13 +77,15 @@
     return total
 
 
-def conv_kernel(residual, h_ref, other_ref, norm_ref, w_ref, add_ref, out_ref, sums_ref, edge_ref, act):
+def conv_kernel(residual, norm_idx, h_ref, other_ref, own_ref, theirs_ref, scale_ref, shift_ref, w_ref, add_ref, out_ref, sums_ref, edge_ref, act, norm_ref):
     rows, cols, channels = h_ref.shape
     width = w_ref.shape[-1]
     _, core = place(lax.axis_index(SP))
 
     @pl.when(pl.program_id(0) == 0)
     def _():
+        count = 2 * rows * cols * (channels // GROUPS)
+        norm_ref[...] = group_rows(own_ref[...] + theirs_ref[...], scale_ref[norm_idx:norm_idx + 1, :], shift_ref[norm_idx:norm_idx + 1, :], count)
         fill_act(core, h_ref, other_ref, norm_ref, act)
 
     full = taps(act, w_ref, rows, cols, channels)
@@ -158,29 +107,243 @@
 def conv_specs(rows, cols, channels, j, nb, residual):
     whole = lambda *s: pl.BlockSpec(s, lambda n: (0,) * len(s))
     add = pl.BlockSpec((rows, cols, nb), lambda n: (0, 0, n)) if residual else pl.BlockSpec((1, nb), lambda n: (0, n))
-    return [whole(rows, cols, channels), whole(rows, 1, channels), whole(3, channels), pl.BlockSpec((None, 3, 3, channels, nb), lambda n: (j, 0, 0, 0, n)), add]
+    return [whole(rows, cols, channels), whole(rows, 1, channels), whole(2, channels), whole(2, channels), whole(5, channels), whole(5, channels), pl.BlockSpec((None, 3, 3, channels, nb), lambda n: (j, 0, 0, 0, n)), add]
 
 
 def conv_cost(rows, cols, channels):
     return pl.CostEstimate(flops=18 * rows * cols * channels * channels, bytes_accessed=18 * channels * channels, transcendentals=rows * cols * channels)
 
 
-def conv(h, other, norm, w, j, add, nb=256):
+def conv(h, other, own, theirs, scale, shift, norm_idx, w, j, add, nb=256):
     rows, cols, channels = h.shape
     return pl.pallas_call(
-        functools.partial(conv_kernel, add.ndim == 3),
+        functools.partial(conv_kernel, add.ndim == 3, norm_idx),
         grid=(channels // nb,),
         in_specs=conv_specs(rows, cols, channels, j, nb, add.ndim == 3),
         out_specs=[pl.BlockSpec((rows, cols, nb), lambda n: (0, 0, n)), pl.BlockSpec((2, nb), lambda n: (0, n)), pl.BlockSpec((rows, 1, nb), lambda n: (0, 0, n))],
         out_shape=[jax.ShapeDtypeStruct((rows, cols, channels), jnp.bfloat16), jax.ShapeDtypeStruct((2, channels), jnp.float32), jax.ShapeDtypeStruct((rows, 1, channels), jnp.bfloat16)],
-        scratch_shapes=[pltpu.VMEM((3, rows + 2, cols, channels), jnp.bfloat16)],
+        scratch_shapes=[pltpu.VMEM((3, rows + 2, cols, channels), jnp.bfloat16), pltpu.VMEM((3, channels), jnp.float32)],
         compiler_params=pltpu.CompilerParams(vmem_limit_bytes=62 * 1024 * 1024),
         cost_estimate=conv_cost(rows, cols, channels),
         name="conv",
-    )(h, other, norm, w, add)
-
-
-def conv_out_kernel(h_ref, other_ref, norm_ref, w_ref, add_ref, out_ref, act, done, send_sem, recv_sem, self_sem):
+    )(h, other, own, theirs, scale, shift, w, add)
+
+
+def conv_in_kernel(x_ref, scale_ref, shift_ref, add_ref, w_ref, out_ref, half_ref, sums_ref, edge_ref,
+                   tile, raw, beside, weights, act, acc, stats, heard, norm_ref,
+                   tile_sem, w_sem, send_sem, recv_sem, self_sem, tell_sem, hear_sem, lend_sem, borrow_sem, keep_sem):
+    images, trows, tcols, channels = x_ref.shape
+    chunks, rows, cols, width = raw.shape
+    sp, z = lax.axis_index(SP), lax.axis_index(SP2)
+    y, core = place(sp)
+    mine = y * 4 + z
+    to_core = z // 2
+    own = to_core == core
+    me = sp * 4 + z
+    load = pltpu.make_async_copy(x_ref, tile, tile_sem)
+    load.start()
+    barrier = pltpu.get_barrier_semaphore()
+    for d in range(16):
+        @pl.when(me != d)
+        def _():
+            pl.semaphore_signal(barrier, inc=1, device_id={SP: d // 4, SP2: d % 4}, device_id_type=MESH)
+
+    def weight(c):
+        return pltpu.make_async_copy(w_ref.at[0, :, :, pl.ds(pl.multiple_of(c * width, width), width), :], weights.at[c], w_sem.at[c])
+
+    def lanes(c):
+        return pl.ds(pl.multiple_of(c * width, width), width)
+
+    def piece(c, src_sp, src_z):
+        return raw.at[c, pl.ds(src_sp * trows, trows), pl.ds(pl.multiple_of(lax.rem(src_z, 2) * tcols, tcols), tcols), :]
+
+    def send(c, i):
+        return pltpu.make_async_remote_copy(
+            src_ref=x_ref.at[i, :, :, lanes(c)], dst_ref=piece(c, sp, z), send_sem=send_sem.at[c, i], recv_sem=recv_sem.at[c, sp * 2 + lax.rem(z, 2)],
+            device_id={SP: (i // 4) * 2 + to_core, SP2: i % 4}, device_id_type=MESH)
+
+    def place_own(c):
+        return pltpu.make_async_copy(x_ref.at[mine, :, :, lanes(c)], piece(c, sp, z), self_sem.at[c])
+
+    def is_self(i):
+        return own & (mine == i)
+
+    def start_chunk(c):
+        for i in range(images):
+            @pl.when(jnp.logical_not(is_self(i)))
+            def _():
+                send(c, i).start()
+
+        @pl.when(own)
+        def _():
+            place_own(c).start()
+
+    def tell(i, k):
+        return pltpu.make_async_remote_copy(
+            src_ref=stats.at[i], dst_ref=heard.at[me], send_sem=tell_sem.at[i, k], recv_sem=hear_sem.at[me],
+            device_id={SP: (i // 4) * 2 + k, SP2: i % 4}, device_id_type=MESH)
+
+    pl.semaphore_wait(barrier, 15)
+    start_chunk(0)
+    for c in range(chunks):
+        weight(c).start()
+    load.wait()
+
+    def sum_image(i, carry):
+        wide = tile[i].reshape(trows * tcols, channels).astype(jnp.float32)
+        stats[i] = jnp.concatenate([jnp.sum(wide, axis=0, keepdims=True), jnp.sum(wide * wide, axis=0, keepdims=True)], axis=0)
+        return carry
+
+    lax.fori_loop(0, images, sum_image, 0)
+    for i in range(images):
+        for k in range(2):
+            @pl.when(jnp.logical_not((mine == i) & (core == k)))
+            def _():
+                tell(i, k).start()
+
+    def start_rest(c, carry):
+        start_chunk(c)
+        return carry
+
+    lax.fori_loop(1, chunks, start_rest, 0)
+    total = stats[mine]
+    for d in range(16):
+        @pl.when(me != d)
+        def _():
+            pltpu.make_async_remote_copy(
+                src_ref=stats.at[0], dst_ref=heard.at[d], send_sem=tell_sem.at[0, 0], recv_sem=hear_sem.at[d],
+                device_id={SP: d // 4, SP2: d % 4}, device_id_type=MESH).wait_recv()
+
+        total = total + jnp.where(me != d, heard[d], 0.0)
+    count = 2 * rows * cols * (channels // GROUPS)
+    norm_ref[...] = group_rows(total, scale_ref[0:1, :], shift_ref[0:1, :], count)
+    zeros = jnp.zeros((cols, width), jnp.bfloat16)
+    for dx in range(3):
+        act[dx, 0] = zeros
+        act[dx, rows + 1] = zeros
+    line = lax.broadcasted_iota(jnp.int32, (cols, width), 0)
+    band = beside.shape[2]
+
+    def lend(c):
+        first = pl.multiple_of((1 - core) * (cols - band), band)
+        return pltpu.make_async_remote_copy(
+            src_ref=raw.at[c, :, pl.ds(first, band), :], dst_ref=beside.at[c], send_sem=lend_sem.at[c], recv_sem=borrow_sem.at[c],
+            device_id={SP: y * 2 + 1 - core}, device_id_type=MESH)
+
+    def keep_raw(c):
+        return pltpu.make_async_copy(raw.at[c], half_ref.at[:, :, lanes(c)], keep_sem.at[c])
+
+    def one_chunk(c, carry):
+        for s in range(8):
+            src_sp, src_z = s // 2, 2 * core + s % 2
+
+            @pl.when(jnp.logical_not((src_sp == sp) & (src_z == z)))
+            def _():
+                pltpu.make_async_remote_copy(
+                    src_ref=x_ref.at[0, :, :, lanes(c)], dst_ref=piece(c, src_sp, src_z), send_sem=send_sem.at[c, 0], recv_sem=recv_sem.at[c, s],
+                    device_id={SP: src_sp, SP2: src_z}, device_id_type=MESH).wait_recv()
+
+        @pl.when(own)
+        def _():
+            place_own(c).wait()
+
+        lend(c).start()
+        keep_raw(c).start()
+        mean, mult, shift = norm_ref[0:1, lanes(c)], norm_ref[1:2, lanes(c)], norm_ref[2:3, lanes(c)]
+
+        def activate(v):
+            return silu((v.astype(jnp.float32) - mean) * mult + shift)
+
+        lend(c).wait_recv()
+
+        def one_row(r, carry2):
+            u = activate(raw[c, r])
+            left = jnp.where(core == 1, activate(beside[c, r, band - 1:band, :]), 0.0)
+            right = jnp.where(core == 0, activate(beside[c, r, 0:1, :]), 0.0)
+            act[1, r + 1] = u.astype(jnp.bfloat16)
+            act[0, r + 1] = jnp.where(line == 0, left, pltpu.roll(u, 1, 0)).astype(jnp.bfloat16)
+            act[2, r + 1] = jnp.where(line == cols - 1, right, pltpu.roll(u, cols - 1, 0)).astype(jnp.bfloat16)
+            return carry2
+
+        lax.fori_loop(0, rows, one_row, 0)
+        weight(c).wait()
+
+        def one_block(n, carry2):
+            part = None
+            for k in range(9):
+                lhs = act[k % 3, pl.ds(k // 3, rows)].reshape(rows * cols, width)
+                dot = jnp.dot(lhs, weights[c, k // 3, k % 3, :, lanes(n)], preferred_element_type=jnp.float32)
+                part = dot if part is None else part + dot
+
+            @pl.when(c == 0)
+            def _():
+                acc[n] = part
+
+            @pl.when(c > 0)
+            def _():
+                acc[n] += part
+            return carry2
+
+        lax.fori_loop(0, chunks, one_block, 0)
+        return carry
+
+    lax.fori_loop(0, chunks, one_chunk, 0)
+    for n in range(chunks):
+        cut = slice(n * width, (n + 1) * width)
+        half = (acc[n] + add_ref[:, cut]).astype(jnp.bfloat16)
+        out_ref[:, :, cut] = half.reshape(rows, cols, width)
+        kept = half.astype(jnp.float32)
+        sums_ref[:, cut] = jnp.concatenate([jnp.sum(kept, axis=0, keepdims=True), jnp.sum(kept * kept, axis=0, keepdims=True)], axis=0)
+
+    @pl.when(core == 0)
+    def _():
+        edge_ref[...] = out_ref[:, cols - 1:, :]
+
+    @pl.when(core == 1)
+    def _():
+        edge_ref[...] = out_ref[:, :1, :]
+
+    def drain(c, carry):
+        for i in range(images):
+            @pl.when(jnp.logical_not(is_self(i)))
+            def _():
+                send(c, i).wait_send()
+
+        lend(c).wait_send()
+        keep_raw(c).wait()
+        return carry
+
+    lax.fori_loop(0, chunks, drain, 0)
+    for i in range(images):
+        for k in range(2):
+            @pl.when(jnp.logical_not((mine == i) & (core == k)))
+            def _():
+                tell(i, k).wait_send()
+
+
+def conv_in(x, scale, shift, add, w, width=256, band=16):
+    images, trows, tcols, channels = x.shape
+    rows, cols, chunks = 4 * trows, 2 * tcols, channels // width
+    vmem, hbm = pl.BlockSpec(memory_space=pltpu.VMEM), pl.BlockSpec(memory_space=pl.ANY)
+    dma = pltpu.SemaphoreType.DMA
+    shape = jax.ShapeDtypeStruct
+    return pl.pallas_call(
+        conv_in_kernel,
+        in_specs=[hbm, vmem, vmem, vmem, hbm],
+        out_specs=[vmem, hbm, vmem, vmem],
+        out_shape=[shape((rows, cols, channels), jnp.bfloat16), shape((rows, cols, channels), jnp.bfloat16), shape((2, channels), jnp.float32), shape((rows, 1, channels), jnp.bfloat16)],
+        scratch_shapes=[
+            pltpu.VMEM(x.shape, jnp.bfloat16), pltpu.VMEM((chunks, rows, cols, width), jnp.bfloat16), pltpu.VMEM((chunks, rows, band, width), jnp.bfloat16),
+            pltpu.VMEM((chunks, 3, 3, width, channels), jnp.bfloat16), pltpu.VMEM((3, rows + 2, cols, width), jnp.bfloat16), pltpu.VMEM((chunks, rows * cols, width), jnp.float32),
+            pltpu.VMEM((images, 2, channels), jnp.float32), pltpu.VMEM((16, 2, channels), jnp.float32), pltpu.VMEM((3, channels), jnp.float32),
+            dma, dma((chunks,)), dma((chunks, 8)), dma((chunks, 8)), dma((chunks,)), dma((8, 2)), dma((16,)), dma((chunks,)), dma((chunks,)), dma((chunks,))],
+        compiler_params=pltpu.CompilerParams(collective_id=0, has_side_effects=True, vmem_limit_bytes=63 * 1024 * 1024),
+        cost_estimate=conv_cost(rows, cols, channels),
+        name="conv_in",
+    )(x, scale, shift, add, w)
+
+
+def conv_out_kernel(norm_idx, h_ref, other_ref, own_ref, theirs_ref, scale_ref, shift_ref, w_ref, add_ref, out_ref, act, norm_ref, done, send_sem, recv_sem, self_sem):
     rows, cols, channels = h_ref.shape
     images, trows, tcols, _ = out_ref.shape
     width = w_ref.shape[-1]
@@ -199,6 +362,8 @@
             def _():
                 pl.semaphore_signal(barrier, inc=1, device_id={SP: (i // 4) * 2 + from_core, SP2: i % 4}, device_id_type=MESH)
 
+        count = 2 * rows * cols * (channels // GROUPS)
+        norm_ref[...] = group_rows(own_ref[...] + theirs_ref[...], scale_ref[norm_idx:norm_idx + 1, :], shift_ref[norm_idx:norm_idx + 1, :], count)
         fill_act(core, h_ref, other_ref, norm_ref, act)
         pl.semaphore_wait(barrier, 8 - own.astype(jnp.int32))
 
@@ -255,21 +420,21 @@
         lax.fori_loop(0, channels // width, drain, 0)
 
 
-def conv_out(h, other, norm, w, j, add, nb=256):
+def conv_out(h, other, own, theirs, scale, shift, norm_idx, w, j, add, nb=256):
     rows, cols, channels = h.shape
     chunks = channels // nb
     return pl.pallas_call(
-        conv_out_kernel,
+        functools.partial(conv_out_kernel, norm_idx),
         grid=(chunks,),
         in_specs=conv_specs(rows, cols, channels, j, nb, True),
         out_specs=pl.BlockSpec(memory_space=pl.ANY),
         out_shape=jax.ShapeDtypeStruct((8, rows // 4, cols // 2, channels), jnp.bfloat16),
-        scratch_shapes=[pltpu.VMEM((3, rows + 2, cols, channels), jnp.bfloat16), pltpu.VMEM((chunks, rows, cols, nb), jnp.bfloat16),
+        scratch_shapes=[pltpu.VMEM((3, rows + 2, cols, channels), jnp.bfloat16), pltpu.VMEM((3, channels), jnp.float32), pltpu.VMEM((chunks, rows, cols, nb), jnp.bfloat16),
                         pltpu.SemaphoreType.DMA((chunks, 8)), pltpu.SemaphoreType.DMA((chunks, 8)), pltpu.SemaphoreType.DMA((chunks,))],
         compiler_params=pltpu.CompilerParams(collective_id=1, has_side_effects=True, vmem_limit_bytes=62 * 1024 * 1024),
         cost_estimate=conv_cost(rows, cols, channels),
         name="conv_out",
-    )(h, other, norm, w, add)
+    )(h, other, own, theirs, scale, shift, w, add)
 
 
 NT = (((1,), (1,)), ((), ()))
@@ -327,15 +492,7 @@
 
 
 def edge_of(half, core):
-    return swap_cores(jnp.where(core == 0, half[:, -1:], half[:, :1]))
-
-
-def res_block(half, sums, time_vec, gn_scale, gn_shift, conv_w, norm_idx, conv_idx, core, last):
-    count = 2 * half.shape[0] * half.shape[1] * (half.shape[2] // GROUPS)
-    norm = norm_rows(sums, gn_scale[norm_idx], gn_shift[norm_idx], count)
-    hidden, sums, edge = conv(half, edge_of(half, core), norm, conv_w, conv_idx, time_vec[None])
-    norm = norm_rows(sums, gn_scale[norm_idx + 1], gn_shift[norm_idx + 1], count)
-    return last(hidden, swap_cores(edge), norm, conv_w, conv_idx + 1, half)
+    return jnp.where(core == 0, half[:, -1:], half[:, :1])
 
 
 def attention_block(half, sums, scale, shift, w_qkv, w_out):
@@ -364,9 +521,12 @@
         time_act = jax.nn.silu(time_emb.astype(jnp.float32)).astype(jnp.bfloat16)
         time_vecs = jnp.einsum("bt,stc->sbc", time_act, time_w, preferred_element_type=jnp.float32)
         time_vecs = lax.dynamic_index_in_dim(time_vecs, image, 1, keepdims=False)
-        half = to_images(x)
-        first, sums, _ = res_block(half, channel_sums(half), time_vecs[0], gn_scale, gn_shift, conv_w, 0, 0, core, conv)
+        norms = gn_scale, gn_shift
+        hidden, half, sums, edge = conv_in(x, gn_scale, gn_shift, time_vecs[0][None], conv_w)
+        first, sums, _ = conv(hidden, swap_cores(edge), sums, swap_cores(sums), *norms, 1, conv_w, 1, half)
         middle = attention_block(first, sums, gn_scale[2], gn_shift[2], w_qkv, w_out)
-        return res_block(middle, channel_sums(middle), time_vecs[1], gn_scale, gn_shift, conv_w, 3, 2, core, conv_out)
+        sums, edge = channel_sums(middle), edge_of(middle, core)
+        hidden, sums, edge = conv(middle, swap_cores(edge), sums, swap_cores(sums), *norms, 3, conv_w, 2, time_vecs[1][None])
+        return conv_out(hidden, swap_cores(edge), sums, swap_cores(sums), *norms, 4, conv_w, 3, middle)
 
     return jax.shard_map(local, mesh=mesh, in_specs=(lat_spec, P("dp", None), P(), P(), P(), P(), P(), P()), out_specs=lat_spec, check_vma=False)

time: 381 us -> 364 us (0.955)
  starting transfers between devices: 19.6 us -> 2.35 us
  Pallas kernels: 304 us -> 310 us
  other arithmetic: 9.43 us -> 4.26 us
  local copies, waits for them, and re-layouts: 20.5 us -> 15.7 us
    ppermute x11 -> x9, starting transfers between devices: 19.6 us -> 2.35 us  [swap_cores(): return lax.ppermute(value, SP, [(0, 1), (1, 0), (2, 3), (3, 2)])]
    pallas_call x5 -> x4, Pallas kernels: 235 us -> 241 us  [the longest x1 87.6 us: conv_in(): pl.pallas_call(conv_in_kernel, in_specs=[hbm, vmem, vmem, vmem, hbm], out...]
    dot_general x3, matrix products: 12.5 us -> 16.7 us  [project(): jnp.dot(normed, weight, preferred_element_type=jnp.float32)]
    unnamed x31 -> x27, local copies, waits for them, and re-layouts: 8.47 us -> 6.81 us
  transfers between devices with their start and end apart: 11 -> 9, of which waited for: 4 -> 4; matrix products, arithmetic and copies ran while one was open for 6% -> 4% of each run, Pallas kernels for 0% -> 0%
where the time goes in v3:
time: 364 us; the launch traced here: 363 us
  Pallas kernels  310 us (85%)
  matrix products  26.9 us (7%)
  local copies, waits for them, and re-layouts  15.7 us (4%)
  other arithmetic  4.26 us (1%)
    pallas_call x1, Pallas kernels, conv_in(): pl.pallas_call(conv_in_kernel, in_specs=[hbm, vmem, vmem, vmem, hbm], out...  87.6 us
    pallas_call x2, Pallas kernels, conv(): pl.pallas_call(functools.partial(conv_kernel, add.ndim == 3, norm_idx), g...  80.2 us
    pallas_call x1, Pallas kernels, conv_out(): pl.pallas_call(functools.partial(conv_out_kernel, norm_idx), grid=(chunks...  73.7 us
    pallas_call x1, Pallas kernels, attend(): pl.pallas_call(attend_kernel, grid=(width // 128, tokens // block), in_sp...  68.9 us
    dot_general x3, matrix products, project(): jnp.dot(normed, weight, preferred_element_type=jnp.float32)  16.7 us
  transfers between devices with their start and end apart: 9, of which 4 were waited for; matrix products, arithmetic and copies ran while one was open for 4% of the time, Pallas kernels for 0%

profile of v3, /device:TPU:31, one launch (start us, length us, event | category | flops | bytes accessed | tf_op | source)
XLA Modules:
  0.0 363.3 jit_solution(15455035209409633398)
XLA Ops:
  0.0 3.8 %fusion.10 = f32[8,2,1280]{2,0,1:T(8,128)S(1)} fusion(bf16[2,1280,1280]{2,1,0:T(8,128)(2,1)} %param.13, bf16[8,1280]{1,0:T(8,128)(2,1)} %param.9), kind=kOutput, calls=%fused_computation.20 | convolution fusion | flops 52490240 | bytes 6656000 | tf_op jit(solution)/shard_map/bt,stc->sbc/dot_general | solution.py:522
  3.8 0.6 dynamic-slice_bitcast_fusion
  4.4 87.6 %conv_in.1 = (bf16[16,64,1280]{2,1,0:T(8,128)(2,1)}, bf16[16,64,1280]{2,1,0:T(8,128)(2,1)}, f32[2,1280]{1,0:T(2,128)}, bf16[16,1,1280]{2,1,0:T(2,128)(2,1)}) custom-call(bf16[8,4,32,1280]{3,2,1,0:T(8,128)(2,1)} %x_ref.1, bf16[5,1280]{1,0:T(8,128)(2,1)} %scale_ref.7, bf16[5,1280]{1,0:T(8,128)(2,1)} %shift_ref.7, f32[1,1280]{1,0:T(1,128)} %get-tuple-element.29.add_ref, ...), custom_call_target="tpu_custom_call" | custom-call | flops 30198988800 | bytes 29491200 | tf_op jit(solution)/shard_map/conv_in/pallas_call | solution.py:330
  92.0 0.1 collective-permute-start.1
  92.1 0.5 collective-permute-start
  92.6 7.0 %fusion.16 = (bf16[1,1280,20,64]{1,3,2,0:T(8,128)(2,1)}, bf16[1,1280,20,64]{1,3,2,0:T(8,128)(2,1)}, bf16[1,1280,20,64]{1,3,2,0:T(8,128)(2,1)}) fusion(bf16[3,1280,20,64]{1,3,2,0:T(8,128)(2,1)} %param.14), kind=kLoop, calls=%fused_computation.33 | loop fusion | bytes 19660800 | tf_op jit(solution)/shard_map/slice | solution.py:507
  99.7 0.7 convert_reduce_fusion.2
  100.4 0.0 collective-permute-done.1.theirs_ref
  100.4 0.0 copy-start.10
  100.4 0.0 collective-permute-done.other_ref
  100.4 0.0 copy-start.6
  100.4 0.6 copy-done.10
  101.0 0.1 copy-done.6
  101.1 40.2 %conv.2 = (bf16[16,64,1280]{2,1,0:T(8,128)(2,1)}, f32[2,1280]{1,0:T(2,128)}, bf16[16,1,1280]{2,1,0:T(2,128)(2,1)}) custom-call(bf16[16,64,1280]{2,1,0:T(8,128)(2,1)} %get-tuple-element.14.h_ref, bf16[16,1,1280]{2,1,0:T(2,128)(2,1)} %copy-done.6, f32[2,1280]{1,0:T(2,128)} %get-tuple-element.16.own_ref, f32[2,1280]{1,0:T(2,128)} %copy-done.10, ...), custom_call_target="tpu_custom_call" | custom-call | flops 30198988800 | bytes 29491200 | tf_op jit(solution)/shard_map/conv/pallas_call | solution.py:119
  141.2 0.0 copy-start.3
  141.2 0.9 reshape.48
  142.2 0.1 reduce_sum.27
  142.3 0.1 collective-permute-start.2
  142.3 0.7 convert_reduce_fusion.1
  143.1 0.4 collective-permute-done.2
  143.5 0.1 broadcast_in_dim.6
  143.5 0.1 sub.18
  143.6 0.1 broadcast_in_dim.7
  143.7 0.1 reshape.49
  143.8 2.5 fusion.2
  146.3 0.0 copy-start.5
  146.3 0.0 copy-done.3
  146.3 0.0 copy-start.2
  146.4 5.0 %convolution_convert_fusion.v0_ref = bf16[1024,1280]{1,0:T(8,128)(2,1)} fusion(bf16[1024,1280]{1,0:T(8,128)(2,1)S(1)} %bitcast.37, bf16[1280,1280]{0,1:T(8,128)(2,1)S(1)} %bitcast.36), kind=kOutput, calls=%fused_computation.9 | convolution fusion | flops 3356753920 | bytes 8519680 | tf_op jit(solution)/shard_map/dot_general | solution.py:505
  151.3 0.0 copy-done.5
  151.3 0.0 copy-done.2
  151.3 0.0 copy-start.1
  151.3 4.9 %convolution_convert_fusion.1.k0_ref = bf16[1024,1280]{1,0:T(8,128)(2,1)} fusion(bf16[1024,1280]{1,0:T(8,128)(2,1)S(1)} %bitcast.38, bf16[1280,1280]{0,1:T(8,128)(2,1)S(1)} %bitcast.35), kind=kOutput, calls=%fused_computation.10 | convolution fusion | flops 3356753920 | bytes 8519680 | tf_op jit(solution)/shard_map/dot_general | solution.py:505
  156.3 0.1 collective-permute-start.3
  156.4 0.4 collective-permute-start.4
  156.8 0.0 copy-done.1
  156.8 6.8 %convolution_convert_fusion.2.q_ref = bf16[1024,1280]{1,0:T(8,128)(2,1)} fusion(bf16[1024,1280]{1,0:T(8,128)(2,1)} %bitcast.39, bf16[1280,1280]{0,1:T(8,128)(2,1)S(1)} %bitcast.34), kind=kOutput, calls=%fused_computation.11 | convolution fusion | flops 3356753920 | bytes 8519680 | tf_op jit(solution)/shard_map/dot_general | solution.py:505
  163.6 0.0 collective-permute-done.3.k1_ref
  163.6 1.3 collective-permute-done.4.v1_ref
  164.9 68.9 %attend.1 = bf16[1024,1280]{1,0:T(8,128)(2,1)} custom-call(bf16[1024,1280]{1,0:T(8,128)(2,1)} %convolution_convert_fusion.2.q_ref, bf16[1024,1280]{1,0:T(8,128)(2,1)} %convolution_convert_fusion.1.k0_ref, bf16[1024,1280]{1,0:T(8,128)(2,1)} %collective-permute-done.3.k1_ref, bf16[1024,1280]{1,0:T(8,128)(2,1)} %convolution_convert_fusion.v0_ref, ...), custom_call_target="tpu_custom_call" | custom-call | tf_op jit(solution)/shard_map/attend/pallas_call | solution.py:469
  233.8 0.0 copy-done.4
  233.8 6.4 %convert_reduce_fusion = (f32[1280]{0:T(1024)S(1)}, f32[1280]{0:T(1024)S(1)}, bf16[16,64,1280]{2,1,0:T(8,128)(2,1)S(1)}) fusion(bf16[16,64,1280]{2,1,0:T(8,128)(2,1)} %bitcast.40, bf16[1280,1280,1]{1,0,2:T(8,128)(2,1)} %bitcast.41, bf16[16,64,1280]{2,1,0:T(8,128)(2,1)S(1)} %copy-done.4), kind=kOutput, calls=%fused_computation.1 | convolution fusion | flops 3364615680 | bytes 11151360 | tf_op jit(solution)/shard_map/dot_general | solution.py:511
  240.2 0.0 copy-start
  240.2 1.5 copy-done
  241.7 0.1 broadcast_select_fusion
  241.8 0.3 collective-permute-start.5
  242.1 0.0 copy-start.9
  242.1 0.4 collective-permute-start.6
  242.5 0.9 collective-permute-done.6.theirs_ref
  243.3 0.0 copy-start.11
  243.3 0.0 collective-permute-done.5.other_ref
  243.3 0.0 copy-start.7
  243.3 0.0 copy-done.9
  243.3 0.6 copy-done.11
  243.9 0.1 copy-done.7
  244.0 40.1 %conv.3 = (bf16[16,64,1280]{2,1,0:T(8,128)(2,1)}, f32[2,1280]{1,0:T(2,128)}, bf16[16,1,1280]{2,1,0:T(2,128)(2,1)}) custom-call(bf16[16,64,1280]{2,1,0:T(8,128)(2,1)} %copy-done, bf16[16,1,1280]{2,1,0:T(2,128)(2,1)} %copy-done.7, f32[2,1280]{1,0:T(2,128)} %copy-done.9, f32[2,1280]{1,0:T(2,128)} %copy-done.11, bf16[5,1280]{1,0:T(8,128)(2,1)} %scale_ref.7, ...), custom_call_target="tpu_custom_call" | custom-call | flops 30198988800 | bytes 29491200 | tf_op jit(solution)/shard_map/conv/pallas_call | solution.py:119
  284.0 0.4 collective-permute-start.7
  284.4 0.2 collective-permute-start.8
  284.6 1.0 collective-permute-done.8.theirs_ref
  285.6 0.0 collective-permute-done.7.other_ref
  285.6 0.6 copy-done.12
  286.2 0.0 copy-done.8
  286.2 73.7 %conv_out.1 = bf16[8,4,32,1280]{3,2,1,0:T(8,128)(2,1)} custom-call(bf16[16,64,1280]{2,1,0:T(8,128)(2,1)} %get-tuple-element.20.h_ref, bf16[16,1,1280]{2,1,0:T(2,128)(2,1)} %copy-done.8, f32[2,1280]{1,0:T(2,128)} %get-tuple-element.22.own_ref, f32[2,1280]{1,0:T(2,128)} %copy-done.12, bf16[5,1280]{1,0:T(8,128)(2,1)} %scale_ref.7, bf16[5,1280]{1,0:T(8,128)(2,1)} %shift_ref.7, ...), custom_call_target="tpu_custom_call" | custom-call | flops 30198988800 | bytes 29491200 | tf_op jit(solution)/shard_map/conv_out/pallas_call | solution.py:426
  359.9 3.4 copy.10
  (10 shorter events, 0.0 us)
Async XLA Ops:
  92.0 8.4 %collective-permute-start.1 = (f32[2,1280]{1,0:T(2,128)}, f32[2,1280]{1,0:T(2,128)S(1)}, u32[]{:S(2)}, u32[]{:S(2)}) collective-permute-start(f32[2,1280]{1,0:T(2,128)} %get-tuple-element.16.own_ref), channel_id=1, source_target_pairs={{0,1},{1,0},{2,3},{3,2},{4,5},{5,4},{6,7},{7,6},{8,9},{9,8},{10,11... | collective-permute-start | bytes 30728 | tf_op jit(solution)/shard_map/ppermute | solution.py:21
  92.1 8.3 %collective-permute-start = (bf16[16,1,1280]{2,1,0:T(2,128)(2,1)}, bf16[16,1,1280]{2,1,0:T(2,128)(2,1)S(1)}, u32[]{:S(2)}, u32[]{:S(2)}) collective-permute-start(bf16[16,1,1280]{2,1,0:T(2,128)(2,1)} %get-tuple-element.15), channel_id=1, source_target_pairs={{0,1},{1,0},{2,3},{3,2},{4,5},{5,4},{6,7},{7,6},{8,9},{9,8},{10,11... | collective-permute-start | bytes 122888 | tf_op jit(solution)/shard_map/ppermute | solution.py:21
  100.4 0.6 copy-start.10
  100.4 0.6 copy-start.6
  141.2 5.1 %copy-start.3 = (bf16[1,1280,20,64]{1,3,2,0:T(8,128)(2,1)S(1)}, bf16[1,1280,20,64]{1,3,2,0:T(8,128)(2,1)}, u32[]{:S(2)}) copy-start(bf16[1,1280,20,64]{1,3,2,0:T(8,128)(2,1)} %get-tuple-element.25) | copy-start | bytes 9830404
  142.3 1.2 collective-permute-start.2
  146.3 5.0 %copy-start.5 = (bf16[16,64,1280]{2,1,0:T(8,128)(2,1)}, bf16[16,64,1280]{2,1,0:T(8,128)(2,1)S(1)}, u32[]{:S(2)}) copy-start(bf16[16,64,1280]{2,1,0:T(8,128)(2,1)S(1)} %fusion.2) | copy-start | bytes 7864324
  146.3 5.0 %copy-start.2 = (bf16[1,1280,20,64]{1,3,2,0:T(8,128)(2,1)S(1)}, bf16[1,1280,20,64]{1,3,2,0:T(8,128)(2,1)}, u32[]{:S(2)}) copy-start(bf16[1,1280,20,64]{1,3,2,0:T(8,128)(2,1)} %get-tuple-element.27) | copy-start | bytes 9830404
  151.3 5.4 %copy-start.1 = (bf16[1,1280,20,64]{1,3,2,0:T(8,128)(2,1)S(1)}, bf16[1,1280,20,64]{1,3,2,0:T(8,128)(2,1)}, u32[]{:S(2)}) copy-start(bf16[1,1280,20,64]{1,3,2,0:T(8,128)(2,1)} %get-tuple-element.26) | copy-start | bytes 9830404
  156.3 7.3 %collective-permute-start.3 = (bf16[1024,1280]{1,0:T(8,128)(2,1)}, bf16[1024,1280]{1,0:T(8,128)(2,1)}, u32[]{:S(2)}, u32[]{:S(2)}) collective-permute-start(bf16[1024,1280]{1,0:T(8,128)(2,1)} %convolution_convert_fusion.1.k0_ref), channel_id=1, source_target_pairs={{0,1},{1,0},{2,3},{3,2},{4,5},{5,4},{6,7},{7,6},{8,9},{9,8},{10,11... | collective-permute-start | bytes 7864328 | tf_op jit(solution)/shard_map/ppermute | solution.py:21
  156.4 8.5 %collective-permute-start.4 = (bf16[1024,1280]{1,0:T(8,128)(2,1)}, bf16[1024,1280]{1,0:T(8,128)(2,1)}, u32[]{:S(2)}, u32[]{:S(2)}) collective-permute-start(bf16[1024,1280]{1,0:T(8,128)(2,1)} %convolution_convert_fusion.v0_ref), channel_id=1, source_target_pairs={{0,1},{1,0},{2,3},{3,2},{4,5},{5,4},{6,7},{7,6},{8,9},{9,8},{10,11... | collective-permute-start | bytes 7864328 | tf_op jit(solution)/shard_map/ppermute | solution.py:21
  163.6 70.2 %copy-start.4 = (bf16[16,64,1280]{2,1,0:T(8,128)(2,1)S(1)}, bf16[16,64,1280]{2,1,0:T(8,128)(2,1)}, u32[]{:S(2)}) copy-start(bf16[16,64,1280]{2,1,0:T(8,128)(2,1)} %get-tuple-element.18) | copy-start | bytes 7864324
  240.2 1.5 copy-start
  241.8 1.5 collective-permute-start.5
  242.1 1.3 copy-start.9
  242.1 1.2 collective-permute-start.6
  243.3 0.6 copy-start.11
  243.3 0.6 copy-start.7
  284.0 1.5 collective-permute-start.7
  284.4 1.2 collective-permute-start.8
  285.6 0.6 copy-start.12
  285.6 0.6 copy-start.8

commit v4 on v3

--- a/solution.py
+++ b/solution.py
@@ -68,27 +68,40 @@
     lax.fori_loop(0, rows, one_row, 0)
 
 
-def taps(act, w_ref, rows, cols, channels):
+def fetch(w_ref, wbuf, w_sem, j, n):
+    width = wbuf.shape[-1]
+    slot = lax.rem(n, 2)
+    return pltpu.make_async_copy(w_ref.at[j, :, :, :, pl.ds(pl.multiple_of(n * width, width), width)], wbuf.at[slot], w_sem.at[slot])
+
+
+def taps(act, wbuf, slot, first, rows, cols, channels):
     total = None
     for k in range(9):
-        lhs = act[k % 3, pl.ds(k // 3, rows)].reshape(rows * cols, channels)
-        part = jnp.dot(lhs, w_ref[k // 3, k % 3], preferred_element_type=jnp.float32)
+        lhs = act[k % 3, pl.ds(k // 3 + first, rows)].reshape(rows * cols, channels)
+        part = jnp.dot(lhs, wbuf[slot, k // 3, k % 3], preferred_element_type=jnp.float32)
         total = part if total is None else total + part
     return total
 
 
-def conv_kernel(residual, norm_idx, h_ref, other_ref, own_ref, theirs_ref, scale_ref, shift_ref, w_ref, add_ref, out_ref, sums_ref, edge_ref, act, norm_ref):
+def conv_kernel(residual, norm_idx, j, h_ref, other_ref, own_ref, theirs_ref, scale_ref, shift_ref, w_ref, add_ref, out_ref, sums_ref, edge_ref, act, norm_ref, wbuf, w_sem):
     rows, cols, channels = h_ref.shape
-    width = w_ref.shape[-1]
+    width = wbuf.shape[-1]
+    n = pl.program_id(0)
     _, core = place(lax.axis_index(SP))
 
-    @pl.when(pl.program_id(0) == 0)
-    def _():
+    @pl.when(n == 0)
+    def _():
+        fetch(w_ref, wbuf, w_sem, j, n).start()
         count = 2 * rows * cols * (channels // GROUPS)
         norm_ref[...] = group_rows(own_ref[...] + theirs_ref[...], scale_ref[norm_idx:norm_idx + 1, :], shift_ref[norm_idx:norm_idx + 1, :], count)
         fill_act(core, h_ref, other_ref, norm_ref, act)
 
-    full = taps(act, w_ref, rows, cols, channels)
+    @pl.when(n + 1 < pl.num_programs(0))
+    def _():
+        fetch(w_ref, wbuf, w_sem, j, n + 1).start()
+
+    fetch(w_ref, wbuf, w_sem, j, n).wait()
+    full = taps(act, wbuf, lax.rem(n, 2), 0, rows, cols, channels)
     full = full + (add_ref[...].reshape(rows * cols, width).astype(jnp.float32) if residual else add_ref[...])
     half = full.astype(jnp.bfloat16)
     out_ref[...] = half.reshape(rows, cols, width)
@@ -104,10 +117,10 @@
         edge_ref[...] = out_ref[:, :1, :]
 
 
-def conv_specs(rows, cols, channels, j, nb, residual):
+def conv_specs(rows, cols, channels, nb, residual):
     whole = lambda *s: pl.BlockSpec(s, lambda n: (0,) * len(s))
     add = pl.BlockSpec((rows, cols, nb), lambda n: (0, 0, n)) if residual else pl.BlockSpec((1, nb), lambda n: (0, n))
-    return [whole(rows, cols, channels), whole(rows, 1, channels), whole(2, channels), whole(2, channels), whole(5, channels), whole(5, channels), pl.BlockSpec((None, 3, 3, channels, nb), lambda n: (j, 0, 0, 0, n)), add]
+    return [whole(rows, cols, channels), whole(rows, 1, channels), whole(2, channels), whole(2, channels), whole(5, channels), whole(5, channels), pl.BlockSpec(memory_space=pl.ANY), add]
 
 
 def conv_cost(rows, cols, channels):
@@ -117,12 +130,12 @@
 def conv(h, other, own, theirs, scale, shift, norm_idx, w, j, add, nb=256):
     rows, cols, channels = h.shape
     return pl.pallas_call(
-        functools.partial(conv_kernel, add.ndim == 3, norm_idx),
+        functools.partial(conv_kernel, add.ndim == 3, norm_idx, j),
         grid=(channels // nb,),
-        in_specs=conv_specs(rows, cols, channels, j, nb, add.ndim == 3),
+        in_specs=conv_specs(rows, cols, channels, nb, add.ndim == 3),
         out_specs=[pl.BlockSpec((rows, cols, nb), lambda n: (0, 0, n)), pl.BlockSpec((2, nb), lambda n: (0, n)), pl.BlockSpec((rows, 1, nb), lambda n: (0, 0, n))],
         out_shape=[jax.ShapeDtypeStruct((rows, cols, channels), jnp.bfloat16), jax.ShapeDtypeStruct((2, channels), jnp.float32), jax.ShapeDtypeStruct((rows, 1, channels), jnp.bfloat16)],
-        scratch_shapes=[pltpu.VMEM((3, rows + 2, cols, channels), jnp.bfloat16), pltpu.VMEM((3, channels), jnp.float32)],
+        scratch_shapes=[pltpu.VMEM((3, rows + 2, cols, channels), jnp.bfloat16), pltpu.VMEM((3, channels), jnp.float32), pltpu.VMEM((2, 3, 3, channels, nb), jnp.bfloat16), pltpu.SemaphoreType.DMA((2,))],
         compiler_params=pltpu.CompilerParams(vmem_limit_bytes=62 * 1024 * 1024),
         cost_estimate=conv_cost(rows, cols, channels),
         name="conv",
@@ -201,11 +214,7 @@
             def _():
                 tell(i, k).start()
 
-    def start_rest(c, carry):
-        start_chunk(c)
-        return carry
-
-    lax.fori_loop(1, chunks, start_rest, 0)
+    start_chunk(1)
     total = stats[mine]
     for d in range(16):
         @pl.when(me != d)
@@ -217,6 +226,7 @@
         total = total + jnp.where(me != d, heard[d], 0.0)
     count = 2 * rows * cols * (channels // GROUPS)
     norm_ref[...] = group_rows(total, scale_ref[0:1, :], shift_ref[0:1, :], count)
+    acc[...] = jnp.zeros_like(acc)
     zeros = jnp.zeros((cols, width), jnp.bfloat16)
     for dx in range(3):
         act[dx, 0] = zeros
@@ -249,6 +259,11 @@
 
         lend(c).start()
         keep_raw(c).start()
+
+        @pl.when(c + 2 < chunks)
+        def _():
+            start_chunk(c + 2)
+
         mean, mult, shift = norm_ref[0:1, lanes(c)], norm_ref[1:2, lanes(c)], norm_ref[2:3, lanes(c)]
 
         def activate(v):
@@ -269,19 +284,11 @@
         weight(c).wait()
 
         def one_block(n, carry2):
-            part = None
+            part = acc[n]
             for k in range(9):
                 lhs = act[k % 3, pl.ds(k // 3, rows)].reshape(rows * cols, width)
-                dot = jnp.dot(lhs, weights[c, k // 3, k % 3, :, lanes(n)], preferred_element_type=jnp.float32)
-                part = dot if part is None else part + dot
-
-            @pl.when(c == 0)
-            def _():
-                acc[n] = part
-
-            @pl.when(c > 0)
-            def _():
-                acc[n] += part
+                part = part + jnp.dot(lhs, weights[c, k // 3, k % 3, :, lanes(n)], preferred_element_type=jnp.float32)
+            acc[n] = part
             return carry2
 
         lax.fori_loop(0, chunks, one_block, 0)
@@ -343,10 +350,10 @@
     )(x, scale, shift, add, w)
 
 
-def conv_out_kernel(norm_idx, h_ref, other_ref, own_ref, theirs_ref, scale_ref, shift_ref, w_ref, add_ref, out_ref, act, norm_ref, done, send_sem, recv_sem, self_sem):
+def conv_out_kernel(norm_idx, j, h_ref, other_ref, own_ref, theirs_ref, scale_ref, shift_ref, w_ref, add_ref, out_ref, act, norm_ref, wbuf, done, w_sem, send_sem, recv_sem, self_sem):
     rows, cols, channels = h_ref.shape
     images, trows, tcols, _ = out_ref.shape
-    width = w_ref.shape[-1]
+    width = wbuf.shape[-1]
     n, chunks = pl.program_id(0), pl.num_programs(0)
     sp, z = lax.axis_index(SP), lax.axis_index(SP2)
     y, core = place(sp)
@@ -356,6 +363,7 @@
 
     @pl.when(n == 0)
     def _():
+        fetch(w_ref, wbuf, w_sem, j, n).start()
         barrier = pltpu.get_barrier_semaphore()
         for i in range(images):
             @pl.when(jnp.logical_not(own & (mine == i)))
@@ -366,9 +374,6 @@
         norm_ref[...] = group_rows(own_ref[...] + theirs_ref[...], scale_ref[norm_idx:norm_idx + 1, :], shift_ref[norm_idx:norm_idx + 1, :], count)
         fill_act(core, h_ref, other_ref, norm_ref, act)
         pl.semaphore_wait(barrier, 8 - own.astype(jnp.int32))
-
-    full = taps(act, w_ref, rows, cols, channels) + add_ref[...].reshape(rows * cols, width).astype(jnp.float32)
-    done[n] = full.astype(jnp.bfloat16).reshape(rows, cols, width)
 
     def lanes(c):
         return pl.ds(pl.multiple_of(c * width, width), width)
@@ -388,10 +393,20 @@
     def is_self(s):
         return (s // 2 == sp) & (2 * core + s % 2 == z)
 
-    for s in range(8):
-        @pl.when(jnp.logical_not(is_self(s)))
-        def _():
-            send(n, s).start()
+    @pl.when(n + 1 < chunks)
+    def _():
+        fetch(w_ref, wbuf, w_sem, j, n + 1).start()
+
+    fetch(w_ref, wbuf, w_sem, j, n).wait()
+    part = rows // 2
+    for m in range(2):
+        span = slice(m * part, (m + 1) * part)
+        full = taps(act, wbuf, lax.rem(n, 2), m * part, part, cols, channels) + add_ref[span].reshape(part * cols, width).astype(jnp.float32)
+        done[n, span] = full.astype(jnp.bfloat16).reshape(part, cols, width)
+        for s in range(4 * m, 4 * m + 4):
+            @pl.when(jnp.logical_not(is_self(s)))
+            def _():
+                send(n, s).start()
 
     @pl.when(own)
     def _():
@@ -424,12 +439,12 @@
     rows, cols, channels = h.shape
     chunks = channels // nb
     return pl.pallas_call(
-        functools.partial(conv_out_kernel, norm_idx),
+        functools.partial(conv_out_kernel, norm_idx, j),
         grid=(chunks,),
-        in_specs=conv_specs(rows, cols, channels, j, nb, True),
+        in_specs=conv_specs(rows, cols, channels, nb, True),
         out_specs=pl.BlockSpec(memory_space=pl.ANY),
         out_shape=jax.ShapeDtypeStruct((8, rows // 4, cols // 2, channels), jnp.bfloat16),
-        scratch_shapes=[pltpu.VMEM((3, rows + 2, cols, channels), jnp.bfloat16), pltpu.VMEM((3, channels), jnp.float32), pltpu.VMEM((chunks, rows, cols, nb), jnp.bfloat16),
+        scratch_shapes=[pltpu.VMEM((3, rows + 2, cols, channels), jnp.bfloat16), pltpu.VMEM((3, channels), jnp.float32), pltpu.VMEM((2, 3, 3, channels, nb), jnp.bfloat16), pltpu.VMEM((chunks, rows, cols, nb), jnp.bfloat16), pltpu.SemaphoreType.DMA((2,)),
                         pltpu.SemaphoreType.DMA((chunks, 8)), pltpu.SemaphoreType.DMA((chunks, 8)), pltpu.SemaphoreType.DMA((chunks,))],
         compiler_params=pltpu.CompilerParams(collective_id=1, has_side_effects=True, vmem_limit_bytes=62 * 1024 * 1024),
         cost_estimate=conv_cost(rows, cols, channels),
@@ -439,41 +454,81 @@
 
 NT = (((1,), (1,)), ((), ()))
 
-def attend_kernel(q_ref, k0_ref, k1_ref, v0_ref, v1_ref, o_ref, vt):
+def attend_kernel(block, chunk, q_ref, k0_ref, k1_ref, v0_ref, v1_ref, qn_ref, k0n_ref, k1n_ref, o_ref, sa, sb, peak_ref, vt):
     tokens = k0_ref.shape[0]
-    @pl.when(pl.program_id(1) == 0)
-    def _():
-        vt[:, :tokens] = v0_ref[...].T
-        vt[:, tokens:] = v1_ref[...].T
-    q = q_ref[...] * jnp.bfloat16(0.125)
-    lane = lax.broadcasted_iota(jnp.int32, q.shape, 1)
+    pieces = 2 * tokens // chunk
+    blocks = tokens // block
+    items = [(b, h) for b in range(blocks) for h in range(2)]
+    bufs = [sa, sb]
+    lane = lax.broadcasted_iota(jnp.int32, (block, 128), 1)
+
+    def query(ref, item):
+        b, h = item
+        q = ref[b * block:(b + 1) * block, :] * jnp.bfloat16(0.125)
+        keep = (lane >= 64) if h else (lane < 64)
+        return jnp.where(keep, q, jnp.zeros_like(q))
+
+    def part(first, second, c):
+        lo = c * chunk
+        return first[lo:lo + chunk, :] if lo < tokens else second[lo - tokens:lo - tokens + chunk, :]
+
+    def score(buf, q, first, second, c, peak):
+        s = lax.dot_general(part(first, second, c), q, NT, preferred_element_type=jnp.float32)
+        buf[c * chunk:(c + 1) * chunk, :] = s
+        top = jnp.max(s.reshape(chunk // 8, 8, block), axis=0)
+        return top if peak is None else jnp.maximum(peak, top)
+
+    p = pl.program_id(0)
+
+    @pl.when(p == 0)
+    def _():
+        q = query(q_ref, items[0])
+        peak = None
+        for c in range(pieces):
+            peak = score(sa, q, k0_ref, k1_ref, c, peak)
+        peak_ref[...] = peak
+
+    vt[:, :tokens] = v0_ref[...].T
+    vt[:, tokens:] = v1_ref[...].T
+    peak8 = peak_ref[...]
     outs = []
-    for head in range(2):
-        keep = (lane >= 64) if head else (lane < 64)
-        qh = jnp.where(keep, q, jnp.zeros_like(q))
-        s0 = lax.dot_general(k0_ref[...], qh, NT, preferred_element_type=jnp.float32)
-        s1 = lax.dot_general(k1_ref[...], qh, NT, preferred_element_type=jnp.float32)
-        peak = jnp.maximum(jnp.max(s0, axis=0, keepdims=True), jnp.max(s1, axis=0, keepdims=True))
-        p0 = jnp.exp(s0 - peak)
-        p1 = jnp.exp(s1 - peak)
-        total = jnp.sum(p0, axis=0, keepdims=True) + jnp.sum(p1, axis=0, keepdims=True)
-        vh = vt[64 * head:64 * head + 64, :]
-        acc = jnp.dot(vh[:, :tokens], p0.astype(jnp.bfloat16), preferred_element_type=jnp.float32)
-        acc = acc + jnp.dot(vh[:, tokens:], p1.astype(jnp.bfloat16), preferred_element_type=jnp.float32)
-        outs.append(acc / total)
-    o_ref[...] = jnp.concatenate(outs, axis=0).T.astype(o_ref.dtype)
-
-def attend(query, keys, vals, other_keys, other_vals, block=512):
+    for t, item in enumerate(items):
+        b, h = item
+        cur, nxt = bufs[t % 2], bufs[(t + 1) % 2]
+        last = t == len(items) - 1
+        q = query(qn_ref, items[0]) if last else query(q_ref, items[t + 1])
+        kf, ks = (k0n_ref, k1n_ref) if last else (k0_ref, k1_ref)
+        peak = jnp.max(peak8, axis=0, keepdims=True)
+        nextp, total, acc = None, None, None
+        for c in range(pieces):
+            nextp = score(nxt, q, kf, ks, c, nextp)
+            e = jnp.exp(cur[c * chunk:(c + 1) * chunk, :] - peak)
+            part_sum = jnp.sum(e.reshape(chunk // 8, 8, block), axis=0)
+            total = part_sum if total is None else total + part_sum
+            d = jnp.dot(vt[64 * h:64 * h + 64, c * chunk:(c + 1) * chunk], e.astype(jnp.bfloat16), preferred_element_type=jnp.float32)
+            acc = d if acc is None else acc + d
+        outs.append(acc / jnp.sum(total, axis=0, keepdims=True))
+        peak8 = nextp
+        if h == 1:
+            o_ref[b * block:(b + 1) * block, :] = jnp.concatenate(outs, axis=0).T.astype(o_ref.dtype)
+            outs = []
+    peak_ref[...] = peak8
+
+def attend(query, keys, vals, other_keys, other_vals, block=512, chunk=512):
     tokens, width = query.shape
-    kv = lambda p, b: (0, p)
+    pairs = width // 128
+    here = pl.BlockSpec((tokens, 128), lambda p: (0, p))
+    after = pl.BlockSpec((tokens, 128), lambda p: (0, jnp.minimum(p + 1, pairs - 1)))
     return pl.pallas_call(
-        attend_kernel, grid=(width // 128, tokens // block),
-        in_specs=[pl.BlockSpec((block, 128), lambda p, b: (b, p))] + [pl.BlockSpec((tokens, 128), kv)] * 4,
-        out_specs=pl.BlockSpec((block, 128), lambda p, b: (b, p)),
+        functools.partial(attend_kernel, block, chunk), grid=(pairs,),
+        in_specs=[here] * 5 + [after] * 3,
+        out_specs=here,
         out_shape=jax.ShapeDtypeStruct((tokens, width), jnp.bfloat16),
-        scratch_shapes=[pltpu.VMEM((128, 2 * tokens), jnp.bfloat16)],
-        compiler_params=pltpu.CompilerParams(vmem_limit_bytes=60 * 1024 * 1024), name="attend",
-    )(query, keys, other_keys, vals, other_vals)
+        scratch_shapes=[pltpu.VMEM((2 * tokens, block), jnp.float32), pltpu.VMEM((2 * tokens, block), jnp.float32), pltpu.VMEM((8, block), jnp.float32), pltpu.VMEM((128, 2 * tokens), jnp.bfloat16)],
+        compiler_params=pltpu.CompilerParams(vmem_limit_bytes=60 * 1024 * 1024),
+        cost_estimate=pl.CostEstimate(flops=32 * tokens * tokens * width, bytes_accessed=10 * tokens * width, transcendentals=2 * tokens * tokens * width // 64),
+        name="attend",
+    )(query, keys, other_keys, vals, other_vals, query, keys, other_keys)
 
 
 def norm_rows(sums, scale, shift, count):

time: 364 us -> 342 us (0.940)
  Pallas kernels: 310 us -> 287 us
    pallas_call x4, Pallas kernels: 223 us -> 204 us  [the longest x2 77.1 us: conv(): pl.pallas_call(functools.partial(conv_kernel, add.ndim == 3, norm_idx, j)...]
    pallas_call x1, Pallas kernels: 87.6 us -> 83.1 us  [conv_in(): pl.pallas_call(conv_in_kernel, in_specs=[hbm, vmem, vmem, vmem, hbm], out...]
  transfers between devices with their start and end apart: 9 -> 9, of which waited for: 4 -> 4; matrix products, arithmetic and copies ran while one was open for 4% -> 5% of each run, Pallas kernels for 0% -> 0%
where the time goes in v4:
time: 342 us; the launch traced here: 340 us
  Pallas kernels  287 us (84%)
  matrix products  26.9 us (8%)
  local copies, waits for them, and re-layouts  15.7 us (5%)
  other arithmetic  4.26 us (1%)
    pallas_call x1, Pallas kernels, conv_in(): pl.pallas_call(conv_in_kernel, in_specs=[hbm, vmem, vmem, vmem, hbm], out...  83.1 us
    pallas_call x2, Pallas kernels, conv(): pl.pallas_call(functools.partial(conv_kernel, add.ndim == 3, norm_idx, j)...  77.1 us
    pallas_call x1, Pallas kernels, conv_out(): pl.pallas_call(functools.partial(conv_out_kernel, norm_idx, j), grid=(chu...  76.7 us
    pallas_call x1, Pallas kernels, attend(): pl.pallas_call(functools.partial(attend_kernel, block, chunk), grid=(pair...  49.9 us
    dot_general x3, matrix products, project(): jnp.dot(normed, weight, preferred_element_type=jnp.float32)  16.7 us
    slice x1, local copies, waits for them, and re-layouts, attention_block(): keys, vals = (project(flat[1]), project(flat[2]))  7.04 us
  transfers between devices with their start and end apart: 9, of which 4 were waited for; matrix products, arithmetic and copies ran while one was open for 5% of the time, Pallas kernels for 0%

profile of v4, /device:TPU:31, one launch (start us, length us, event | category | flops | bytes accessed | tf_op | source)
XLA Modules:
  0.0 339.9 jit_solution(3209704856768598087)
XLA Ops:
  0.0 3.8 %fusion.10 = f32[8,2,1280]{2,0,1:T(8,128)S(1)} fusion(bf16[2,1280,1280]{2,1,0:T(8,128)(2,1)} %param.13, bf16[8,1280]{1,0:T(8,128)(2,1)} %param.9), kind=kOutput, calls=%fused_computation.20 | convolution fusion | flops 52490240 | bytes 6656000 | tf_op jit(solution)/shard_map/bt,stc->sbc/dot_general | solution.py:577
  3.8 0.6 dynamic-slice_bitcast_fusion
  4.4 83.1 %conv_in.1 = (bf16[16,64,1280]{2,1,0:T(8,128)(2,1)}, bf16[16,64,1280]{2,1,0:T(8,128)(2,1)}, f32[2,1280]{1,0:T(2,128)}, bf16[16,1,1280]{2,1,0:T(2,128)(2,1)}) custom-call(bf16[8,4,32,1280]{3,2,1,0:T(8,128)(2,1)} %x_ref.1, bf16[5,1280]{1,0:T(8,128)(2,1)} %scale_ref.7, bf16[5,1280]{1,0:T(8,128)(2,1)} %shift_ref.7, f32[1,1280]{1,0:T(1,128)} %get-tuple-element.29.add_ref, ...), custom_call_target="tpu_custom_call" | custom-call | flops 30198988800 | bytes 29491200 | tf_op jit(solution)/shard_map/conv_in/pallas_call | solution.py:337
  87.6 0.2 collective-permute-start.1
  87.8 0.4 collective-permute-start
  88.2 7.0 %fusion.16 = (bf16[1,1280,20,64]{1,3,2,0:T(8,128)(2,1)}, bf16[1,1280,20,64]{1,3,2,0:T(8,128)(2,1)}, bf16[1,1280,20,64]{1,3,2,0:T(8,128)(2,1)}) fusion(bf16[3,1280,20,64]{1,3,2,0:T(8,128)(2,1)} %param.14), kind=kLoop, calls=%fused_computation.33 | loop fusion | bytes 19660800 | tf_op jit(solution)/shard_map/slice | solution.py:562
  95.2 0.7 convert_reduce_fusion.2
  96.0 0.0 collective-permute-done.1.theirs_ref
  96.0 0.0 copy-start.10
  96.0 0.0 collective-permute-done.other_ref
  96.0 0.0 copy-start.6
  96.0 0.6 copy-done.10
  96.6 0.1 copy-done.6
  96.6 38.5 %conv.2 = (bf16[16,64,1280]{2,1,0:T(8,128)(2,1)}, f32[2,1280]{1,0:T(2,128)}, bf16[16,1,1280]{2,1,0:T(2,128)(2,1)}) custom-call(bf16[16,64,1280]{2,1,0:T(8,128)(2,1)} %get-tuple-element.14.h_ref, bf16[16,1,1280]{2,1,0:T(2,128)(2,1)} %copy-done.6, f32[2,1280]{1,0:T(2,128)} %get-tuple-element.16.own_ref, f32[2,1280]{1,0:T(2,128)} %copy-done.10, ...), custom_call_target="tpu_custom_call" | custom-call | flops 30198988800 | bytes 29491200 | tf_op jit(solution)/shard_map/conv/pallas_call | solution.py:132
  135.1 0.0 copy-start.3
  135.2 0.9 reshape.48
  136.1 0.1 reduce_sum.27
  136.2 0.1 collective-permute-start.2
  136.3 0.7 convert_reduce_fusion.1
  137.0 0.3 collective-permute-done.2
  137.4 0.1 broadcast_in_dim.6
  137.5 0.1 sub.18
  137.5 0.1 broadcast_in_dim.7
  137.6 0.1 reshape.49
  137.7 2.5 fusion.2
  140.2 0.0 copy-start.5
  140.3 0.0 copy-done.3
  140.3 0.0 copy-start.2
  140.3 5.0 %convolution_convert_fusion.v0_ref = bf16[1024,1280]{1,0:T(8,128)(2,1)} fusion(bf16[1024,1280]{1,0:T(8,128)(2,1)S(1)} %bitcast.37, bf16[1280,1280]{0,1:T(8,128)(2,1)S(1)} %bitcast.36), kind=kOutput, calls=%fused_computation.9 | convolution fusion | flops 3356753920 | bytes 8519680 | tf_op jit(solution)/shard_map/dot_general | solution.py:560
  145.2 0.0 copy-done.5
  145.2 0.0 copy-done.2
  145.2 0.0 copy-start.1
  145.2 4.9 %convolution_convert_fusion.1.k0_ref.k0n_ref = bf16[1024,1280]{1,0:T(8,128)(2,1)} fusion(bf16[1024,1280]{1,0:T(8,128)(2,1)S(1)} %bitcast.38, bf16[1280,1280]{0,1:T(8,128)(2,1)S(1)} %bitcast.35), kind=kOutput, calls=%fused_computation.10 | convolution fusion | flops 3356753920 | bytes 8519680 | tf_op jit(solution)/shard_map/dot_general | solution.py:560
  150.2 0.2 collective-permute-start.3
  150.3 0.3 collective-permute-start.4
  150.7 0.0 copy-done.1
  150.7 6.8 %convolution_convert_fusion.2.q_ref.qn_ref = bf16[1024,1280]{1,0:T(8,128)(2,1)} fusion(bf16[1024,1280]{1,0:T(8,128)(2,1)} %bitcast.39, bf16[1280,1280]{0,1:T(8,128)(2,1)S(1)} %bitcast.34), kind=kOutput, calls=%fused_computation.11 | convolution fusion | flops 3356753920 | bytes 8519680 | tf_op jit(solution)/shard_map/dot_general | solution.py:560
  157.5 0.0 copy-start.4
  157.5 0.0 collective-permute-done.3.k1_ref.k1n_ref
  157.5 1.3 collective-permute-done.4.v1_ref
  158.8 49.9 %attend.1 = bf16[1024,1280]{1,0:T(8,128)(2,1)} custom-call(bf16[1024,1280]{1,0:T(8,128)(2,1)} %convolution_convert_fusion.2.q_ref.qn_ref, bf16[1024,1280]{1,0:T(8,128)(2,1)} %convolution_convert_fusion.1.k0_ref.k0n_ref, bf16[1024,1280]{1,0:T(8,128)(2,1)} %collective-permute-done.3.k1_ref.k1n_ref, bf16[1024,1280]{1,0:T(8,128)(2,1)} %convolution_convert_fusion.v0_ref, ...), custom_call_target="tpu_custom_call" | custom-call | flops 42949672960 | bytes 13107200 | tf_op jit(solution)/shard_map/attend/pallas_call | solution.py:522
  208.7 0.0 copy-done.4
  208.7 6.4 %convert_reduce_fusion = (f32[1280]{0:T(1024)S(1)}, f32[1280]{0:T(1024)S(1)}, bf16[16,64,1280]{2,1,0:T(8,128)(2,1)S(1)}) fusion(bf16[16,64,1280]{2,1,0:T(8,128)(2,1)} %bitcast.41, bf16[1280,1280,1]{1,0,2:T(8,128)(2,1)} %bitcast.40, bf16[16,64,1280]{2,1,0:T(8,128)(2,1)S(1)} %copy-done.4), kind=kOutput, calls=%fused_computation.1 | convolution fusion | flops 3364615680 | bytes 11151360 | tf_op jit(solution)/shard_map/dot_general | solution.py:566
  215.1 0.0 copy-start
  215.2 1.5 copy-done
  216.6 0.1 broadcast_select_fusion
  216.7 0.3 collective-permute-start.5
  217.0 0.0 copy-start.9
  217.0 0.4 collective-permute-start.6
  217.4 0.9 collective-permute-done.6.theirs_ref
  218.3 0.0 copy-start.11
  218.3 0.0 collective-permute-done.5.other_ref
  218.3 0.0 copy-done.9
  218.3 0.6 copy-done.11
  218.9 0.1 copy-done.7
  218.9 38.6 %conv.3 = (bf16[16,64,1280]{2,1,0:T(8,128)(2,1)}, f32[2,1280]{1,0:T(2,128)}, bf16[16,1,1280]{2,1,0:T(2,128)(2,1)}) custom-call(bf16[16,64,1280]{2,1,0:T(8,128)(2,1)} %copy-done, bf16[16,1,1280]{2,1,0:T(2,128)(2,1)} %copy-done.7, f32[2,1280]{1,0:T(2,128)} %copy-done.9, f32[2,1280]{1,0:T(2,128)} %copy-done.11, bf16[5,1280]{1,0:T(8,128)(2,1)} %scale_ref.7, ...), custom_call_target="tpu_custom_call" | custom-call | flops 30198988800 | bytes 29491200 | tf_op jit(solution)/shard_map/conv/pallas_call | solution.py:132
  257.6 0.4 collective-permute-start.7
  257.9 0.2 collective-permute-start.8
  258.1 1.0 collective-permute-done.8.theirs_ref
  259.1 0.0 collective-permute-done.7.other_ref
  259.1 0.6 copy-done.12
  259.7 0.0 copy-done.8
  259.7 76.7 %conv_out.1 = bf16[8,4,32,1280]{3,2,1,0:T(8,128)(2,1)} custom-call(bf16[16,64,1280]{2,1,0:T(8,128)(2,1)} %get-tuple-element.20.h_ref, bf16[16,1,1280]{2,1,0:T(2,128)(2,1)} %copy-done.8, f32[2,1280]{1,0:T(2,128)} %get-tuple-element.22.own_ref, f32[2,1280]{1,0:T(2,128)} %copy-done.12, bf16[5,1280]{1,0:T(8,128)(2,1)} %scale_ref.7, bf16[5,1280]{1,0:T(8,128)(2,1)} %shift_ref.7, ...), custom_call_target="tpu_custom_call" | custom-call | flops 30198988800 | bytes 29491200 | tf_op jit(solution)/shard_map/conv_out/pallas_call | solution.py:441
  336.5 3.4 %copy.10 = bf16[8,4,32,1280]{3,2,1,0:T(8,128)(2,1)} copy(bf16[8,4,32,1280]{3,2,1,0:T(8,128)(2,1)} %conv_out.1) | data formatting | bytes 5242880
  (10 shorter events, 0.0 us)
Async XLA Ops:
  87.6 8.4 %collective-permute-start.1 = (f32[2,1280]{1,0:T(2,128)}, f32[2,1280]{1,0:T(2,128)S(1)}, u32[]{:S(2)}, u32[]{:S(2)}) collective-permute-start(f32[2,1280]{1,0:T(2,128)} %get-tuple-element.16.own_ref), channel_id=1, source_target_pairs={{0,1},{1,0},{2,3},{3,2},{4,5},{5,4},{6,7},{7,6},{8,9},{9,8},{10,11... | collective-permute-start | bytes 30728 | tf_op jit(solution)/shard_map/ppermute | solution.py:21
  87.8 8.2 %collective-permute-start = (bf16[16,1,1280]{2,1,0:T(2,128)(2,1)}, bf16[16,1,1280]{2,1,0:T(2,128)(2,1)S(1)}, u32[]{:S(2)}, u32[]{:S(2)}) collective-permute-start(bf16[16,1,1280]{2,1,0:T(2,128)(2,1)} %get-tuple-element.15), channel_id=1, source_target_pairs={{0,1},{1,0},{2,3},{3,2},{4,5},{5,4},{6,7},{7,6},{8,9},{9,8},{10,11... | collective-permute-start | bytes 122888 | tf_op jit(solution)/shard_map/ppermute | solution.py:21
  96.0 0.6 copy-start.10
  96.0 0.6 copy-start.6
  135.1 5.1 %copy-start.3 = (bf16[1,1280,20,64]{1,3,2,0:T(8,128)(2,1)S(1)}, bf16[1,1280,20,64]{1,3,2,0:T(8,128)(2,1)}, u32[]{:S(2)}) copy-start(bf16[1,1280,20,64]{1,3,2,0:T(8,128)(2,1)} %get-tuple-element.25) | copy-start | bytes 9830404
  136.2 1.2 collective-permute-start.2
  140.2 5.0 %copy-start.5 = (bf16[16,64,1280]{2,1,0:T(8,128)(2,1)}, bf16[16,64,1280]{2,1,0:T(8,128)(2,1)S(1)}, u32[]{:S(2)}) copy-start(bf16[16,64,1280]{2,1,0:T(8,128)(2,1)S(1)} %fusion.2) | copy-start | bytes 7864324
  140.3 5.0 %copy-start.2 = (bf16[1,1280,20,64]{1,3,2,0:T(8,128)(2,1)S(1)}, bf16[1,1280,20,64]{1,3,2,0:T(8,128)(2,1)}, u32[]{:S(2)}) copy-start(bf16[1,1280,20,64]{1,3,2,0:T(8,128)(2,1)} %get-tuple-element.27) | copy-start | bytes 9830404
  145.2 5.4 %copy-start.1 = (bf16[1,1280,20,64]{1,3,2,0:T(8,128)(2,1)S(1)}, bf16[1,1280,20,64]{1,3,2,0:T(8,128)(2,1)}, u32[]{:S(2)}) copy-start(bf16[1,1280,20,64]{1,3,2,0:T(8,128)(2,1)} %get-tuple-element.26) | copy-start | bytes 9830404
  150.2 7.4 %collective-permute-start.3 = (bf16[1024,1280]{1,0:T(8,128)(2,1)}, bf16[1024,1280]{1,0:T(8,128)(2,1)}, u32[]{:S(2)}, u32[]{:S(2)}) collective-permute-start(bf16[1024,1280]{1,0:T(8,128)(2,1)} %convolution_convert_fusion.1.k0_ref.k0n_ref), channel_id=1, source_target_pairs={{0,1},{1,0},{2,3},{3,2},{4,5},{5,4},{6,7},{7,6},{8,9},{9,8},{10,11... | collective-permute-start | bytes 7864328 | tf_op jit(solution)/shard_map/ppermute | solution.py:21
  150.3 8.4 %collective-permute-start.4 = (bf16[1024,1280]{1,0:T(8,128)(2,1)}, bf16[1024,1280]{1,0:T(8,128)(2,1)}, u32[]{:S(2)}, u32[]{:S(2)}) collective-permute-start(bf16[1024,1280]{1,0:T(8,128)(2,1)} %convolution_convert_fusion.v0_ref), channel_id=1, source_target_pairs={{0,1},{1,0},{2,3},{3,2},{4,5},{5,4},{6,7},{7,6},{8,9},{9,8},{10,11... | collective-permute-start | bytes 7864328 | tf_op jit(solution)/shard_map/ppermute | solution.py:21
  157.5 51.2 %copy-start.4 = (bf16[16,64,1280]{2,1,0:T(8,128)(2,1)S(1)}, bf16[16,64,1280]{2,1,0:T(8,128)(2,1)}, u32[]{:S(2)}) copy-start(bf16[16,64,1280]{2,1,0:T(8,128)(2,1)} %get-tuple-element.18) | copy-start | bytes 7864324
  215.1 1.5 copy-start
  216.7 1.5 collective-permute-start.5
  217.0 1.3 copy-start.9
  217.0 1.2 collective-permute-start.6
  218.3 0.6 copy-start.11
  218.3 0.6 copy-start.7
  257.6 1.5 collective-permute-start.7
  257.9 1.2 collective-permute-start.8
  259.1 0.6 copy-start.12
  259.1 0.6 copy-start.8

commit v5 on v4

--- a/solution.py
+++ b/solution.py
@@ -39,7 +39,7 @@
 
 
 def silu(v):
-    return v / (1.0 + jnp.exp(-v))
+    return v * lax.logistic(v)
 
 
 def fill_act(core, h_ref, other_ref, norm_ref, act):
@@ -142,9 +142,9 @@
     )(h, other, own, theirs, scale, shift, w, add)
 
 
-def conv_in_kernel(x_ref, scale_ref, shift_ref, add_ref, w_ref, out_ref, half_ref, sums_ref, edge_ref,
-                   tile, raw, beside, weights, act, acc, stats, heard, norm_ref,
-                   tile_sem, w_sem, send_sem, recv_sem, self_sem, tell_sem, hear_sem, lend_sem, borrow_sem, keep_sem):
+def conv_in_kernel(x_ref, scale_ref, shift_ref, time_ref, tw_ref, w_ref, out_ref, half_ref, sums_ref, edge_ref, later_ref,
+                   tile, raw, beside, weights, tweights, times, act, acc, stats, heard, norm_ref,
+                   tile_sem, w_sem, send_sem, recv_sem, self_sem, tell_sem, hear_sem, lend_sem, borrow_sem, keep_sem, time_sem):
     images, trows, tcols, channels = x_ref.shape
     chunks, rows, cols, width = raw.shape
     sp, z = lax.axis_index(SP), lax.axis_index(SP2)
@@ -173,7 +173,7 @@
     def send(c, i):
         return pltpu.make_async_remote_copy(
             src_ref=x_ref.at[i, :, :, lanes(c)], dst_ref=piece(c, sp, z), send_sem=send_sem.at[c, i], recv_sem=recv_sem.at[c, sp * 2 + lax.rem(z, 2)],
-            device_id={SP: (i // 4) * 2 + to_core, SP2: i % 4}, device_id_type=MESH)
+            device_id={SP: (i // 4) * 2 + to_core, SP2: lax.rem(i, 4)}, device_id_type=MESH)
 
     def place_own(c):
         return pltpu.make_async_copy(x_ref.at[mine, :, :, lanes(c)], piece(c, sp, z), self_sem.at[c])
@@ -182,7 +182,10 @@
         return own & (mine == i)
 
     def start_chunk(c):
-        for i in range(images):
+        for far, near in ((0, 2), (1, 3), (1, 2), (0, 3), (0, 1), (1, 1), (1, 0), (0, 0)):
+            to_z = (lax.rem(z + 2, 4), 3 - z)[near - 2] if near > 1 else (z + 1 - 2 * lax.rem(z, 2) if near else z)
+            i = lax.rem(y + far, 2) * 4 + to_z
+
             @pl.when(jnp.logical_not(is_self(i)))
             def _():
                 send(c, i).start()
@@ -198,6 +201,8 @@
 
     pl.semaphore_wait(barrier, 15)
     start_chunk(0)
+    time_load = pltpu.make_async_copy(tw_ref, tweights, time_sem)
+    time_load.start()
     for c in range(chunks):
         weight(c).start()
     load.wait()
@@ -227,6 +232,11 @@
     count = 2 * rows * cols * (channels // GROUPS)
     norm_ref[...] = group_rows(total, scale_ref[0:1, :], shift_ref[0:1, :], count)
     acc[...] = jnp.zeros_like(acc)
+    time_load.wait()
+    time_act = silu(time_ref[...].astype(jnp.float32)).astype(jnp.bfloat16)
+    for s in range(2):
+        times[s] = jnp.dot(time_act, tweights[s], preferred_element_type=jnp.float32)
+    later_ref[...] = times[1, pl.ds(mine, 1), :]
     zeros = jnp.zeros((cols, width), jnp.bfloat16)
     for dx in range(3):
         act[dx, 0] = zeros
@@ -297,7 +307,7 @@
     lax.fori_loop(0, chunks, one_chunk, 0)
     for n in range(chunks):
         cut = slice(n * width, (n + 1) * width)
-        half = (acc[n] + add_ref[:, cut]).astype(jnp.bfloat16)
+        half = (acc[n] + times[0, pl.ds(mine, 1), cut]).astype(jnp.bfloat16)
         out_ref[:, :, cut] = half.reshape(rows, cols, width)
         kept = half.astype(jnp.float32)
         sums_ref[:, cut] = jnp.concatenate([jnp.sum(kept, axis=0, keepdims=True), jnp.sum(kept * kept, axis=0, keepdims=True)], axis=0)
@@ -328,7 +338,7 @@
                 tell(i, k).wait_send()
 
 
-def conv_in(x, scale, shift, add, w, width=256, band=16):
+def conv_in(x, scale, shift, time_emb, time_w, w, width=256, band=16):
     images, trows, tcols, channels = x.shape
     rows, cols, chunks = 4 * trows, 2 * tcols, channels // width
     vmem, hbm = pl.BlockSpec(memory_space=pltpu.VMEM), pl.BlockSpec(memory_space=pl.ANY)
@@ -336,18 +346,18 @@
     shape = jax.ShapeDtypeStruct
     return pl.pallas_call(
         conv_in_kernel,
-        in_specs=[hbm, vmem, vmem, vmem, hbm],
-        out_specs=[vmem, hbm, vmem, vmem],
-        out_shape=[shape((rows, cols, channels), jnp.bfloat16), shape((rows, cols, channels), jnp.bfloat16), shape((2, channels), jnp.float32), shape((rows, 1, channels), jnp.bfloat16)],
+        in_specs=[hbm, vmem, vmem, vmem, hbm, hbm],
+        out_specs=[vmem, hbm, vmem, vmem, vmem],
+        out_shape=[shape((rows, cols, channels), jnp.bfloat16), shape((rows, cols, channels), jnp.bfloat16), shape((2, channels), jnp.float32), shape((rows, 1, channels), jnp.bfloat16), shape((1, channels), jnp.float32)],
         scratch_shapes=[
             pltpu.VMEM(x.shape, jnp.bfloat16), pltpu.VMEM((chunks, rows, cols, width), jnp.bfloat16), pltpu.VMEM((chunks, rows, band, width), jnp.bfloat16),
-            pltpu.VMEM((chunks, 3, 3, width, channels), jnp.bfloat16), pltpu.VMEM((3, rows + 2, cols, width), jnp.bfloat16), pltpu.VMEM((chunks, rows * cols, width), jnp.float32),
+            pltpu.VMEM((chunks, 3, 3, width, channels), jnp.bfloat16), pltpu.VMEM(time_w.shape, jnp.bfloat16), pltpu.VMEM((2, images, channels), jnp.float32), pltpu.VMEM((3, rows + 2, cols, width), jnp.bfloat16), pltpu.VMEM((chunks, rows * cols, width), jnp.float32),
             pltpu.VMEM((images, 2, channels), jnp.float32), pltpu.VMEM((16, 2, channels), jnp.float32), pltpu.VMEM((3, channels), jnp.float32),
-            dma, dma((chunks,)), dma((chunks, 8)), dma((chunks, 8)), dma((chunks,)), dma((8, 2)), dma((16,)), dma((chunks,)), dma((chunks,)), dma((chunks,))],
+            dma, dma((chunks,)), dma((chunks, 8)), dma((chunks, 8)), dma((chunks,)), dma((8, 2)), dma((16,)), dma((chunks,)), dma((chunks,)), dma((chunks,)), dma],
         compiler_params=pltpu.CompilerParams(collective_id=0, has_side_effects=True, vmem_limit_bytes=63 * 1024 * 1024),
         cost_estimate=conv_cost(rows, cols, channels),
         name="conv_in",
-    )(x, scale, shift, add, w)
+    )(x, scale, shift, time_emb, time_w, w)
 
 
 def conv_out_kernel(norm_idx, j, h_ref, other_ref, own_ref, theirs_ref, scale_ref, shift_ref, w_ref, add_ref, out_ref, act, norm_ref, wbuf, done, w_sem, send_sem, recv_sem, self_sem):
@@ -382,7 +392,7 @@
         return done.at[c, pl.ds(dst_sp * trows, trows), pl.ds(pl.multiple_of(lax.rem(dst_z, 2) * tcols, tcols), tcols), :]
 
     def send(c, s):
-        dst_sp, dst_z = s // 2, 2 * core + s % 2
+        dst_sp, dst_z = s // 2, 2 * core + lax.rem(s, 2)
         return pltpu.make_async_remote_copy(
             src_ref=piece(c, dst_sp, dst_z), dst_ref=out_ref.at[mine, :, :, lanes(c)], send_sem=send_sem.at[c, s], recv_sem=recv_sem.at[c, mine],
             device_id={SP: dst_sp, SP2: dst_z}, device_id_type=MESH)
@@ -391,22 +401,21 @@
         return pltpu.make_async_copy(piece(c, sp, z), out_ref.at[mine, :, :, lanes(c)], self_sem.at[c])
 
     def is_self(s):
-        return (s // 2 == sp) & (2 * core + s % 2 == z)
+        return (s // 2 == sp) & (2 * core + lax.rem(s, 2) == z)
 
     @pl.when(n + 1 < chunks)
     def _():
         fetch(w_ref, wbuf, w_sem, j, n + 1).start()
 
     fetch(w_ref, wbuf, w_sem, j, n).wait()
-    part = rows // 2
-    for m in range(2):
-        span = slice(m * part, (m + 1) * part)
-        full = taps(act, wbuf, lax.rem(n, 2), m * part, part, cols, channels) + add_ref[span].reshape(part * cols, width).astype(jnp.float32)
-        done[n, span] = full.astype(jnp.bfloat16).reshape(part, cols, width)
-        for s in range(4 * m, 4 * m + 4):
-            @pl.when(jnp.logical_not(is_self(s)))
-            def _():
-                send(n, s).start()
+    full = taps(act, wbuf, lax.rem(n, 2), 0, rows, cols, channels) + add_ref[...].reshape(rows * cols, width).astype(jnp.float32)
+    done[n] = full.astype(jnp.bfloat16).reshape(rows, cols, width)
+    for k in range(8):
+        s = (lax.rem(y + k, 2) * 2 + (k // 2) % 2) * 2 + lax.rem(z + k // 4, 2)
+
+        @pl.when(jnp.logical_not(is_self(s)))
+        def _():
+            send(n, s).start()
 
     @pl.when(own)
     def _():
@@ -571,17 +580,13 @@
     lat_spec = P("dp", "sp", "sp2", None)
 
     def local(x, time_emb, gn_scale, gn_shift, conv_w, time_w, w_qkv, w_out):
-        y, core = place(lax.axis_index(SP))
-        image = y * 4 + lax.axis_index(SP2)
-        time_act = jax.nn.silu(time_emb.astype(jnp.float32)).astype(jnp.bfloat16)
-        time_vecs = jnp.einsum("bt,stc->sbc", time_act, time_w, preferred_element_type=jnp.float32)
-        time_vecs = lax.dynamic_index_in_dim(time_vecs, image, 1, keepdims=False)
+        _, core = place(lax.axis_index(SP))
         norms = gn_scale, gn_shift
-        hidden, half, sums, edge = conv_in(x, gn_scale, gn_shift, time_vecs[0][None], conv_w)
+        hidden, half, sums, edge, time_vec = conv_in(x, gn_scale, gn_shift, time_emb, time_w, conv_w)
         first, sums, _ = conv(hidden, swap_cores(edge), sums, swap_cores(sums), *norms, 1, conv_w, 1, half)
         middle = attention_block(first, sums, gn_scale[2], gn_shift[2], w_qkv, w_out)
         sums, edge = channel_sums(middle), edge_of(middle, core)
-        hidden, sums, edge = conv(middle, swap_cores(edge), sums, swap_cores(sums), *norms, 3, conv_w, 2, time_vecs[1][None])
+        hidden, sums, edge = conv(middle, swap_cores(edge), sums, swap_cores(sums), *norms, 3, conv_w, 2, time_vec)
         return conv_out(hidden, swap_cores(edge), sums, swap_cores(sums), *norms, 4, conv_w, 3, middle)
 
     return jax.shard_map(local, mesh=mesh, in_specs=(lat_spec, P("dp", None), P(), P(), P(), P(), P(), P()), out_specs=lat_spec, check_vma=False)

time: 342 us -> 330 us (0.965)
  Pallas kernels: 287 us -> 276 us
  matrix products: 26.9 us -> 23.1 us
    pallas_call x1, Pallas kernels: 76.7 us -> 71.1 us  [conv_out(): pl.pallas_call(functools.partial(conv_out_kernel, norm_idx, j), grid=(chu...]
    pallas_call x1, Pallas kernels: 83.1 us -> 79.1 us  [conv_in(): pl.pallas_call(conv_in_kernel, in_specs=[hbm, vmem, vmem, vmem, hbm, hbm]...]
    dot_general x1 -> x0, matrix products: 3.83 us -> none  [local(): jnp.einsum('bt,stc->sbc', time_act, time_w, preferred_element_type=jnp.fl...]
where the time goes in v5:
time: 330 us; the launch traced here: 326 us
  Pallas kernels  276 us (84%)
  matrix products  23.1 us (7%)
  local copies, waits for them, and re-layouts  15.1 us (5%)
  other arithmetic  4.26 us (1%)
  starting transfers between devices  3.62 us (1%)
    pallas_call x1, Pallas kernels, conv_in(): pl.pallas_call(conv_in_kernel, in_specs=[hbm, vmem, vmem, vmem, hbm, hbm]...  79.1 us
    pallas_call x2, Pallas kernels, conv(): pl.pallas_call(functools.partial(conv_kernel, add.ndim == 3, norm_idx, j)...  76.1 us
    pallas_call x1, Pallas kernels, conv_out(): pl.pallas_call(functools.partial(conv_out_kernel, norm_idx, j), grid=(chu...  71.1 us
    pallas_call x1, Pallas kernels, attend(): pl.pallas_call(functools.partial(attend_kernel, block, chunk), grid=(pair...  49.9 us
    dot_general x3, matrix products, project(): jnp.dot(normed, weight, preferred_element_type=jnp.float32)  16.7 us
    slice x1, local copies, waits for them, and re-layouts, attention_block(): keys, vals = (project(flat[1]), project(flat[2]))  7.09 us
    unnamed x27, local copies, waits for them, and re-layouts  6.8 us
  transfers between devices with their start and end apart: 9, of which 4 were waited for; matrix products, arithmetic and copies ran while one was open for 5% of the time, Pallas kernels for 0%

profile of v5, /device:TPU:31, one launch (start us, length us, event | category | flops | bytes accessed | tf_op | source)
XLA Modules:
  0.0 325.8 jit_solution(1067697888900526754)
XLA Ops:
  0.0 79.1 %conv_in.1 = (bf16[16,64,1280]{2,1,0:T(8,128)(2,1)}, bf16[16,64,1280]{2,1,0:T(8,128)(2,1)}, f32[2,1280]{1,0:T(2,128)}, bf16[16,1,1280]{2,1,0:T(2,128)(2,1)}, f32[1,1280]{1,0:T(1,128)}) custom-call(bf16[8,4,32,1280]{3,2,1,0:T(8,128)(2,1)} %x_ref.1, bf16[5,1280]{1,0:T(8,128)(2,1)} %scale_ref.7, bf16[5,1280]{1,0:T(8,128)(2,1)} %shift_ref.7, ...), custom_call_target="tpu_custom_call" | custom-call | flops 30198988800 | bytes 29491200 | tf_op jit(solution)/shard_map/conv_in/pallas_call | solution.py:347
  79.1 1.4 collective-permute-start.1
  80.5 0.1 collective-permute-start
  80.6 7.1 %fusion.7 = (bf16[1,1280,20,64]{1,3,2,0:T(8,128)(2,1)}, bf16[1,1280,20,64]{1,3,2,0:T(8,128)(2,1)}, bf16[1,1280,20,64]{1,3,2,0:T(8,128)(2,1)}) fusion(bf16[3,1280,20,64]{1,3,2,0:T(8,128)(2,1)} %param.14), kind=kLoop, calls=%fused_computation.21 | loop fusion | bytes 19660800 | tf_op jit(solution)/shard_map/slice | solution.py:571
  87.6 0.7 convert_reduce_fusion.2
  88.4 0.0 collective-permute-done.1.theirs_ref
  88.4 0.0 copy-start.10
  88.4 0.0 collective-permute-done.other_ref
  88.4 0.0 copy-start.6
  88.4 0.6 copy-done.10
  89.0 0.1 copy-done.6
  89.1 38.0 %conv.2 = (bf16[16,64,1280]{2,1,0:T(8,128)(2,1)}, f32[2,1280]{1,0:T(2,128)}, bf16[16,1,1280]{2,1,0:T(2,128)(2,1)}) custom-call(bf16[16,64,1280]{2,1,0:T(8,128)(2,1)} %get-tuple-element.15.h_ref, bf16[16,1,1280]{2,1,0:T(2,128)(2,1)} %copy-done.6, f32[2,1280]{1,0:T(2,128)} %get-tuple-element.17.own_ref, f32[2,1280]{1,0:T(2,128)} %copy-done.10, ...), custom_call_target="tpu_custom_call" | custom-call | flops 30198988800 | bytes 29491200 | tf_op jit(solution)/shard_map/conv/pallas_call | solution.py:132
  127.0 0.0 copy-start.3
  127.0 0.9 reshape.41
  128.0 0.1 reduce_sum.27
  128.1 0.4 collective-permute-start.2
  128.5 0.7 convert_reduce_fusion.1
  129.2 0.1 collective-permute-done.2
  129.3 0.1 broadcast_in_dim.6
  129.4 0.1 sub.13
  129.5 0.1 broadcast_in_dim.7
  129.6 0.1 reshape.42
  129.7 2.5 fusion.2
  132.2 0.0 copy-start.5
  132.2 0.0 copy-done.3
  132.2 0.0 copy-start.2
  132.2 5.0 %convolution_convert_fusion.v0_ref = bf16[1024,1280]{1,0:T(8,128)(2,1)} fusion(bf16[1024,1280]{1,0:T(8,128)(2,1)S(1)} %bitcast.29, bf16[1280,1280]{0,1:T(8,128)(2,1)S(1)} %bitcast.28), kind=kOutput, calls=%fused_computation.9 | convolution fusion | flops 3356753920 | bytes 8519680 | tf_op jit(solution)/shard_map/dot_general | solution.py:569
  137.2 0.0 copy-done.5
  137.2 0.0 copy-done.2
  137.2 0.0 copy-start.1
  137.2 4.9 %convolution_convert_fusion.1.k0_ref.k0n_ref = bf16[1024,1280]{1,0:T(8,128)(2,1)} fusion(bf16[1024,1280]{1,0:T(8,128)(2,1)S(1)} %bitcast.30, bf16[1280,1280]{0,1:T(8,128)(2,1)S(1)} %bitcast.27), kind=kOutput, calls=%fused_computation.10 | convolution fusion | flops 3356753920 | bytes 8519680 | tf_op jit(solution)/shard_map/dot_general | solution.py:569
  142.1 0.3 collective-permute-start.3
  142.4 0.2 collective-permute-start.4
  142.6 0.0 copy-done.1
  142.6 6.8 %convolution_convert_fusion.2.q_ref.qn_ref = bf16[1024,1280]{1,0:T(8,128)(2,1)} fusion(bf16[1024,1280]{1,0:T(8,128)(2,1)} %bitcast.31, bf16[1280,1280]{0,1:T(8,128)(2,1)S(1)} %bitcast.26), kind=kOutput, calls=%fused_computation.11 | convolution fusion | flops 3356753920 | bytes 8519680 | tf_op jit(solution)/shard_map/dot_general | solution.py:569
  149.5 0.0 copy-start.4
  149.5 0.0 collective-permute-done.3.k1_ref.k1n_ref
  149.5 1.3 collective-permute-done.4.v1_ref
  150.7 49.9 %attend.1 = bf16[1024,1280]{1,0:T(8,128)(2,1)} custom-call(bf16[1024,1280]{1,0:T(8,128)(2,1)} %convolution_convert_fusion.2.q_ref.qn_ref, bf16[1024,1280]{1,0:T(8,128)(2,1)} %convolution_convert_fusion.1.k0_ref.k0n_ref, bf16[1024,1280]{1,0:T(8,128)(2,1)} %collective-permute-done.3.k1_ref.k1n_ref, bf16[1024,1280]{1,0:T(8,128)(2,1)} %convolution_convert_fusion.v0_ref, ...), custom_call_target="tpu_custom_call" | custom-call | flops 42949672960 | bytes 13107200 | tf_op jit(solution)/shard_map/attend/pallas_call | solution.py:531
  200.6 0.0 copy-done.4
  200.7 6.4 %convert_reduce_fusion = (f32[1280]{0:T(1024)S(1)}, f32[1280]{0:T(1024)S(1)}, bf16[16,64,1280]{2,1,0:T(8,128)(2,1)S(1)}) fusion(bf16[16,64,1280]{2,1,0:T(8,128)(2,1)} %bitcast.33, bf16[1280,1280,1]{1,0,2:T(8,128)(2,1)} %bitcast.32, bf16[16,64,1280]{2,1,0:T(8,128)(2,1)S(1)} %copy-done.4), kind=kOutput, calls=%fused_computation.1 | convolution fusion | flops 3364615680 | bytes 11151360 | tf_op jit(solution)/shard_map/dot_general | solution.py:575
  207.1 0.0 copy-start
  207.1 1.5 copy-done
  208.6 0.1 broadcast_select_fusion
  208.7 0.4 collective-permute-start.5
  209.1 0.0 copy-start.9
  209.1 0.2 collective-permute-start.6
  209.4 1.0 collective-permute-done.6.theirs_ref
  210.4 0.0 copy-start.11
  210.4 0.0 collective-permute-done.5.other_ref
  210.4 0.0 copy-start.7
  210.4 0.0 copy-done.9
  210.4 0.6 copy-done.11
  211.0 0.0 copy-done.7
  211.0 38.1 %conv.3 = (bf16[16,64,1280]{2,1,0:T(8,128)(2,1)}, f32[2,1280]{1,0:T(2,128)}, bf16[16,1,1280]{2,1,0:T(2,128)(2,1)}) custom-call(bf16[16,64,1280]{2,1,0:T(8,128)(2,1)} %copy-done, bf16[16,1,1280]{2,1,0:T(2,128)(2,1)} %copy-done.7, f32[2,1280]{1,0:T(2,128)} %copy-done.9, f32[2,1280]{1,0:T(2,128)} %copy-done.11, bf16[5,1280]{1,0:T(8,128)(2,1)} %scale_ref.7, ...), custom_call_target="tpu_custom_call" | custom-call | flops 30198988800 | bytes 29491200 | tf_op jit(solution)/shard_map/conv/pallas_call | solution.py:132
  249.1 0.2 collective-permute-start.7
  249.4 0.4 collective-permute-start.8
  249.7 0.8 collective-permute-done.8.theirs_ref
  250.6 0.0 copy-start.12
  250.6 0.0 collective-permute-done.7.other_ref
  250.6 0.6 copy-done.12
  251.2 0.0 copy-done.8
  251.2 71.1 %conv_out.1 = bf16[8,4,32,1280]{3,2,1,0:T(8,128)(2,1)} custom-call(bf16[16,64,1280]{2,1,0:T(8,128)(2,1)} %get-tuple-element.22.h_ref, bf16[16,1,1280]{2,1,0:T(2,128)(2,1)} %copy-done.8, f32[2,1280]{1,0:T(2,128)} %get-tuple-element.24.own_ref, f32[2,1280]{1,0:T(2,128)} %copy-done.12, bf16[5,1280]{1,0:T(8,128)(2,1)} %scale_ref.7, bf16[5,1280]{1,0:T(8,128)(2,1)} %shift_ref.7, ...), custom_call_target="tpu_custom_call" | custom-call | flops 30198988800 | bytes 29491200 | tf_op jit(solution)/shard_map/conv_out/pallas_call | solution.py:450
  322.3 3.4 %copy.10 = bf16[8,4,32,1280]{3,2,1,0:T(8,128)(2,1)} copy(bf16[8,4,32,1280]{3,2,1,0:T(8,128)(2,1)} %conv_out.1) | data formatting | bytes 5242880
  (8 shorter events, 0.0 us)
Async XLA Ops:
  79.1 9.3 %collective-permute-start.1 = (f32[2,1280]{1,0:T(2,128)}, f32[2,1280]{1,0:T(2,128)S(1)}, u32[]{:S(2)}, u32[]{:S(2)}) collective-permute-start(f32[2,1280]{1,0:T(2,128)} %get-tuple-element.17.own_ref), channel_id=1, source_target_pairs={{0,1},{1,0},{2,3},{3,2},{4,5},{5,4},{6,7},{7,6},{8,9},{9,8},{10,11... | collective-permute-start | bytes 30728 | tf_op jit(solution)/shard_map/ppermute | solution.py:21
  80.5 7.9 %collective-permute-start = (bf16[16,1,1280]{2,1,0:T(2,128)(2,1)}, bf16[16,1,1280]{2,1,0:T(2,128)(2,1)S(1)}, u32[]{:S(2)}, u32[]{:S(2)}) collective-permute-start(bf16[16,1,1280]{2,1,0:T(2,128)(2,1)} %get-tuple-element.16), channel_id=1, source_target_pairs={{0,1},{1,0},{2,3},{3,2},{4,5},{5,4},{6,7},{7,6},{8,9},{9,8},{10,11... | collective-permute-start | bytes 122888 | tf_op jit(solution)/shard_map/ppermute | solution.py:21
  88.4 0.6 copy-start.10
  88.4 0.6 copy-start.6
  127.0 5.2 %copy-start.3 = (bf16[1,1280,20,64]{1,3,2,0:T(8,128)(2,1)S(1)}, bf16[1,1280,20,64]{1,3,2,0:T(8,128)(2,1)}, u32[]{:S(2)}) copy-start(bf16[1,1280,20,64]{1,3,2,0:T(8,128)(2,1)} %get-tuple-element.27) | copy-start | bytes 9830404
  128.1 1.2 collective-permute-start.2
  132.2 5.0 %copy-start.5 = (bf16[16,64,1280]{2,1,0:T(8,128)(2,1)}, bf16[16,64,1280]{2,1,0:T(8,128)(2,1)S(1)}, u32[]{:S(2)}) copy-start(bf16[16,64,1280]{2,1,0:T(8,128)(2,1)S(1)} %fusion.2) | copy-start | bytes 7864324
  132.2 5.0 %copy-start.2 = (bf16[1,1280,20,64]{1,3,2,0:T(8,128)(2,1)S(1)}, bf16[1,1280,20,64]{1,3,2,0:T(8,128)(2,1)}, u32[]{:S(2)}) copy-start(bf16[1,1280,20,64]{1,3,2,0:T(8,128)(2,1)} %get-tuple-element.29) | copy-start | bytes 9830404
  137.2 5.4 %copy-start.1 = (bf16[1,1280,20,64]{1,3,2,0:T(8,128)(2,1)S(1)}, bf16[1,1280,20,64]{1,3,2,0:T(8,128)(2,1)}, u32[]{:S(2)}) copy-start(bf16[1,1280,20,64]{1,3,2,0:T(8,128)(2,1)} %get-tuple-element.28) | copy-start | bytes 9830404
  142.1 7.4 %collective-permute-start.3 = (bf16[1024,1280]{1,0:T(8,128)(2,1)}, bf16[1024,1280]{1,0:T(8,128)(2,1)}, u32[]{:S(2)}, u32[]{:S(2)}) collective-permute-start(bf16[1024,1280]{1,0:T(8,128)(2,1)} %convolution_convert_fusion.1.k0_ref.k0n_ref), channel_id=1, source_target_pairs={{0,1},{1,0},{2,3},{3,2},{4,5},{5,4},{6,7},{7,6},{8,9},{9,8},{10,11... | collective-permute-start | bytes 7864328 | tf_op jit(solution)/shard_map/ppermute | solution.py:21
  142.4 8.3 %collective-permute-start.4 = (bf16[1024,1280]{1,0:T(8,128)(2,1)}, bf16[1024,1280]{1,0:T(8,128)(2,1)}, u32[]{:S(2)}, u32[]{:S(2)}) collective-permute-start(bf16[1024,1280]{1,0:T(8,128)(2,1)} %convolution_convert_fusion.v0_ref), channel_id=1, source_target_pairs={{0,1},{1,0},{2,3},{3,2},{4,5},{5,4},{6,7},{7,6},{8,9},{9,8},{10,11... | collective-permute-start | bytes 7864328 | tf_op jit(solution)/shard_map/ppermute | solution.py:21
  149.5 51.2 %copy-start.4 = (bf16[16,64,1280]{2,1,0:T(8,128)(2,1)S(1)}, bf16[16,64,1280]{2,1,0:T(8,128)(2,1)}, u32[]{:S(2)}) copy-start(bf16[16,64,1280]{2,1,0:T(8,128)(2,1)} %get-tuple-element.19) | copy-start | bytes 7864324
  207.1 1.5 copy-start
  208.7 1.7 collective-permute-start.5
  209.1 1.3 copy-start.9
  209.1 1.2 collective-permute-start.6
  210.4 0.6 copy-start.11
  210.4 0.6 copy-start.7
  249.1 1.4 collective-permute-start.7
  249.4 1.2 collective-permute-start.8
  250.6 0.6 copy-start.12
  250.6 0.6 copy-start.8

commit v6 on v5

--- a/solution.py
+++ b/solution.py
@@ -172,7 +172,7 @@
 
     def send(c, i):
         return pltpu.make_async_remote_copy(
-            src_ref=x_ref.at[i, :, :, lanes(c)], dst_ref=piece(c, sp, z), send_sem=send_sem.at[c, i], recv_sem=recv_sem.at[c, sp * 2 + lax.rem(z, 2)],
+            src_ref=tile.at[i, :, :, lanes(c)], dst_ref=piece(c, sp, z), send_sem=send_sem.at[c, i], recv_sem=recv_sem.at[c, sp * 2 + lax.rem(z, 2)],
             device_id={SP: (i // 4) * 2 + to_core, SP2: lax.rem(i, 4)}, device_id_type=MESH)
 
     def place_own(c):
@@ -199,13 +199,13 @@
             src_ref=stats.at[i], dst_ref=heard.at[me], send_sem=tell_sem.at[i, k], recv_sem=hear_sem.at[me],
             device_id={SP: (i // 4) * 2 + k, SP2: i % 4}, device_id_type=MESH)
 
+    load.wait()
     pl.semaphore_wait(barrier, 15)
     start_chunk(0)
     time_load = pltpu.make_async_copy(tw_ref, tweights, time_sem)
     time_load.start()
     for c in range(chunks):
         weight(c).start()
-    load.wait()
 
     def sum_image(i, carry):
         wide = tile[i].reshape(trows * tcols, channels).astype(jnp.float32)

time: 330 us -> 331 us (level)
  no operation moved by 1% of the time
where the time goes in v6:
time: 331 us; the launch traced here: 325 us
  Pallas kernels  276 us (83%)
  matrix products  23.1 us (7%)
  local copies, waits for them, and re-layouts  15.1 us (5%)
  other arithmetic  4.26 us (1%)
  starting transfers between devices  3.62 us (1%)
    pallas_call x1, Pallas kernels, conv_in(): pl.pallas_call(conv_in_kernel, in_specs=[hbm, vmem, vmem, vmem, hbm, hbm]...  79.6 us
    pallas_call x2, Pallas kernels, conv(): pl.pallas_call(functools.partial(conv_kernel, add.ndim == 3, norm_idx, j)...  76.1 us
    pallas_call x1, Pallas kernels, conv_out(): pl.pallas_call(functools.partial(conv_out_kernel, norm_idx, j), grid=(chu...  70.2 us
    pallas_call x1, Pallas kernels, attend(): pl.pallas_call(functools.partial(attend_kernel, block, chunk), grid=(pair...  49.9 us
    dot_general x3, matrix products, project(): jnp.dot(normed, weight, preferred_element_type=jnp.float32)  16.7 us
    slice x1, local copies, waits for them, and re-layouts, attention_block(): keys, vals = (project(flat[1]), project(flat[2]))  7.09 us
    unnamed x27, local copies, waits for them, and re-layouts  6.8 us
  transfers between devices with their start and end apart: 9, of which 4 were waited for; matrix products, arithmetic and copies ran while one was open for 5% of the time, Pallas kernels for 0%

profile of v6, /device:TPU:31, one launch (start us, length us, event | category | flops | bytes accessed | tf_op | source)
XLA Modules:
  0.0 325.4 jit_solution(13519771876307350148)
XLA Ops:
  0.0 79.6 %conv_in.1 = (bf16[16,64,1280]{2,1,0:T(8,128)(2,1)}, bf16[16,64,1280]{2,1,0:T(8,128)(2,1)}, f32[2,1280]{1,0:T(2,128)}, bf16[16,1,1280]{2,1,0:T(2,128)(2,1)}, f32[1,1280]{1,0:T(1,128)}) custom-call(bf16[8,4,32,1280]{3,2,1,0:T(8,128)(2,1)} %x_ref.1, bf16[5,1280]{1,0:T(8,128)(2,1)} %scale_ref.7, bf16[5,1280]{1,0:T(8,128)(2,1)} %shift_ref.7, ...), custom_call_target="tpu_custom_call" | custom-call | flops 30198988800 | bytes 29491200 | tf_op jit(solution)/shard_map/conv_in/pallas_call | solution.py:347
  79.6 1.4 collective-permute-start.1
  81.0 0.1 collective-permute-start
  81.1 7.1 %fusion.7 = (bf16[1,1280,20,64]{1,3,2,0:T(8,128)(2,1)}, bf16[1,1280,20,64]{1,3,2,0:T(8,128)(2,1)}, bf16[1,1280,20,64]{1,3,2,0:T(8,128)(2,1)}) fusion(bf16[3,1280,20,64]{1,3,2,0:T(8,128)(2,1)} %param.14), kind=kLoop, calls=%fused_computation.21 | loop fusion | bytes 19660800 | tf_op jit(solution)/shard_map/slice | solution.py:571
  88.2 0.7 convert_reduce_fusion.2
  89.0 0.0 collective-permute-done.1.theirs_ref
  89.0 0.0 copy-start.10
  89.0 0.0 collective-permute-done.other_ref
  89.0 0.0 copy-start.6
  89.0 0.6 copy-done.10
  89.6 0.1 copy-done.6
  89.6 38.0 %conv.2 = (bf16[16,64,1280]{2,1,0:T(8,128)(2,1)}, f32[2,1280]{1,0:T(2,128)}, bf16[16,1,1280]{2,1,0:T(2,128)(2,1)}) custom-call(bf16[16,64,1280]{2,1,0:T(8,128)(2,1)} %get-tuple-element.15.h_ref, bf16[16,1,1280]{2,1,0:T(2,128)(2,1)} %copy-done.6, f32[2,1280]{1,0:T(2,128)} %get-tuple-element.17.own_ref, f32[2,1280]{1,0:T(2,128)} %copy-done.10, ...), custom_call_target="tpu_custom_call" | custom-call | flops 30198988800 | bytes 29491200 | tf_op jit(solution)/shard_map/conv/pallas_call | solution.py:132
  127.6 0.0 copy-start.3
  127.6 0.9 reshape.41
  128.5 0.1 reduce_sum.27
  128.6 0.4 collective-permute-start.2
  129.0 0.7 convert_reduce_fusion.1
  129.8 0.1 collective-permute-done.2
  129.9 0.1 broadcast_in_dim.6
  130.0 0.1 sub.13
  130.1 0.1 broadcast_in_dim.7
  130.1 0.1 reshape.42
  130.2 2.5 fusion.2
  132.7 0.0 copy-start.5
  132.8 0.0 copy-done.3
  132.8 0.0 copy-start.2
  132.8 4.9 %convolution_convert_fusion.v0_ref = bf16[1024,1280]{1,0:T(8,128)(2,1)} fusion(bf16[1024,1280]{1,0:T(8,128)(2,1)S(1)} %bitcast.29, bf16[1280,1280]{0,1:T(8,128)(2,1)S(1)} %bitcast.28), kind=kOutput, calls=%fused_computation.9 | convolution fusion | flops 3356753920 | bytes 8519680 | tf_op jit(solution)/shard_map/dot_general | solution.py:569
  137.7 0.0 copy-done.5
  137.7 0.0 copy-done.2
  137.7 0.0 copy-start.1
  137.7 4.9 %convolution_convert_fusion.1.k0_ref.k0n_ref = bf16[1024,1280]{1,0:T(8,128)(2,1)} fusion(bf16[1024,1280]{1,0:T(8,128)(2,1)S(1)} %bitcast.30, bf16[1280,1280]{0,1:T(8,128)(2,1)S(1)} %bitcast.27), kind=kOutput, calls=%fused_computation.10 | convolution fusion | flops 3356753920 | bytes 8519680 | tf_op jit(solution)/shard_map/dot_general | solution.py:569
  142.7 0.4 collective-permute-start.3
  143.0 0.2 collective-permute-start.4
  143.2 0.0 copy-done.1
  143.2 6.8 %convolution_convert_fusion.2.q_ref.qn_ref = bf16[1024,1280]{1,0:T(8,128)(2,1)} fusion(bf16[1024,1280]{1,0:T(8,128)(2,1)} %bitcast.31, bf16[1280,1280]{0,1:T(8,128)(2,1)S(1)} %bitcast.26), kind=kOutput, calls=%fused_computation.11 | convolution fusion | flops 3356753920 | bytes 8519680 | tf_op jit(solution)/shard_map/dot_general | solution.py:569
  150.0 0.0 copy-start.4
  150.0 0.0 collective-permute-done.3.k1_ref.k1n_ref
  150.0 1.3 collective-permute-done.4.v1_ref
  151.3 49.9 %attend.1 = bf16[1024,1280]{1,0:T(8,128)(2,1)} custom-call(bf16[1024,1280]{1,0:T(8,128)(2,1)} %convolution_convert_fusion.2.q_ref.qn_ref, bf16[1024,1280]{1,0:T(8,128)(2,1)} %convolution_convert_fusion.1.k0_ref.k0n_ref, bf16[1024,1280]{1,0:T(8,128)(2,1)} %collective-permute-done.3.k1_ref.k1n_ref, bf16[1024,1280]{1,0:T(8,128)(2,1)} %convolution_convert_fusion.v0_ref, ...), custom_call_target="tpu_custom_call" | custom-call | flops 42949672960 | bytes 13107200 | tf_op jit(solution)/shard_map/attend/pallas_call | solution.py:531
  201.3 0.0 copy-done.4
  201.3 6.4 %convert_reduce_fusion = (f32[1280]{0:T(1024)S(1)}, f32[1280]{0:T(1024)S(1)}, bf16[16,64,1280]{2,1,0:T(8,128)(2,1)S(1)}) fusion(bf16[16,64,1280]{2,1,0:T(8,128)(2,1)} %bitcast.33, bf16[1280,1280,1]{1,0,2:T(8,128)(2,1)} %bitcast.32, bf16[16,64,1280]{2,1,0:T(8,128)(2,1)S(1)} %copy-done.4), kind=kOutput, calls=%fused_computation.1 | convolution fusion | flops 3364615680 | bytes 11151360 | tf_op jit(solution)/shard_map/dot_general | solution.py:575
  207.7 0.0 copy-start
  207.7 1.5 copy-done
  209.2 0.1 broadcast_select_fusion
  209.3 0.4 collective-permute-start.5
  209.7 0.0 copy-start.9
  209.7 0.3 collective-permute-start.6
  210.0 1.0 collective-permute-done.6.theirs_ref
  211.0 0.0 copy-start.11
  211.0 0.0 collective-permute-done.5.other_ref
  211.0 0.0 copy-start.7
  211.0 0.0 copy-done.9
  211.0 0.6 copy-done.11
  211.5 0.0 copy-done.7
  211.6 38.1 %conv.3 = (bf16[16,64,1280]{2,1,0:T(8,128)(2,1)}, f32[2,1280]{1,0:T(2,128)}, bf16[16,1,1280]{2,1,0:T(2,128)(2,1)}) custom-call(bf16[16,64,1280]{2,1,0:T(8,128)(2,1)} %copy-done, bf16[16,1,1280]{2,1,0:T(2,128)(2,1)} %copy-done.7, f32[2,1280]{1,0:T(2,128)} %copy-done.9, f32[2,1280]{1,0:T(2,128)} %copy-done.11, bf16[5,1280]{1,0:T(8,128)(2,1)} %scale_ref.7, ...), custom_call_target="tpu_custom_call" | custom-call | flops 30198988800 | bytes 29491200 | tf_op jit(solution)/shard_map/conv/pallas_call | solution.py:132
  249.7 0.2 collective-permute-start.7
  250.0 0.3 collective-permute-start.8
  250.3 0.8 collective-permute-done.8.theirs_ref
  251.1 0.0 copy-start.12
  251.1 0.0 collective-permute-done.7.other_ref
  251.2 0.6 copy-done.12
  251.7 0.0 copy-done.8
  251.8 70.2 %conv_out.1 = bf16[8,4,32,1280]{3,2,1,0:T(8,128)(2,1)} custom-call(bf16[16,64,1280]{2,1,0:T(8,128)(2,1)} %get-tuple-element.22.h_ref, bf16[16,1,1280]{2,1,0:T(2,128)(2,1)} %copy-done.8, f32[2,1280]{1,0:T(2,128)} %get-tuple-element.24.own_ref, f32[2,1280]{1,0:T(2,128)} %copy-done.12, bf16[5,1280]{1,0:T(8,128)(2,1)} %scale_ref.7, bf16[5,1280]{1,0:T(8,128)(2,1)} %shift_ref.7, ...), custom_call_target="tpu_custom_call" | custom-call | flops 30198988800 | bytes 29491200 | tf_op jit(solution)/shard_map/conv_out/pallas_call | solution.py:450
  322.0 3.4 %copy.10 = bf16[8,4,32,1280]{3,2,1,0:T(8,128)(2,1)} copy(bf16[8,4,32,1280]{3,2,1,0:T(8,128)(2,1)} %conv_out.1) | data formatting | bytes 5242880
  (8 shorter events, 0.0 us)
Async XLA Ops:
  79.6 9.3 %collective-permute-start.1 = (f32[2,1280]{1,0:T(2,128)}, f32[2,1280]{1,0:T(2,128)S(1)}, u32[]{:S(2)}, u32[]{:S(2)}) collective-permute-start(f32[2,1280]{1,0:T(2,128)} %get-tuple-element.17.own_ref), channel_id=1, source_target_pairs={{0,1},{1,0},{2,3},{3,2},{4,5},{5,4},{6,7},{7,6},{8,9},{9,8},{10,11... | collective-permute-start | bytes 30728 | tf_op jit(solution)/shard_map/ppermute | solution.py:21
  81.0 7.9 %collective-permute-start = (bf16[16,1,1280]{2,1,0:T(2,128)(2,1)}, bf16[16,1,1280]{2,1,0:T(2,128)(2,1)S(1)}, u32[]{:S(2)}, u32[]{:S(2)}) collective-permute-start(bf16[16,1,1280]{2,1,0:T(2,128)(2,1)} %get-tuple-element.16), channel_id=1, source_target_pairs={{0,1},{1,0},{2,3},{3,2},{4,5},{5,4},{6,7},{7,6},{8,9},{9,8},{10,11... | collective-permute-start | bytes 122888 | tf_op jit(solution)/shard_map/ppermute | solution.py:21
  89.0 0.6 copy-start.10
  89.0 0.6 copy-start.6
  127.6 5.2 %copy-start.3 = (bf16[1,1280,20,64]{1,3,2,0:T(8,128)(2,1)S(1)}, bf16[1,1280,20,64]{1,3,2,0:T(8,128)(2,1)}, u32[]{:S(2)}) copy-start(bf16[1,1280,20,64]{1,3,2,0:T(8,128)(2,1)} %get-tuple-element.27) | copy-start | bytes 9830404
  128.6 1.2 collective-permute-start.2
  132.7 5.0 %copy-start.5 = (bf16[16,64,1280]{2,1,0:T(8,128)(2,1)}, bf16[16,64,1280]{2,1,0:T(8,128)(2,1)S(1)}, u32[]{:S(2)}) copy-start(bf16[16,64,1280]{2,1,0:T(8,128)(2,1)S(1)} %fusion.2) | copy-start | bytes 7864324
  132.8 5.0 %copy-start.2 = (bf16[1,1280,20,64]{1,3,2,0:T(8,128)(2,1)S(1)}, bf16[1,1280,20,64]{1,3,2,0:T(8,128)(2,1)}, u32[]{:S(2)}) copy-start(bf16[1,1280,20,64]{1,3,2,0:T(8,128)(2,1)} %get-tuple-element.29) | copy-start | bytes 9830404
  137.7 5.5 %copy-start.1 = (bf16[1,1280,20,64]{1,3,2,0:T(8,128)(2,1)S(1)}, bf16[1,1280,20,64]{1,3,2,0:T(8,128)(2,1)}, u32[]{:S(2)}) copy-start(bf16[1,1280,20,64]{1,3,2,0:T(8,128)(2,1)} %get-tuple-element.28) | copy-start | bytes 9830404
  142.7 7.4 %collective-permute-start.3 = (bf16[1024,1280]{1,0:T(8,128)(2,1)}, bf16[1024,1280]{1,0:T(8,128)(2,1)}, u32[]{:S(2)}, u32[]{:S(2)}) collective-permute-start(bf16[1024,1280]{1,0:T(8,128)(2,1)} %convolution_convert_fusion.1.k0_ref.k0n_ref), channel_id=1, source_target_pairs={{0,1},{1,0},{2,3},{3,2},{4,5},{5,4},{6,7},{7,6},{8,9},{9,8},{10,11... | collective-permute-start | bytes 7864328 | tf_op jit(solution)/shard_map/ppermute | solution.py:21
  143.0 8.3 %collective-permute-start.4 = (bf16[1024,1280]{1,0:T(8,128)(2,1)}, bf16[1024,1280]{1,0:T(8,128)(2,1)}, u32[]{:S(2)}, u32[]{:S(2)}) collective-permute-start(bf16[1024,1280]{1,0:T(8,128)(2,1)} %convolution_convert_fusion.v0_ref), channel_id=1, source_target_pairs={{0,1},{1,0},{2,3},{3,2},{4,5},{5,4},{6,7},{7,6},{8,9},{9,8},{10,11... | collective-permute-start | bytes 7864328 | tf_op jit(solution)/shard_map/ppermute | solution.py:21
  150.0 51.2 %copy-start.4 = (bf16[16,64,1280]{2,1,0:T(8,128)(2,1)S(1)}, bf16[16,64,1280]{2,1,0:T(8,128)(2,1)}, u32[]{:S(2)}) copy-start(bf16[16,64,1280]{2,1,0:T(8,128)(2,1)} %get-tuple-element.19) | copy-start | bytes 7864324
  207.7 1.5 copy-start
  209.3 1.7 collective-permute-start.5
  209.7 1.3 copy-start.9
  209.7 1.2 collective-permute-start.6
  211.0 0.6 copy-start.11
  211.0 0.6 copy-start.7
  249.7 1.4 collective-permute-start.7
  250.0 1.2 collective-permute-start.8
  251.1 0.6 copy-start.12
  251.1 0.6 copy-start.8
